TPU v7x, 1024 devices: a whole 4x4x32 slice. The times are simulated.
1024 devices in a mesh: band: 64 (over z_lo, y), mem: 16 (over z_hi, x, core).
Axes of the slice: x: 4, y: 4, z: 32 (z_hi: 2, z_lo: 16; z = z_hi * 16 + z_lo), core: 2. Of those that a mesh axis runs over, the one named last changes fastest.
Arguments:
- ensemble: float32 [128, 5, 256, 128], P('mem', None, 'band'), may hold values from -5 to 5
- obs_value: float32 [2048, 128], P(('band', 'mem')), may hold values from -6 to 6
- obs_site: int32 [2048, 128], P(('band', 'mem')), may hold values from 0 to 79
- obs_count: int32 [2048], P(('band', 'mem')), may hold values from 32 to 128
- obs_precision: float32 [2048, 128], P(('band', 'mem')), may hold values from 0.25 to 4
- loc_weight: float32 [2048, 3], P(('band', 'mem')), may hold values from 0.1 to 1
- neighbours: int32 [2048, 3], P(('band', 'mem')), may hold values from 0 to 1
Outputs:
- forecast: float32 [128, 5, 256, 128], P('mem', None, 'band')
Inputs may be any that keep to these rules, and one draw needn't show every extreme that they name: `obs_site`: site v * 16 + c observes variable v at the tile's c-th cell. Slots 0 to obs_count - 1 of a tile are live. `neighbours`: entries are positions within the aligned block of 2 tiles that holds the tile.
All inputs are finite; a program needn't handle non-finite values.
Results may differ from a plain program's by a relative error of at most 0.0003.
Values sent between devices are 32-bit elements; how exact they have to be, the bound alone decides.
No kernel may reach another device: no remote copies, remote signals or barrier semaphores. Data moves between devices by JAX's collectives and lax.ppermute only.
A program may use at most 32 MiB of HBM per device.

v0:
```python
import jax
import jax.numpy as jnp
from jax import lax
from jax.sharding import PartitionSpec as P

TILE = 16
NSI = 6
STEPS = 2


COURANT = 0.08
HIGHEST = lax.Precision.HIGHEST


def extended_2(block, sides, width):
    for axis, dim in sides:
        count = lax.axis_size(axis)
        forward = [(i, i + 1) for i in range(count - 1)]
        backward = [(target, source) for source, target in forward]
        low = lax.ppermute(
            lax.slice_in_dim(block, block.shape[dim] - width, None, axis=dim), axis, forward
        )
        high = lax.ppermute(lax.slice_in_dim(block, 0, width, axis=dim), axis, backward)
        block = jnp.concatenate([low, block, high], axis=dim)
    return block


def minmod(lower_jump, upper_jump):
    return jnp.maximum(0.0, jnp.minimum(lower_jump, upper_jump)) + jnp.minimum(
        0.0, jnp.maximum(lower_jump, upper_jump)
    )


def flux_divergence(halo_extended_field, sweep_direction, advected_field):
    extent = halo_extended_field.shape[sweep_direction]
    differences = lax.slice_in_dim(
        halo_extended_field, 1, extent, axis=sweep_direction
    ) - lax.slice_in_dim(halo_extended_field, 0, extent - 1, axis=sweep_direction)
    slopes = minmod(
        lax.slice_in_dim(differences, 0, extent - 2, axis=sweep_direction),
        lax.slice_in_dim(differences, 1, extent - 1, axis=sweep_direction),
    )
    state_left_side = lax.slice_in_dim(
        halo_extended_field, 1, extent - 2, axis=sweep_direction
    ) + 0.5 * lax.slice_in_dim(slopes, 0, extent - 3, axis=sweep_direction)
    state_right_side = lax.slice_in_dim(
        halo_extended_field, 2, extent - 1, axis=sweep_direction
    ) - 0.5 * lax.slice_in_dim(slopes, 1, extent - 2, axis=sweep_direction)
    advected_field_left = state_left_side[:, advected_field : advected_field + 1]
    advected_field_right = state_right_side[:, advected_field : advected_field + 1]
    signal_velocity = jnp.maximum(jnp.abs(advected_field_left), jnp.abs(advected_field_right))
    interface_fluxes = 0.5 * (
        advected_field_left * state_left_side + advected_field_right * state_right_side
    ) - 0.5 * signal_velocity * (state_right_side - state_left_side)
    return lax.slice_in_dim(
        interface_fluxes, 1, extent - 3, axis=sweep_direction
    ) - lax.slice_in_dim(interface_fluxes, 0, extent - 4, axis=sweep_direction)


def advance(halo_extended_field):
    centre = halo_extended_field[:, :, 2:-2]
    lat_div = flux_divergence(halo_extended_field, 2, 1)
    wrapped = jnp.concatenate([centre[..., -2:], centre, centre[..., :2]], axis=3)
    lon_div = flux_divergence(wrapped, 3, 0)
    return centre - COURANT * (lat_div + lon_div)


def obs_space(tile_state, obs_value, obs_site):
    site_count = tile_state.shape[2]
    ens_mean = jnp.mean(tile_state, axis=1)
    anomaly = tile_state - ens_mean[:, None, :]
    selector = (obs_site[:, :, None] == jnp.arange(site_count)[None, None, :]).astype(jnp.float32)
    obs_anomaly = jnp.einsum("bos,bks->bok", selector, anomaly, precision=HIGHEST)
    obs_mean = jnp.einsum("bos,bs->bo", selector, ens_mean, precision=HIGHEST)
    return (ens_mean, anomaly, obs_anomaly, obs_value - obs_mean)


def transform(local_anomaly, local_innovation, local_weight, ens_mean, anomaly):
    members = local_anomaly.shape[2]
    identity = jnp.eye(members, dtype=jnp.float32)
    weighted = local_anomaly * local_weight[:, :, None]
    gram_matrix = (
        jnp.einsum("bpk,bpj->bkj", weighted, local_anomaly, precision=HIGHEST)
        + (members - 1.0) * identity
    )
    frob_norm = jnp.sqrt(jnp.sum(gram_matrix * gram_matrix, axis=(1, 2)))
    root_iter = gram_matrix / frob_norm[:, None, None]
    inverse = jnp.broadcast_to(identity, gram_matrix.shape)
    for sweep in range(NSI):
        factor = 1.5 * identity - 0.5 * jnp.matmul(inverse, root_iter, precision=HIGHEST)
        root_iter = jnp.matmul(root_iter, factor, precision=HIGHEST)
        inverse = jnp.matmul(factor, inverse, precision=HIGHEST)
    projected = jnp.einsum("bpk,bp->bk", weighted, local_innovation, precision=HIGHEST)
    halfway = jnp.einsum("bkj,bj->bk", inverse, projected, precision=HIGHEST)
    mean_weights = (
        jnp.einsum("bkj,bj->bk", inverse, halfway, precision=HIGHEST) / frob_norm[:, None]
    )
    spread_weights = inverse * jnp.sqrt((members - 1.0) / frob_norm)[:, None, None]
    combined = spread_weights + mean_weights[:, :, None]
    return ens_mean[:, None, :] + jnp.einsum("bjk,bjs->bks", combined, anomaly, precision=HIGHEST)


def localise(obs_anomaly, innovation, slot_weight, neighbour_tiles, loc_weight, ens_mean, anomaly):
    batch_tiles = neighbour_tiles.shape[0]
    local_anomaly = obs_anomaly[neighbour_tiles].reshape(batch_tiles, -1, obs_anomaly.shape[2])
    local_innovation = innovation[neighbour_tiles].reshape(batch_tiles, -1)
    local_weight = (loc_weight[:, :, None] * slot_weight[neighbour_tiles]).reshape(batch_tiles, -1)
    return transform(local_anomaly, local_innovation, local_weight, ens_mean, anomaly)


def shards(ensemble, obs_value, obs_site, obs_count, obs_precision, loc_weight, neighbours):
    fields = ensemble
    lat_rows = fields.shape[2]
    margin = 2 * STEPS
    extended = extended_2(fields, (("band", 2),), margin)
    offset = lax.axis_index("band") * lat_rows
    lat_total = lat_rows * lax.axis_size("band")
    for repeat in range(STEPS):
        extended = advance(extended)
        remaining = margin - 2 * (repeat + 1)
        if remaining > 0:
            global_row = (
                lax.broadcasted_iota(jnp.int32, (1, 1, extended.shape[2], 1), 2)
                - remaining
                + offset
            )
            inside = (global_row >= 0) & (global_row < lat_total)
            extended = jnp.where(inside, extended, 0.0)
    fields = extended
    members, variables, lon_total = (fields.shape[0], fields.shape[1], fields.shape[3])
    flattened = fields.reshape(members, variables, lat_rows * lon_total)
    grouped = lax.all_to_all(flattened, "mem", split_axis=2, concat_axis=0, tiled=True)
    all_members = grouped.shape[0]
    tile_count = neighbours.shape[0]
    tile_state = (
        grouped.reshape(all_members, variables, tile_count, TILE)
        .transpose(2, 0, 1, 3)
        .reshape(tile_count, all_members, variables * TILE)
    )
    ens_mean, anomaly, obs_anomaly, innovation = obs_space(tile_state, obs_value, obs_site)
    live_slots = jnp.arange(obs_value.shape[1])[None, :] < obs_count[:, None]
    slot_weight = jnp.where(live_slots, obs_precision, 0.0)
    analysed = localise(
        obs_anomaly, innovation, slot_weight, neighbours, loc_weight, ens_mean, anomaly
    )
    outgoing = (
        analysed.reshape(tile_count, all_members, variables, TILE)
        .transpose(1, 2, 0, 3)
        .reshape(all_members, variables, tile_count * TILE)
    )
    returned = lax.all_to_all(outgoing, "mem", split_axis=0, concat_axis=2, tiled=True)
    fields = returned.reshape(members, variables, lat_rows, lon_total)
    return advance(extended_2(fields, (("band", 2),), 2))


def solution(mesh):
    return jax.shard_map(
        shards,
        mesh=mesh,
        in_specs=(
            P("mem", None, "band", None),
            P(("band", "mem"), None),
            P(("band", "mem"), None),
            P(("band", "mem")),
            P(("band", "mem"), None),
            P(("band", "mem"), None),
            P(("band", "mem"), None),
        ),
        out_specs=P("mem", None, "band", None),
        check_vma=False,
    )
```

profile of v0, /device:TPU:120, one launch (start us, length us, event | category | flops | bytes accessed | tf_op | source)
XLA Modules:
  0.0 126.6 jit_solution(7004798391175508819)
XLA Ops:
  0.0 0.9 copy.39
  0.9 4.7 %collective-permute-start = (f32[8,5,4,128]{3,0,2,1:T(8,128)S(1)}, f32[8,5,4,128]{3,0,2,1:T(8,128)S(1)}, u32[]{:S(2)}, u32[]{:S(2)}) collective-permute-start(f32[8,5,4,128]{3,0,2,1:T(8,128)S(1)} %copy.39), channel_id=1, source_target_pairs={{0,16},{16,32},{32,48},{48,64},{64,80},{80,96},{96,112},{112,128},... | collective-permute-start | bytes 245768 | tf_op jit(solution)/shard_map/ppermute | solution.py:20
  5.6 1.9 %collective-permute-start.1 = (f32[8,5,4,128]{3,0,2,1:T(8,128)S(1)}, f32[8,5,4,128]{3,0,2,1:T(8,128)S(1)}, u32[]{:S(2)}, u32[]{:S(2)}) collective-permute-start(f32[8,5,4,128]{3,0,2,1:T(8,128)S(1)} %copy.39), channel_id=1, source_target_pairs={{16,0},{32,16},{48,32},{64,48},{80,64},{96,80},{112,96},{128,112},... | collective-permute-start | bytes 245768 | tf_op jit(solution)/shard_map/ppermute | solution.py:23
  7.5 0.7 compare_select_fusion
  8.3 0.8 compare_select_fusion.1
  9.1 0.9 constant_dynamic-update-slice_fusion.1
  10.0 5.3 %collective-permute-done.1 = f32[8,5,4,128]{3,0,2,1:T(8,128)S(1)} collective-permute-done((f32[8,5,4,128]{3,0,2,1:T(8,128)S(1)}, f32[8,5,4,128]{3,0,2,1:T(8,128)S(1)}, u32[]{:S(2)}, u32[]{:S(2)}) %collective-permute-start.1) | collective-permute-done | bytes 81952 | tf_op jit(solution)/shard_map/ppermute | solution.py:23
  17.6 0.7 copy.42
  18.3 1.2 reshape.139
  19.5 26.1 %all-to-all-start = ((f32[16,1,1280]{2,1,0:T(1,128)}), f32[16,1,1280]{2,1,0:T(1,128)S(1)}, u32[]{:S(2)}, u32[]{:S(2)}) async-start(f32[16,1,1280]{2,1,0:T(1,128)} %reshape.139), calls=%async_computation | async-start | bytes 163840 | tf_op jit(solution)/shard_map/all_to_all | solution.py:132
  45.6 0.6 gather_fusion.1
  46.3 24.3 %all-to-all-done = f32[16,1,1280]{2,1,0:T(1,128)S(1)} async-done(((f32[16,1,1280]{2,1,0:T(1,128)}), f32[16,1,1280]{2,1,0:T(1,128)S(1)}, u32[]{:S(2)}, u32[]{:S(2)}) %all-to-all-start) | async-done | bytes 81952 | tf_op jit(solution)/shard_map/all_to_all | solution.py:132
  70.6 0.5 broadcast.188
  71.1 0.8 reduce.1
  71.9 0.6 reshape.140
  72.6 0.5 copy.44
  73.1 0.4 reshape.89
  74.4 0.6 gather_fusion
  75.2 0.6 multiply_reduce_fusion
  75.8 0.3 fusion.5
  76.2 0.3 fusion.47
  80.2 0.6 gather_fusion.2
  80.8 0.5 convolution_bitcast_fusion
  81.9 0.3 convolution_bitcast_fusion.1
  82.2 0.3 fusion.61
  82.6 0.4 convolution_add_fusion.1
  83.4 27.1 %all_to_all.30 = f32[16,1,1280]{2,1,0:T(1,128)S(1)} all-to-all(f32[16,1,1280]{2,1,0:T(1,128)S(1)} %reshape.141), channel_id=1, replica_groups=mesh['band'=64,'mem'=16] {'mem'}, dimensions={0} | all-to-all | bytes 163840 | tf_op jit(solution)/shard_map/all_to_all | solution.py:151
  110.6 0.8 reduce.2
  112.0 4.4 %collective-permute-start.2 = (f32[8,5,2,128]{3,0,2,1:T(8,128)S(1)}, f32[8,5,2,128]{3,0,2,1:T(8,128)S(1)}, u32[]{:S(2)}, u32[]{:S(2)}) collective-permute-start(f32[8,5,2,128]{3,0,2,1:T(8,128)S(1)} %get-tuple-element.40), channel_id=1, source_target_pairs={{0,16},{16,32},{32,48},{48,64},{64,80},{80,96},{96,112},{112,128},... | collective-permute-start | bytes 122888 | tf_op jit(solution)/shard_map/ppermute | solution.py:20
  116.5 1.9 %collective-permute-start.3 = (f32[8,5,2,128]{3,0,2,1:T(8,128)S(1)}, f32[8,5,2,128]{3,0,2,1:T(8,128)S(1)}, u32[]{:S(2)}, u32[]{:S(2)}) collective-permute-start(f32[8,5,2,128]{3,0,2,1:T(8,128)S(1)} %get-tuple-element.39), channel_id=1, source_target_pairs={{16,0},{32,16},{48,32},{64,48},{80,64},{96,80},{112,96},{128,112},... | collective-permute-start | bytes 122888 | tf_op jit(solution)/shard_map/ppermute | solution.py:23
  119.1 6.6 %collective-permute-done.3 = f32[8,5,2,128]{3,0,2,1:T(8,128)S(1)} collective-permute-done((f32[8,5,2,128]{3,0,2,1:T(8,128)S(1)}, f32[8,5,2,128]{3,0,2,1:T(8,128)S(1)}, u32[]{:S(2)}, u32[]{:S(2)}) %collective-permute-start.3) | collective-permute-done | bytes 40992 | tf_op jit(solution)/shard_map/ppermute | solution.py:23
  125.9 0.7 copy.63
  (100 shorter events, 9.5 us)
Async XLA Ops:
  0.9 8.2 %collective-permute-start = (f32[8,5,4,128]{3,0,2,1:T(8,128)S(1)}, f32[8,5,4,128]{3,0,2,1:T(8,128)S(1)}, u32[]{:S(2)}, u32[]{:S(2)}) collective-permute-start(f32[8,5,4,128]{3,0,2,1:T(8,128)S(1)} %copy.39), channel_id=1, source_target_pairs={{0,16},{16,32},{32,48},{48,64},{64,80},{80,96},{96,112},{112,128},... | collective-permute-start | bytes 245768 | tf_op jit(solution)/shard_map/ppermute | solution.py:20
  5.6 9.7 %collective-permute-start.1 = (f32[8,5,4,128]{3,0,2,1:T(8,128)S(1)}, f32[8,5,4,128]{3,0,2,1:T(8,128)S(1)}, u32[]{:S(2)}, u32[]{:S(2)}) collective-permute-start(f32[8,5,4,128]{3,0,2,1:T(8,128)S(1)} %copy.39), channel_id=1, source_target_pairs={{16,0},{32,16},{48,32},{64,48},{80,64},{96,80},{112,96},{128,112},... | collective-permute-start | bytes 245768 | tf_op jit(solution)/shard_map/ppermute | solution.py:23
  17.6 28.6 %copy-start.1 = (f32[2,3]{1,0:T(2,128)S(1)}, f32[2,3]{1,0:T(2,128)}, u32[]{:S(2)}) copy-start(f32[2,3]{1,0:T(2,128)} %param.12) | copy-start | bytes 76
  19.5 51.1 %all-to-all-start = ((f32[16,1,1280]{2,1,0:T(1,128)}), f32[16,1,1280]{2,1,0:T(1,128)S(1)}, u32[]{:S(2)}, u32[]{:S(2)}) async-start(f32[16,1,1280]{2,1,0:T(1,128)} %reshape.139), calls=%async_computation | async-start | bytes 163840 | tf_op jit(solution)/shard_map/all_to_all | solution.py:132
  72.6 1.6 %copy-start = (s32[2,128]{1,0:T(2,128)S(1)}, s32[2,128]{1,0:T(2,128)}, u32[]{:S(2)}) copy-start(s32[2,128]{1,0:T(2,128)} %param.9) | copy-start | bytes 3076
  77.3 2.9 %copy-start.2 = (f32[2,128]{1,0:T(2,128)S(1)}, f32[2,128]{1,0:T(2,128)}, u32[]{:S(2)}) copy-start(f32[2,128]{1,0:T(2,128)} %param.8) | copy-start | bytes 3076
  112.0 7.0 %collective-permute-start.2 = (f32[8,5,2,128]{3,0,2,1:T(8,128)S(1)}, f32[8,5,2,128]{3,0,2,1:T(8,128)S(1)}, u32[]{:S(2)}, u32[]{:S(2)}) collective-permute-start(f32[8,5,2,128]{3,0,2,1:T(8,128)S(1)} %get-tuple-element.40), channel_id=1, source_target_pairs={{0,16},{16,32},{32,48},{48,64},{64,80},{80,96},{96,112},{112,128},... | collective-permute-start | bytes 122888 | tf_op jit(solution)/shard_map/ppermute | solution.py:20
  116.5 9.2 %collective-permute-start.3 = (f32[8,5,2,128]{3,0,2,1:T(8,128)S(1)}, f32[8,5,2,128]{3,0,2,1:T(8,128)S(1)}, u32[]{:S(2)}, u32[]{:S(2)}) collective-permute-start(f32[8,5,2,128]{3,0,2,1:T(8,128)S(1)} %get-tuple-element.39), channel_id=1, source_target_pairs={{16,0},{32,16},{48,32},{64,48},{80,64},{96,80},{112,96},{128,112},... | collective-permute-start | bytes 122888 | tf_op jit(solution)/shard_map/ppermute | solution.py:23
where the time goes:
time: 127 us
  starting transfers between devices  39.1 us (31%)
  waiting for transfers between devices  36.2 us (29%)
  blocking collectives  27.1 us (21%)
  local copies, waits for them, and re-layouts  9.92 us (8%)
  matrix products  7.26 us (6%)
  other arithmetic  6.3 us (5%)
    all_to_all x1, blocking collectives, shards(): lax.all_to_all(outgoing, 'mem', split_axis=0, concat_axis=2, tiled=True)  27.1 us
    all_to_all x1, starting transfers between devices, shards(): lax.all_to_all(flattened, 'mem', split_axis=2, concat_axis=0, tiled=True)  26.1 us
    all_to_all x1, waiting for transfers between devices, shards(): lax.all_to_all(flattened, 'mem', split_axis=2, concat_axis=0, tiled=True)  24.3 us
    ppermute x2, waiting for transfers between devices, extended_2(): lax.ppermute(lax.slice_in_dim(block, 0, width, axis=dim), axis, backward)  11.9 us
    ppermute x2, starting transfers between devices, extended_2(): lax.ppermute(lax.slice_in_dim(block, block.shape[dim] - width, None, axis...  9.11 us
    unnamed x16, local copies, waits for them, and re-layouts  3.91 us
    ppermute x2, starting transfers between devices, extended_2(): lax.ppermute(lax.slice_in_dim(block, 0, width, axis=dim), axis, backward)  3.84 us
  transfers between devices with their start and end apart: 5, of which 3 were waited for; matrix products, arithmetic and copies ran while one was open for 3% of the time, Pallas kernels for 0%

commit v1 on v0

v1 whole, which is shorter than its diff:
```python
import jax
import jax.numpy as jnp
from jax import lax
from jax.experimental import pallas as pl
from jax.experimental.pallas import tpu as pltpu
from jax.sharding import Mesh, PartitionSpec as P

NSI = 6
STEPS = 2
COURANT = 0.08
HIGHEST = lax.Precision.HIGHEST
MEMBERS = 128
VMEM = pl.BlockSpec(memory_space=pltpu.VMEM)
SMEM = pl.BlockSpec(memory_space=pltpu.SMEM)


def half_minmod(lower, upper):
    return 0.5 * (
        jnp.maximum(0.0, jnp.minimum(lower, upper)) + jnp.minimum(0.0, jnp.maximum(lower, upper))
    )


def twice_flux(left, right, carrier):
    speed = jnp.maximum(jnp.abs(left[carrier]), jnp.abs(right[carrier]))
    gain_left = left[carrier] + speed
    gain_right = right[carrier] - speed
    return [gain_left * l + gain_right * r for l, r in zip(left, right)]


def transport(rows):
    count, variables = len(rows), range(len(rows[0]))
    jumps = [[rows[i + 1][v] - rows[i][v] for v in variables] for i in range(count - 1)]
    halves = [None] + [
        [half_minmod(jumps[i - 1][v], jumps[i][v]) for v in variables] for i in range(1, count - 1)
    ]
    fluxes = [None] + [
        twice_flux(
            [rows[i][v] + halves[i][v] for v in variables],
            [rows[i + 1][v] - halves[i + 1][v] for v in variables],
            1,
        )
        for i in range(1, count - 2)
    ]
    result = []
    for i in range(2, count - 2):
        left, right = [], []
        for v in variables:
            q = rows[i][v]
            jump = pltpu.roll(q, 127, 1) - q
            half = half_minmod(pltpu.roll(jump, 1, 1), jump)
            left.append(q + half)
            right.append(pltpu.roll(q - half, 127, 1))
        flux = twice_flux(left, right, 0)
        result.append(
            [
                rows[i][v]
                - (0.5 * COURANT)
                * ((fluxes[i][v] - fluxes[i - 1][v]) + (flux[v] - pltpu.roll(flux[v], 1, 1)))
                for v in variables
            ]
        )
    return result


def turned(x, groups):
    shift = (16 * groups) % 128
    return pltpu.roll(x, shift, 1) if shift else x


def lanes_of(shape):
    return lax.broadcasted_iota(jnp.int32, shape, 1)


def background_kernel(band_ref, centre_ref, low_ref, high_ref, out_ref):
    def row(ref, r):
        return [ref[pl.ds(v * 4 + r, 8, stride=20), :] for v in range(5)]

    rows = [row(ref, r) for ref in (low_ref, centre_ref, high_ref) for r in range(4)]
    rows = transport(rows)
    keep_low = (band_ref[0] > 0).astype(jnp.float32)
    keep_high = (band_ref[0] < band_ref[1] - 1).astype(jnp.float32)
    for i in (0, 1):
        rows[i] = [x * keep_low for x in rows[i]]
    for i in (6, 7):
        rows[i] = [x * keep_high for x in rows[i]]
    rows = transport(rows)
    lane = lanes_of((8, 128))
    group = lane >> 4
    for q in range(8):
        j = q % 4
        chosen = (q // 4, 2 + q // 4)
        for b in (0, 1):
            slab = None
            for g in range(8):
                u, v = g // 4, g % 4
                piece = turned(rows[chosen[b]][v], g - (2 * j + u))
                slab = piece if slab is None else jnp.where(group == g, piece, slab)
            out_ref[q * 20 + 8 * b : q * 20 + 8 * b + 8, :] = slab
        last = jnp.where(
            lane < 32, turned(rows[chosen[0]][4], -2 * j), turned(rows[chosen[1]][4], 2 - 2 * j)
        )
        out_ref[q * 20 + 16 : q * 20 + 20, :] = jnp.where(
            lane[:4] < 64, last[:4], pltpu.roll(last, 64, 1)[4:]
        )


def statistics_kernel(count_ref, loc_ref, near_ref, value_ref, site_ref, precision_ref, out_ref):
    slot = lanes_of((1, 128))
    sub = lax.broadcasted_iota(jnp.int32, (8, 128), 0)
    lane = lanes_of((8, 128))
    cell = lax.broadcasted_iota(jnp.int32, (128, 128), 0)
    slab = jnp.zeros((8, 128), jnp.float32)
    last = jnp.zeros((8, 128), jnp.float32)
    for u in (0, 1):
        weight = jnp.where(slot < count_ref[u], precision_ref[u : u + 1, :], 0.0)
        both = jnp.where(sub == 0, weight, jnp.where(sub == 1, weight * value_ref[u : u + 1, :], 0.0))
        site = site_ref[u : u + 1, :]
        in_slab = ((cell & 63) == site) & ((cell >> 6) == u)
        in_last = ((64 + (cell & 15)) == site) & (((cell >> 4) & 1) == u)
        dims = (((1,), (1,)), ((), ()))
        slab += lax.dot_general(
            both, in_slab.astype(jnp.float32), dims, precision=HIGHEST,
            preferred_element_type=jnp.float32,
        )
        last += lax.dot_general(
            both, in_last.astype(jnp.float32), dims, precision=HIGHEST,
            preferred_element_type=jnp.float32,
        )
    out = jnp.where(sub < 2, slab, jnp.where(sub < 4, pltpu.roll(last, 2, 0), 0.0))
    for t in (0, 1):
        gain = []
        for u in (0, 1):
            total = jnp.float32(0.0)
            for n in range(3):
                total += jnp.where(near_ref[t, n] == u, loc_ref[t, n], 0.0)
            gain.append(total)
        out = jnp.where(sub == 4 + t, jnp.where((lane >> 6) == 0, gain[0], gain[1]), out)
        out = jnp.where(sub == 6 + t, jnp.where(((lane >> 4) & 1) == 0, gain[0], gain[1]), out)
    out_ref[...] = out


def dot(a, b):
    return jnp.dot(a, b, precision=HIGHEST, preferred_element_type=jnp.float32)


def analysis_kernel(half_ref, own_ref, other_ref, own_stats_ref, out_ref):
    lane8 = lanes_of((8, 128))
    sub8 = lax.broadcasted_iota(jnp.int32, (8, 128), 0)
    lane = lanes_of((MEMBERS, 128))
    lane1 = lanes_of((1, 128))
    slabs = []
    for b in (0, 1):
        slabs.append(
            jnp.concatenate(
                [
                    ref[s * 20 + 8 * b : s * 20 + 8 * b + 8, :]
                    for ref in (own_ref, other_ref)
                    for s in range(8)
                ],
                axis=0,
            )
        )
    parts = []
    for ref in (own_ref, other_ref):
        for s in range(8):
            four = ref[s * 20 + 16 : s * 20 + 20, :]
            eight = jnp.concatenate([four, four], axis=0)
            eight = jnp.where(sub8 < 4, eight, pltpu.roll(eight, 64, 1))
            parts.append(jnp.where(lane8 < 64, eight, 0.0))
    slabs.append(jnp.concatenate(parts, axis=0))
    means = [jnp.sum(x, axis=0, keepdims=True) * (1.0 / MEMBERS) for x in slabs]
    slabs = [x - m for x, m in zip(slabs, means)]
    first = half_ref[0] == 0
    own = own_stats_ref[...]
    other = other_ref[160:168, :]
    stats = [jnp.where(first, own, other), jnp.where(first, other, own)]
    eye = (lax.broadcasted_iota(jnp.int32, (MEMBERS, 128), 0) == lane).astype(jnp.float32)
    tiles = [(b, t) for b in (0, 1) for t in (0, 1)]
    tops, fields, norms = [], [], []
    for b, t in tiles:
        s = stats[b]
        mine = (lane1 >> 5) == b
        gain = s[4 + t : 5 + t]
        gain_last = jnp.where(mine, s[6 + t : 7 + t], 0.0)
        pull = gain * (s[1:2] - s[0:1] * means[b])
        pull_last = gain_last * (s[3:4] - s[2:3] * means[2])
        p, r = slabs[b], slabs[2]
        gram = lax.dot_general(
            jnp.concatenate([p * (gain * s[0:1]), r * (gain_last * s[2:3])], axis=1),
            jnp.concatenate([p, r], axis=1),
            (((1,), (1,)), ((), ())),
            precision=HIGHEST,
            preferred_element_type=jnp.float32,
        )
        gram = gram + (MEMBERS - 1.0) * eye
        norm = jnp.sqrt(jnp.sum(jnp.sum(gram * gram, axis=0, keepdims=True), axis=1, keepdims=True))
        norms.append(norm)
        tops.append(gram * (1.0 / norm))
        b_col = jnp.sum(p * pull + r * pull_last, axis=1, keepdims=True)
        if t == 0:
            field = jnp.where(
                lane < 64, p, jnp.where((lane >> 4) == 4 + 2 * b, pltpu.roll(r, 64, 1), 0.0)
            )
            field = jnp.where(lane == 127, b_col, field)
        else:
            field = jnp.where(lane >= 64, p, jnp.where((lane >> 4) == 2 * b + 1, r, 0.0))
            field = jnp.where(lane == 0, b_col, field)
        fields.append(field)
    for sweep in range(NSI):
        factors = [1.5 * eye - 0.5 * x for x in tops]
        if sweep < NSI - 1:
            both = [
                dot(f, jnp.concatenate([x, y], axis=1)) for f, x, y in zip(factors, tops, fields)
            ]
            fields = [x[:, 128:] for x in both]
            tops = [dot(x[:, :128], f) for f, x in zip(factors, both)]
        else:
            fields = [dot(f, y) for f, y in zip(factors, fields)]
    moved = []
    for (b, t), field, norm in zip(tiles, fields, norms):
        column = field[:, 127:128] if t == 0 else field[:, 0:1]
        shift = jnp.sum(column * field, axis=0, keepdims=True) * (1.0 / norm)
        moved.append(field[:64] * jnp.sqrt((MEMBERS - 1.0) / norm) + shift)
    lane64 = lanes_of((64, 128))
    outs = [
        jnp.where(lane64 < 64, moved[0], moved[1]) + means[0],
        jnp.where(lane64 < 64, moved[2], moved[3]) + means[1],
    ]
    group = lane64 >> 4
    last = jnp.where(group == 1, moved[1], pltpu.roll(moved[0], 64, 1))
    last = jnp.where(group == 2, pltpu.roll(moved[2], 64, 1), last)
    last = jnp.where(group == 3, moved[3], last) + means[2]
    for d in range(8):
        for b in (0, 1):
            out_ref[d * 20 + 8 * b : d * 20 + 8 * b + 8, :] = outs[b][8 * d : 8 * d + 8]
        piece = last[8 * d : 8 * d + 8]
        out_ref[d * 20 + 16 : d * 20 + 20, :] = jnp.where(
            lane8[:4] < 64, piece[:4], pltpu.roll(piece, 64, 1)[4:]
        )


def unpack_kernel(in_ref, low_ref, high_ref):
    lane = lanes_of((8, 128))
    sub = lax.broadcasted_iota(jnp.int32, (8, 128), 0)
    group = lane >> 4
    lasts = []
    for q in range(8):
        four = in_ref[q * 20 + 16 : q * 20 + 20, :]
        eight = jnp.concatenate([four, four], axis=0)
        lasts.append(jnp.where(sub < 4, eight, pltpu.roll(eight, 64, 1)))
    for r in range(4):
        b, out_ref = r // 2, (low_ref if r < 2 else high_ref)
        for v in range(5):
            field = None
            for j in range(4):
                q = (r % 2) * 4 + j
                if v < 4:
                    slab = in_ref[q * 20 + 8 * b : q * 20 + 8 * b + 8, :]
                    for u in (0, 1):
                        piece = turned(slab, 2 * j + u - 4 * u - v)
                        field = piece if field is None else jnp.where(group == 2 * j + u, piece, field)
                else:
                    piece = turned(lasts[q], 2 * j - 2 * b)
                    field = piece if field is None else jnp.where((group >> 1) == j, piece, field)
            at = (v * 2 + r % 2) * 8
            out_ref[at : at + 8, :] = field


def forecast_kernel(below_ref, low_ref, high_ref, above_ref, out_ref):
    def row(ref, r):
        return [ref[(v * 2 + r) * 8 : (v * 2 + r) * 8 + 8, :] for v in range(5)]

    rows = [row(ref, r) for ref in (below_ref, low_ref, high_ref, above_ref) for r in (0, 1)]
    rows = transport(rows)
    for r in range(4):
        for v in range(5):
            out_ref[pl.ds(v * 4 + r, 8, stride=20), :] = rows[r][v]


def array(*shape):
    return jax.ShapeDtypeStruct(shape, jnp.float32)


def shards(ensemble, obs_value, obs_site, obs_count, obs_precision, loc_weight, neighbours):
    bands = lax.axis_size("band")
    forward = [(i, i + 1) for i in range(bands - 1)]
    backward = [(target, source) for source, target in forward]
    here = jnp.stack([lax.axis_index("band"), jnp.int32(bands)])
    fields = ensemble.reshape(160, 128)
    low = lax.ppermute(fields, "band", forward)
    high = lax.ppermute(fields, "band", backward)
    stats = pl.pallas_call(
        statistics_kernel,
        out_shape=array(8, 128),
        in_specs=[SMEM] * 3 + [VMEM] * 3,
        out_specs=VMEM,
        name="statistics",
    )(obs_count, loc_weight, neighbours, obs_value, obs_site, obs_precision)
    packed = pl.pallas_call(
        background_kernel,
        out_shape=array(160, 128),
        in_specs=[SMEM] + [VMEM] * 3,
        out_specs=VMEM,
        name="background",
    )(here, fields, low, high)
    own = lax.all_to_all(packed.reshape(8, 5, 4, 128), "q", split_axis=0, concat_axis=0, tiled=True)
    own = own.reshape(160, 128)
    other = lax.ppermute(jnp.concatenate([own, stats], axis=0), "half", [(0, 1), (1, 0)])
    analysed = pl.pallas_call(
        analysis_kernel,
        out_shape=array(160, 128),
        in_specs=[SMEM] + [VMEM] * 3,
        out_specs=VMEM,
        name="analysis",
    )(jnp.reshape(lax.axis_index("half"), (1,)), own, other, stats)
    returned = lax.all_to_all(
        analysed.reshape(8, 5, 4, 128), "q", split_axis=0, concat_axis=0, tiled=True
    )
    low, high = pl.pallas_call(
        unpack_kernel,
        out_shape=(array(80, 128), array(80, 128)),
        in_specs=[VMEM],
        out_specs=(VMEM, VMEM),
        name="unpack",
    )(returned.reshape(160, 128))
    below = lax.ppermute(high, "band", forward)
    above = lax.ppermute(low, "band", backward)
    out = pl.pallas_call(
        forecast_kernel,
        out_shape=array(160, 128),
        in_specs=[VMEM] * 4,
        out_specs=VMEM,
        name="forecast",
    )(below, low, high, above)
    return out.reshape(8, 5, 4, 128)


def solution(mesh):
    bands = mesh.shape["band"]
    fine = Mesh(mesh.devices.reshape(bands, 2, 8), ("band", "half", "q"))
    members = ("half", "q")
    tiles = ("band", "half", "q")
    return jax.shard_map(
        shards,
        mesh=fine,
        in_specs=(
            P(members, None, "band", None),
            P(tiles, None),
            P(tiles, None),
            P(tiles),
            P(tiles, None),
            P(tiles, None),
            P(tiles, None),
        ),
        out_specs=P(members, None, "band", None),
        check_vma=False,
    )
```

time: 127 us -> 99.8 us (0.79)
  the two profiles are of different devices: /device:TPU:120 before, /device:TPU:24 now
where the time goes in v1:
time: 99.8 us; the launch traced here: 99.2 us
  starting transfers between devices  57.6 us (58%)
  waiting for transfers between devices  14.6 us (15%)
  Pallas kernels  14.1 us (14%)
  blocking collectives  9.66 us (10%)
  local copies, waits for them, and re-layouts  1.88 us (2%)
  other arithmetic  1.33 us (1%)
    ppermute x1, starting transfers between devices, shards(): lax.ppermute(jnp.concatenate([own, stats], axis=0), 'half', [(0, 1), (1,...  29 us
    ppermute x1, starting transfers between devices, shards(): below = lax.ppermute(high, 'band', forward)  14.5 us
    all_to_all x1, blocking collectives, shards(): lax.all_to_all(analysed.reshape(8, 5, 4, 128), 'q', split_axis=0, concat_...  9.66 us
    ppermute x1, waiting for transfers between devices, shards(): above = lax.ppermute(low, 'band', backward)  6.24 us
    pallas_call x1, Pallas kernels, shards(): pl.pallas_call(analysis_kernel, out_shape=array(160, 128), in_specs=[SMEM...  5.91 us
    ppermute x1, starting transfers between devices, shards(): low = lax.ppermute(fields, 'band', forward)  5.3 us
    all_to_all x1, starting transfers between devices, shards(): lax.all_to_all(packed.reshape(8, 5, 4, 128), 'q', split_axis=0, concat_ax...  4.3 us
    all_to_all x1, waiting for transfers between devices, shards(): lax.all_to_all(packed.reshape(8, 5, 4, 128), 'q', split_axis=0, concat_ax...  3.73 us
  transfers between devices with their start and end apart: 6, of which 4 were waited for; matrix products, arithmetic and copies ran while one was open for 1% of the time, Pallas kernels for 2%

profile of v1, /device:TPU:24, one launch (start us, length us, event | category | flops | bytes accessed | tf_op | source)
XLA Modules:
  0.0 99.2 jit_solution(6064465625491760155)
XLA Ops:
  0.0 2.6 %collective-permute-start.1 = (f32[160,128]{1,0:T(8,128)}, f32[160,128]{1,0:T(8,128)S(1)}, u32[]{:S(2)}, u32[]{:S(2)}) collective-permute-start(f32[160,128]{1,0:T(8,128)} %bitcast.13), channel_id=1, source_target_pairs={{16,0},{32,16},{48,32},{64,48},{80,64},{96,80},{112,96},{128,112},... | collective-permute-start | bytes 245768 | tf_op jit(solution)/shard_map/ppermute | solution.py:291
  2.6 5.3 %collective-permute-start = (f32[160,128]{1,0:T(8,128)}, f32[160,128]{1,0:T(8,128)S(1)}, u32[]{:S(2)}, u32[]{:S(2)}) collective-permute-start(f32[160,128]{1,0:T(8,128)} %bitcast.14), channel_id=1, source_target_pairs={{0,16},{16,32},{32,48},{48,64},{64,80},{80,96},{96,112},{112,128},... | collective-permute-start | bytes 245768 | tf_op jit(solution)/shard_map/ppermute | solution.py:290
  8.0 0.6 pad_add_fusion.band_ref
  8.6 0.0 collective-permute-done.1.high_ref
  8.6 0.0 copy-start.2
  8.6 1.7 %collective-permute-done.low_ref = f32[160,128]{1,0:T(8,128)S(1)} collective-permute-done((f32[160,128]{1,0:T(8,128)}, f32[160,128]{1,0:T(8,128)S(1)}, u32[]{:S(2)}, u32[]{:S(2)}) %collective-permute-start) | collective-permute-done | bytes 81952 | tf_op jit(solution)/shard_map/ppermute | solution.py:290
  10.3 0.0 copy-done.2
  10.3 0.0 copy-start.3
  10.3 0.6 copy-done.3
  11.0 2.7 %background.1 = f32[160,128]{1,0:T(8,128)} custom-call(s32[2]{0:T(128)} %pad_add_fusion.band_ref, f32[160,128]{1,0:T(8,128)} %bitcast.15, f32[160,128]{1,0:T(8,128)} %copy-done.3, f32[160,128]{1,0:T(8,128)} %copy-done.2), custom_call_target="tpu_custom_call" | custom-call | tf_op jit(solution)/shard_map/background/pallas_call | solution.py:299
  13.6 4.3 %all-to-all-start = ((f32[8,5,4,128]{3,2,1,0:T(4,128)}), f32[8,5,4,128]{3,2,1,0:T(4,128)S(1)}, u32[]{:S(2)}, u32[]{:S(2)}) async-start(f32[8,5,4,128]{3,2,1,0:T(4,128)} %bitcast.10), calls=%async_computation | async-start | bytes 163840 | tf_op jit(solution)/shard_map/all_to_all | solution.py:306
  17.9 2.0 %statistics.1.own_stats_ref = f32[8,128]{1,0:T(8,128)} custom-call(s32[2]{0:T(128)} %count_ref.1, f32[2,3]{1,0:T(2,128)} %loc_ref.1, s32[2,3]{1,0:T(2,128)} %near_ref.1, f32[2,128]{1,0:T(2,128)} %value_ref.1, s32[2,128]{1,0:T(2,128)} %site_ref.1, f32[2,128]{1,0:T(2,128)} %precision_ref.1), custom_call_target="tpu_custom_call" | custom-call | tf_op jit(solution)/shard_map/statistics/pallas_call | solution.py:292
  19.9 3.7 %all-to-all-done = f32[8,5,4,128]{3,2,1,0:T(4,128)S(1)} async-done(((f32[8,5,4,128]{3,2,1,0:T(4,128)}), f32[8,5,4,128]{3,2,1,0:T(4,128)S(1)}, u32[]{:S(2)}, u32[]{:S(2)}) %all-to-all-start) | async-done | bytes 81952 | tf_op jit(solution)/shard_map/all_to_all | solution.py:306
  23.7 0.0 copy-start
  23.7 0.7 pad_maximum_fusion
  24.3 0.0 copy-done
  24.3 29.0 %collective-permute-start.2 = (f32[168,128]{1,0:T(8,128)S(1)}, f32[168,128]{1,0:T(8,128)S(1)}, u32[]{:S(2)}, u32[]{:S(2)}) collective-permute-start(f32[168,128]{1,0:T(8,128)S(1)} %pad_maximum_fusion), channel_id=1, source_target_pairs={{0,8},{8,0},{1,9},{9,1},{2,10},{10,2},{3,11},{11,3},{4,12},{12,4},... | collective-permute-start | bytes 258056 | tf_op jit(solution)/shard_map/ppermute | solution.py:308
  53.3 2.9 %collective-permute-done.2.other_ref = f32[168,128]{1,0:T(8,128)S(1)} collective-permute-done((f32[168,128]{1,0:T(8,128)S(1)}, f32[168,128]{1,0:T(8,128)S(1)}, u32[]{:S(2)}, u32[]{:S(2)}) %collective-permute-start.2) | collective-permute-done | bytes 86048 | tf_op jit(solution)/shard_map/ppermute | solution.py:308
  56.2 0.0 copy-start.1
  56.2 0.6 copy-done.1
  56.8 5.9 %analysis.1 = f32[160,128]{1,0:T(8,128)} custom-call(s32[1]{0:T(128)} %bitcast.half_ref, f32[160,128]{1,0:T(8,128)} %bitcast.9, f32[168,128]{1,0:T(8,128)} %copy-done.1, f32[8,128]{1,0:T(8,128)} %statistics.1.own_stats_ref), custom_call_target="tpu_custom_call" | custom-call | tf_op jit(solution)/shard_map/analysis/pallas_call | solution.py:309
  62.8 9.7 %all_to_all.10 = f32[8,5,4,128]{3,2,1,0:T(4,128)} all-to-all(f32[8,5,4,128]{3,2,1,0:T(4,128)} %bitcast.11), channel_id=1, replica_groups=mesh['band'=64,'half'=2,'q'=8] {'q'}, dimensions={0} | all-to-all | bytes 163840 | tf_op jit(solution)/shard_map/all_to_all | solution.py:316
  72.4 1.7 %unpack.1 = (f32[80,128]{1,0:T(8,128)}, f32[80,128]{1,0:T(8,128)}) custom-call(f32[160,128]{1,0:T(8,128)} %bitcast.12), custom_call_target="tpu_custom_call" | custom-call | tf_op jit(solution)/shard_map/unpack/pallas_call | solution.py:319
  74.1 14.5 %collective-permute-start.3 = (f32[80,128]{1,0:T(8,128)}, f32[80,128]{1,0:T(8,128)S(1)}, u32[]{:S(2)}, u32[]{:S(2)}) collective-permute-start(f32[80,128]{1,0:T(8,128)} %get-tuple-element.7.high_ref), channel_id=1, source_target_pairs={{0,16},{16,32},{32,48},{48,64},{64,80},{80,96},{96,112},{112,128},... | collective-permute-start | bytes 122888 | tf_op jit(solution)/shard_map/ppermute | solution.py:326
  88.6 1.9 %collective-permute-start.4 = (f32[80,128]{1,0:T(8,128)}, f32[80,128]{1,0:T(8,128)S(1)}, u32[]{:S(2)}, u32[]{:S(2)}) collective-permute-start(f32[80,128]{1,0:T(8,128)} %get-tuple-element.8.low_ref), channel_id=1, source_target_pairs={{16,0},{32,16},{48,32},{64,48},{80,64},{96,80},{112,96},{128,112},... | collective-permute-start | bytes 122888 | tf_op jit(solution)/shard_map/ppermute | solution.py:327
  90.5 0.0 collective-permute-done.3.below_ref
  90.6 0.0 copy-start.4
  90.6 6.2 %collective-permute-done.4.above_ref = f32[80,128]{1,0:T(8,128)S(1)} collective-permute-done((f32[80,128]{1,0:T(8,128)}, f32[80,128]{1,0:T(8,128)S(1)}, u32[]{:S(2)}, u32[]{:S(2)}) %collective-permute-start.4) | collective-permute-done | bytes 40992 | tf_op jit(solution)/shard_map/ppermute | solution.py:327
  96.8 0.0 copy-done.4
  96.8 0.0 copy-start.5
  96.8 0.6 copy-done.5
  97.4 1.8 %forecast.1 = f32[160,128]{1,0:T(8,128)} custom-call(f32[80,128]{1,0:T(8,128)} %copy-done.4, f32[80,128]{1,0:T(8,128)} %get-tuple-element.8.low_ref, f32[80,128]{1,0:T(8,128)} %get-tuple-element.7.high_ref, f32[80,128]{1,0:T(8,128)} %copy-done.5), custom_call_target="tpu_custom_call" | custom-call | tf_op jit(solution)/shard_map/forecast/pallas_call | solution.py:328
Async XLA Ops:
  0.0 8.6 %collective-permute-start.1 = (f32[160,128]{1,0:T(8,128)}, f32[160,128]{1,0:T(8,128)S(1)}, u32[]{:S(2)}, u32[]{:S(2)}) collective-permute-start(f32[160,128]{1,0:T(8,128)} %bitcast.13), channel_id=1, source_target_pairs={{16,0},{32,16},{48,32},{64,48},{80,64},{96,80},{112,96},{128,112},... | collective-permute-start | bytes 245768 | tf_op jit(solution)/shard_map/ppermute | solution.py:291
  2.6 7.7 %collective-permute-start = (f32[160,128]{1,0:T(8,128)}, f32[160,128]{1,0:T(8,128)S(1)}, u32[]{:S(2)}, u32[]{:S(2)}) collective-permute-start(f32[160,128]{1,0:T(8,128)} %bitcast.14), channel_id=1, source_target_pairs={{0,16},{16,32},{32,48},{48,64},{64,80},{80,96},{96,112},{112,128},... | collective-permute-start | bytes 245768 | tf_op jit(solution)/shard_map/ppermute | solution.py:290
  8.6 1.7 %copy-start.2 = (f32[160,128]{1,0:T(8,128)}, f32[160,128]{1,0:T(8,128)S(1)}, u32[]{:S(2)}) copy-start(f32[160,128]{1,0:T(8,128)S(1)} %collective-permute-done.1.high_ref) | copy-start | bytes 245764
  10.3 0.6 copy-start.3
  13.6 10.0 %all-to-all-start = ((f32[8,5,4,128]{3,2,1,0:T(4,128)}), f32[8,5,4,128]{3,2,1,0:T(4,128)S(1)}, u32[]{:S(2)}, u32[]{:S(2)}) async-start(f32[8,5,4,128]{3,2,1,0:T(4,128)} %bitcast.10), calls=%async_computation | async-start | bytes 163840 | tf_op jit(solution)/shard_map/all_to_all | solution.py:306
  23.7 0.7 copy-start
  24.3 31.9 %collective-permute-start.2 = (f32[168,128]{1,0:T(8,128)S(1)}, f32[168,128]{1,0:T(8,128)S(1)}, u32[]{:S(2)}, u32[]{:S(2)}) collective-permute-start(f32[168,128]{1,0:T(8,128)S(1)} %pad_maximum_fusion), channel_id=1, source_target_pairs={{0,8},{8,0},{1,9},{9,1},{2,10},{10,2},{3,11},{11,3},{4,12},{12,4},... | collective-permute-start | bytes 258056 | tf_op jit(solution)/shard_map/ppermute | solution.py:308
  56.2 0.6 copy-start.1
  74.1 16.5 %collective-permute-start.3 = (f32[80,128]{1,0:T(8,128)}, f32[80,128]{1,0:T(8,128)S(1)}, u32[]{:S(2)}, u32[]{:S(2)}) collective-permute-start(f32[80,128]{1,0:T(8,128)} %get-tuple-element.7.high_ref), channel_id=1, source_target_pairs={{0,16},{16,32},{32,48},{48,64},{64,80},{80,96},{96,112},{112,128},... | collective-permute-start | bytes 122888 | tf_op jit(solution)/shard_map/ppermute | solution.py:326
  88.6 8.2 %collective-permute-start.4 = (f32[80,128]{1,0:T(8,128)}, f32[80,128]{1,0:T(8,128)S(1)}, u32[]{:S(2)}, u32[]{:S(2)}) collective-permute-start(f32[80,128]{1,0:T(8,128)} %get-tuple-element.8.low_ref), channel_id=1, source_target_pairs={{16,0},{32,16},{48,32},{64,48},{80,64},{96,80},{112,96},{128,112},... | collective-permute-start | bytes 122888 | tf_op jit(solution)/shard_map/ppermute | solution.py:327
  90.6 6.2 %copy-start.4 = (f32[80,128]{1,0:T(8,128)}, f32[80,128]{1,0:T(8,128)S(1)}, u32[]{:S(2)}) copy-start(f32[80,128]{1,0:T(8,128)S(1)} %collective-permute-done.3.below_ref) | copy-start | bytes 122884
  96.8 0.6 copy-start.5

commit v2 on v1

--- a/solution.py
+++ b/solution.py
@@ -12,6 +12,7 @@
 MEMBERS = 128
 VMEM = pl.BlockSpec(memory_space=pltpu.VMEM)
 SMEM = pl.BlockSpec(memory_space=pltpu.SMEM)
+SMALL = pltpu.CompilerParams(vmem_limit_bytes=8 * 2**20)
 
 
 def half_minmod(lower, upper):
@@ -294,6 +295,7 @@
         out_shape=array(8, 128),
         in_specs=[SMEM] * 3 + [VMEM] * 3,
         out_specs=VMEM,
+        compiler_params=SMALL,
         name="statistics",
     )(obs_count, loc_weight, neighbours, obs_value, obs_site, obs_precision)
     packed = pl.pallas_call(
@@ -301,6 +303,7 @@
         out_shape=array(160, 128),
         in_specs=[SMEM] + [VMEM] * 3,
         out_specs=VMEM,
+        compiler_params=SMALL,
         name="background",
     )(here, fields, low, high)
     own = lax.all_to_all(packed.reshape(8, 5, 4, 128), "q", split_axis=0, concat_axis=0, tiled=True)
@@ -311,6 +314,7 @@
         out_shape=array(160, 128),
         in_specs=[SMEM] + [VMEM] * 3,
         out_specs=VMEM,
+        compiler_params=SMALL,
         name="analysis",
     )(jnp.reshape(lax.axis_index("half"), (1,)), own, other, stats)
     returned = lax.all_to_all(
@@ -321,6 +325,7 @@
         out_shape=(array(80, 128), array(80, 128)),
         in_specs=[VMEM],
         out_specs=(VMEM, VMEM),
+        compiler_params=SMALL,
         name="unpack",
     )(returned.reshape(160, 128))
     below = lax.ppermute(high, "band", forward)
@@ -330,6 +335,7 @@
         out_shape=array(160, 128),
         in_specs=[VMEM] * 4,
         out_specs=VMEM,
+        compiler_params=SMALL,
         name="forecast",
     )(below, low, high, above)
     return out.reshape(8, 5, 4, 128)

time: 99.8 us -> 92 us (0.922)
  Pallas kernels: 14.1 us -> 8.86 us
  blocking collectives: 9.66 us -> 8.08 us
  other arithmetic: 1.33 us -> 0.08 us
  waiting for transfers between devices: 14.6 us -> 15.8 us
    all_to_all x1, blocking collectives: 9.66 us -> 8.08 us  [shards(): lax.all_to_all(analysed.reshape(8, 5, 4, 128), 'q', split_axis=0, concat_...]
    pallas_call x1, Pallas kernels: 5.91 us -> 4.35 us  [shards(): pl.pallas_call(analysis_kernel, out_shape=array(160, 128), in_specs=[SMEM...]
    pallas_call x1, Pallas kernels: 1.7 us -> 0.2 us  [shards(): pl.pallas_call(unpack_kernel, out_shape=(array(80, 128), array(80, 128)),...]
  transfers between devices with their start and end apart: 6 -> 6, of which waited for: 4 -> 5; matrix products, arithmetic and copies ran while one was open for 1% -> 0% of each run, Pallas kernels for 2% -> 1%
where the time goes in v2:
time: 92 us; the launch traced here: 91.6 us
  starting transfers between devices  57.8 us (63%)
  waiting for transfers between devices  15.8 us (17%)
  Pallas kernels  8.86 us (10%)
  blocking collectives  8.08 us (9%)
    ppermute x1, starting transfers between devices, shards(): lax.ppermute(jnp.concatenate([own, stats], axis=0), 'half', [(0, 1), (1,...  29 us
    ppermute x1, starting transfers between devices, shards(): below = lax.ppermute(high, 'band', forward)  14.5 us
    all_to_all x1, blocking collectives, shards(): lax.all_to_all(analysed.reshape(8, 5, 4, 128), 'q', split_axis=0, concat_...  8.08 us
    ppermute x1, waiting for transfers between devices, shards(): above = lax.ppermute(low, 'band', backward)  6.07 us
    ppermute x1, starting transfers between devices, shards(): low = lax.ppermute(fields, 'band', forward)  5.3 us
    all_to_all x1, waiting for transfers between devices, shards(): lax.all_to_all(packed.reshape(8, 5, 4, 128), 'q', split_axis=0, concat_ax...  4.56 us
    all_to_all x1, starting transfers between devices, shards(): lax.all_to_all(packed.reshape(8, 5, 4, 128), 'q', split_axis=0, concat_ax...  4.44 us
    pallas_call x1, Pallas kernels, shards(): pl.pallas_call(analysis_kernel, out_shape=array(160, 128), in_specs=[SMEM...  4.35 us
  transfers between devices with their start and end apart: 6, of which 5 were waited for; matrix products, arithmetic and copies ran while one was open for 0% of the time, Pallas kernels for 1%

profile of v2, /device:TPU:24, one launch (start us, length us, event | category | flops | bytes accessed | tf_op | source)
XLA Modules:
  0.0 91.6 jit_solution(8640286737957685777)
XLA Ops:
  0.0 2.6 %collective-permute-start.1 = (f32[160,128]{1,0:T(8,128)}, f32[160,128]{1,0:T(8,128)S(1)}, u32[]{:S(2)}, u32[]{:S(2)}) collective-permute-start(f32[160,128]{1,0:T(8,128)} %bitcast.12), channel_id=1, source_target_pairs={{16,0},{32,16},{48,32},{64,48},{80,64},{96,80},{112,96},{128,112},... | collective-permute-start | bytes 245768 | tf_op jit(solution)/shard_map/ppermute | solution.py:292
  2.6 5.3 %collective-permute-start = (f32[160,128]{1,0:T(8,128)}, f32[160,128]{1,0:T(8,128)S(1)}, u32[]{:S(2)}, u32[]{:S(2)}) collective-permute-start(f32[160,128]{1,0:T(8,128)} %bitcast.13), channel_id=1, source_target_pairs={{0,16},{16,32},{32,48},{48,64},{64,80},{80,96},{96,112},{112,128},... | collective-permute-start | bytes 245768 | tf_op jit(solution)/shard_map/ppermute | solution.py:291
  8.0 0.1 pad_add_fusion.band_ref
  8.0 0.6 collective-permute-done.1.high_ref
  8.6 1.7 %collective-permute-done.low_ref = f32[160,128]{1,0:T(8,128)S(1)} collective-permute-done((f32[160,128]{1,0:T(8,128)}, f32[160,128]{1,0:T(8,128)S(1)}, u32[]{:S(2)}, u32[]{:S(2)}) %collective-permute-start) | collective-permute-done | bytes 81952 | tf_op jit(solution)/shard_map/ppermute | solution.py:291
  10.3 0.0 copy-start
  10.3 0.9 copy-done
  11.2 2.3 %background.1 = f32[160,128]{1,0:T(8,128)} custom-call(s32[2]{0:T(128)S(1)} %pad_add_fusion.band_ref, f32[160,128]{1,0:T(8,128)S(1)} %bitcast.14, f32[160,128]{1,0:T(8,128)S(1)} %collective-permute-done.low_ref, f32[160,128]{1,0:T(8,128)S(1)} %collective-permute-done.1.high_ref), custom_call_target="tpu_custom_call" | custom-call | tf_op jit(solution)/shard_map/background/pallas_call | solution.py:301
  13.5 0.0 copy-start.1
  13.5 0.0 copy-start.2
  13.5 0.0 copy-start.3
  13.5 0.0 copy-start.5
  13.5 0.0 copy-start.6
  13.5 4.4 %all-to-all-start = ((f32[8,5,4,128]{3,2,1,0:T(4,128)}), f32[8,5,4,128]{3,2,1,0:T(4,128)S(1)}, u32[]{:S(2)}, u32[]{:S(2)}) async-start(f32[8,5,4,128]{3,2,1,0:T(4,128)} %bitcast.3), calls=%async_computation | async-start | bytes 163840 | tf_op jit(solution)/shard_map/all_to_all | solution.py:309
  17.9 0.0 copy-done.1
  18.0 0.0 copy-done.2
  18.0 0.0 copy-done.3
  18.0 0.0 copy-done.4
  18.0 0.0 copy-done.5
  18.0 0.0 copy-done.6
  18.0 1.1 %statistics.1.own_stats_ref = f32[8,128]{1,0:T(8,128)S(1)} custom-call(s32[2]{0:T(128)S(1)} %copy-done.6, f32[2,3]{1,0:T(2,128)S(1)} %copy-done.1, s32[2,3]{1,0:T(2,128)S(1)} %copy-done.2, f32[2,128]{1,0:T(2,128)S(1)} %copy-done.3, s32[2,128]{1,0:T(2,128)S(1)} %copy-done.4, f32[2,128]{1,0:T(2,128)S(1)} %copy-done.5), custom_call_target="tpu_custom_call" | custom-call | tf_op jit(solution)/shard_map/statistics/pallas_call | solution.py:293
  19.1 4.6 %all-to-all-done = f32[8,5,4,128]{3,2,1,0:T(4,128)S(1)} async-done(((f32[8,5,4,128]{3,2,1,0:T(4,128)}), f32[8,5,4,128]{3,2,1,0:T(4,128)S(1)}, u32[]{:S(2)}, u32[]{:S(2)}) %all-to-all-start) | async-done | bytes 81952 | tf_op jit(solution)/shard_map/all_to_all | solution.py:309
  23.7 29.0 %collective-permute-start.2 = (f32[168,128]{1,0:T(8,128)S(1)}, f32[168,128]{1,0:T(8,128)S(1)}, u32[]{:S(2)}, u32[]{:S(2)}) collective-permute-start(f32[168,128]{1,0:T(8,128)S(1)} %pad_maximum_fusion), channel_id=1, source_target_pairs={{0,8},{8,0},{1,9},{9,1},{2,10},{10,2},{3,11},{11,3},{4,12},{12,4},... | collective-permute-start | bytes 258056 | tf_op jit(solution)/shard_map/ppermute | solution.py:311
  52.6 2.9 %collective-permute-done.2.other_ref = f32[168,128]{1,0:T(8,128)S(1)} collective-permute-done((f32[168,128]{1,0:T(8,128)S(1)}, f32[168,128]{1,0:T(8,128)S(1)}, u32[]{:S(2)}, u32[]{:S(2)}) %collective-permute-start.2) | collective-permute-done | bytes 86048 | tf_op jit(solution)/shard_map/ppermute | solution.py:311
  55.5 4.4 %analysis.1 = f32[160,128]{1,0:T(8,128)S(1)} custom-call(s32[1]{0:T(128)} %bitcast.half_ref, f32[160,128]{1,0:T(8,128)S(1)} %bitcast.9, f32[168,128]{1,0:T(8,128)S(1)} %collective-permute-done.2.other_ref, f32[8,128]{1,0:T(8,128)S(1)} %statistics.1.own_stats_ref), custom_call_target="tpu_custom_call" | custom-call | tf_op jit(solution)/shard_map/analysis/pallas_call | solution.py:312
  59.9 8.1 %all_to_all.10 = f32[8,5,4,128]{3,2,1,0:T(4,128)S(1)} all-to-all(f32[8,5,4,128]{3,2,1,0:T(4,128)S(1)} %bitcast.10), channel_id=1, replica_groups=mesh['band'=64,'half'=2,'q'=8] {'q'}, dimensions={0} | all-to-all | bytes 163840 | tf_op jit(solution)/shard_map/all_to_all | solution.py:320
  68.0 0.2 unpack.1
  68.2 14.5 %collective-permute-start.3 = (f32[80,128]{1,0:T(8,128)S(1)}, f32[80,128]{1,0:T(8,128)S(1)}, u32[]{:S(2)}, u32[]{:S(2)}) collective-permute-start(f32[80,128]{1,0:T(8,128)S(1)} %get-tuple-element.7.high_ref), channel_id=1, source_target_pairs={{0,16},{16,32},{32,48},{48,64},{64,80},{80,96},{96,112},{112,128},... | collective-permute-start | bytes 122888 | tf_op jit(solution)/shard_map/ppermute | solution.py:331
  82.7 1.9 %collective-permute-start.4 = (f32[80,128]{1,0:T(8,128)S(1)}, f32[80,128]{1,0:T(8,128)S(1)}, u32[]{:S(2)}, u32[]{:S(2)}) collective-permute-start(f32[80,128]{1,0:T(8,128)S(1)} %get-tuple-element.8.low_ref), channel_id=1, source_target_pairs={{16,0},{32,16},{48,32},{64,48},{80,64},{96,80},{112,96},{128,112},... | collective-permute-start | bytes 122888 | tf_op jit(solution)/shard_map/ppermute | solution.py:332
  84.6 0.0 collective-permute-done.3.below_ref
  84.6 6.1 %collective-permute-done.4.above_ref = f32[80,128]{1,0:T(8,128)S(1)} collective-permute-done((f32[80,128]{1,0:T(8,128)S(1)}, f32[80,128]{1,0:T(8,128)S(1)}, u32[]{:S(2)}, u32[]{:S(2)}) %collective-permute-start.4) | collective-permute-done | bytes 40992 | tf_op jit(solution)/shard_map/ppermute | solution.py:332
  90.7 0.9 %forecast.1 = f32[160,128]{1,0:T(8,128)} custom-call(f32[80,128]{1,0:T(8,128)S(1)} %collective-permute-done.3.below_ref, f32[80,128]{1,0:T(8,128)S(1)} %get-tuple-element.8.low_ref, f32[80,128]{1,0:T(8,128)S(1)} %get-tuple-element.7.high_ref, f32[80,128]{1,0:T(8,128)S(1)} %collective-permute-done.4.above_ref), custom_call_target="tpu_custom_call" | custom-call | tf_op jit(solution)/shard_map/forecast/pallas_call | solution.py:333
  (2 shorter events, 0.0 us)
Async XLA Ops:
  0.0 8.6 %collective-permute-start.1 = (f32[160,128]{1,0:T(8,128)}, f32[160,128]{1,0:T(8,128)S(1)}, u32[]{:S(2)}, u32[]{:S(2)}) collective-permute-start(f32[160,128]{1,0:T(8,128)} %bitcast.12), channel_id=1, source_target_pairs={{16,0},{32,16},{48,32},{64,48},{80,64},{96,80},{112,96},{128,112},... | collective-permute-start | bytes 245768 | tf_op jit(solution)/shard_map/ppermute | solution.py:292
  2.6 7.7 %collective-permute-start = (f32[160,128]{1,0:T(8,128)}, f32[160,128]{1,0:T(8,128)S(1)}, u32[]{:S(2)}, u32[]{:S(2)}) collective-permute-start(f32[160,128]{1,0:T(8,128)} %bitcast.13), channel_id=1, source_target_pairs={{0,16},{16,32},{32,48},{48,64},{64,80},{80,96},{96,112},{112,128},... | collective-permute-start | bytes 245768 | tf_op jit(solution)/shard_map/ppermute | solution.py:291
  10.3 0.9 copy-start
  13.5 4.5 %copy-start.1 = (f32[2,3]{1,0:T(2,128)S(1)}, f32[2,3]{1,0:T(2,128)}, u32[]{:S(2)}) copy-start(f32[2,3]{1,0:T(2,128)} %loc_ref.1) | copy-start | bytes 76
  13.5 4.5 %copy-start.2 = (s32[2,3]{1,0:T(2,128)S(1)}, s32[2,3]{1,0:T(2,128)}, u32[]{:S(2)}) copy-start(s32[2,3]{1,0:T(2,128)} %near_ref.1) | copy-start | bytes 76
  13.5 4.5 %copy-start.3 = (f32[2,128]{1,0:T(2,128)S(1)}, f32[2,128]{1,0:T(2,128)}, u32[]{:S(2)}) copy-start(f32[2,128]{1,0:T(2,128)} %value_ref.1) | copy-start | bytes 3076
  13.5 4.5 %copy-start.4 = (s32[2,128]{1,0:T(2,128)S(1)}, s32[2,128]{1,0:T(2,128)}, u32[]{:S(2)}) copy-start(s32[2,128]{1,0:T(2,128)} %site_ref.1) | copy-start | bytes 3076
  13.5 4.5 %copy-start.5 = (f32[2,128]{1,0:T(2,128)S(1)}, f32[2,128]{1,0:T(2,128)}, u32[]{:S(2)}) copy-start(f32[2,128]{1,0:T(2,128)} %precision_ref.1) | copy-start | bytes 3076
  13.5 4.5 %copy-start.6 = (s32[2]{0:T(128)S(1)}, s32[2]{0:T(128)}, u32[]{:S(2)}) copy-start(s32[2]{0:T(128)} %count_ref.1) | copy-start | bytes 28
  13.5 10.2 %all-to-all-start = ((f32[8,5,4,128]{3,2,1,0:T(4,128)}), f32[8,5,4,128]{3,2,1,0:T(4,128)S(1)}, u32[]{:S(2)}, u32[]{:S(2)}) async-start(f32[8,5,4,128]{3,2,1,0:T(4,128)} %bitcast.3), calls=%async_computation | async-start | bytes 163840 | tf_op jit(solution)/shard_map/all_to_all | solution.py:309
  23.7 31.9 %collective-permute-start.2 = (f32[168,128]{1,0:T(8,128)S(1)}, f32[168,128]{1,0:T(8,128)S(1)}, u32[]{:S(2)}, u32[]{:S(2)}) collective-permute-start(f32[168,128]{1,0:T(8,128)S(1)} %pad_maximum_fusion), channel_id=1, source_target_pairs={{0,8},{8,0},{1,9},{9,1},{2,10},{10,2},{3,11},{11,3},{4,12},{12,4},... | collective-permute-start | bytes 258056 | tf_op jit(solution)/shard_map/ppermute | solution.py:311
  68.2 16.4 %collective-permute-start.3 = (f32[80,128]{1,0:T(8,128)S(1)}, f32[80,128]{1,0:T(8,128)S(1)}, u32[]{:S(2)}, u32[]{:S(2)}) collective-permute-start(f32[80,128]{1,0:T(8,128)S(1)} %get-tuple-element.7.high_ref), channel_id=1, source_target_pairs={{0,16},{16,32},{32,48},{48,64},{64,80},{80,96},{96,112},{112,128},... | collective-permute-start | bytes 122888 | tf_op jit(solution)/shard_map/ppermute | solution.py:331
  82.7 8.0 %collective-permute-start.4 = (f32[80,128]{1,0:T(8,128)S(1)}, f32[80,128]{1,0:T(8,128)S(1)}, u32[]{:S(2)}, u32[]{:S(2)}) collective-permute-start(f32[80,128]{1,0:T(8,128)S(1)} %get-tuple-element.8.low_ref), channel_id=1, source_target_pairs={{16,0},{32,16},{48,32},{64,48},{80,64},{96,80},{112,96},{128,112},... | collective-permute-start | bytes 122888 | tf_op jit(solution)/shard_map/ppermute | solution.py:332

commit v3 on v1

--- a/solution.py
+++ b/solution.py
@@ -6,12 +6,14 @@
 from jax.sharding import Mesh, PartitionSpec as P
 
 NSI = 6
-STEPS = 2
 COURANT = 0.08
 HIGHEST = lax.Precision.HIGHEST
 MEMBERS = 128
 VMEM = pl.BlockSpec(memory_space=pltpu.VMEM)
+HBM = pl.BlockSpec(memory_space=pltpu.HBM)
 SMEM = pl.BlockSpec(memory_space=pltpu.SMEM)
+LARGE = pltpu.CompilerParams(vmem_limit_bytes=60 * 2**20)
+SMALL = pltpu.CompilerParams(vmem_limit_bytes=8 * 2**20)
 
 
 def half_minmod(lower, upper):
@@ -71,7 +73,7 @@
     return lax.broadcasted_iota(jnp.int32, shape, 1)
 
 
-def background_kernel(band_ref, centre_ref, low_ref, high_ref, out_ref):
+def background(band_ref, centre_ref, low_ref, high_ref, out_ref, offset):
     def row(ref, r):
         return [ref[pl.ds(v * 4 + r, 8, stride=20), :] for v in range(5)]
 
@@ -88,6 +90,7 @@
     group = lane >> 4
     for q in range(8):
         j = q % 4
+        at = q * 40 + offset
         chosen = (q // 4, 2 + q // 4)
         for b in (0, 1):
             slab = None
@@ -95,38 +98,45 @@
                 u, v = g // 4, g % 4
                 piece = turned(rows[chosen[b]][v], g - (2 * j + u))
                 slab = piece if slab is None else jnp.where(group == g, piece, slab)
-            out_ref[q * 20 + 8 * b : q * 20 + 8 * b + 8, :] = slab
+            out_ref[at + 8 * b : at + 8 * b + 8, :] = slab
         last = jnp.where(
             lane < 32, turned(rows[chosen[0]][4], -2 * j), turned(rows[chosen[1]][4], 2 - 2 * j)
         )
-        out_ref[q * 20 + 16 : q * 20 + 20, :] = jnp.where(
+        out_ref[at + 16 : at + 20, :] = jnp.where(
             lane[:4] < 64, last[:4], pltpu.roll(last, 64, 1)[4:]
         )
 
 
-def statistics_kernel(count_ref, loc_ref, near_ref, value_ref, site_ref, precision_ref, out_ref):
+def own_background_kernel(band_ref, centre_ref, low_ref, high_ref, out_ref):
+    background(band_ref, centre_ref, low_ref, high_ref, out_ref, 0)
+
+
+def other_background_kernel(band_ref, centre_ref, low_ref, high_ref, own_ref, out_ref):
+    for q in range(8):
+        out_ref[q * 40 : q * 40 + 20, :] = own_ref[q * 40 : q * 40 + 20, :]
+    background(band_ref, centre_ref, low_ref, high_ref, out_ref, 20)
+
+
+def head_kernel(*refs):
+    sources, out_ref, targets, arrived = refs[:7], refs[7], refs[8:14], refs[14]
+    fields = pltpu.make_async_copy(sources[0], out_ref.at[0:160, :], arrived.at[0])
+    fields.start()
+    rest = [
+        pltpu.make_async_copy(source, target, arrived.at[n + 1])
+        for n, (source, target) in enumerate(zip(sources[1:], targets))
+    ]
+    for copy in rest:
+        copy.start()
+    for copy in rest:
+        copy.wait()
+    count_ref, loc_ref, near_ref, value_ref, site_ref, precision_ref = targets
     slot = lanes_of((1, 128))
-    sub = lax.broadcasted_iota(jnp.int32, (8, 128), 0)
-    lane = lanes_of((8, 128))
-    cell = lax.broadcasted_iota(jnp.int32, (128, 128), 0)
-    slab = jnp.zeros((8, 128), jnp.float32)
-    last = jnp.zeros((8, 128), jnp.float32)
+    out_ref[160:162, :] = value_ref[...]
+    out_ref[162:164, :] = site_ref[...].astype(jnp.float32)
     for u in (0, 1):
-        weight = jnp.where(slot < count_ref[u], precision_ref[u : u + 1, :], 0.0)
-        both = jnp.where(sub == 0, weight, jnp.where(sub == 1, weight * value_ref[u : u + 1, :], 0.0))
-        site = site_ref[u : u + 1, :]
-        in_slab = ((cell & 63) == site) & ((cell >> 6) == u)
-        in_last = ((64 + (cell & 15)) == site) & (((cell >> 4) & 1) == u)
-        dims = (((1,), (1,)), ((), ()))
-        slab += lax.dot_general(
-            both, in_slab.astype(jnp.float32), dims, precision=HIGHEST,
-            preferred_element_type=jnp.float32,
-        )
-        last += lax.dot_general(
-            both, in_last.astype(jnp.float32), dims, precision=HIGHEST,
-            preferred_element_type=jnp.float32,
-        )
-    out = jnp.where(sub < 2, slab, jnp.where(sub < 4, pltpu.roll(last, 2, 0), 0.0))
+        out_ref[164 + u : 165 + u, :] = jnp.where(
+            slot < count_ref[u], precision_ref[u : u + 1, :], 0.0
+        )
     for t in (0, 1):
         gain = []
         for u in (0, 1):
@@ -134,16 +144,47 @@
             for n in range(3):
                 total += jnp.where(near_ref[t, n] == u, loc_ref[t, n], 0.0)
             gain.append(total)
-        out = jnp.where(sub == 4 + t, jnp.where((lane >> 6) == 0, gain[0], gain[1]), out)
-        out = jnp.where(sub == 6 + t, jnp.where(((lane >> 4) & 1) == 0, gain[0], gain[1]), out)
-    out_ref[...] = out
+        out_ref[166 + t : 167 + t, :] = jnp.where(slot < 64, gain[0], gain[1])
+    fields.wait()
+
+
+def statistics_kernel(own_ref, other_ref, out_ref):
+    sub = lax.broadcasted_iota(jnp.int32, (8, 128), 0)
+    lane = lanes_of((8, 128))
+    cell = lax.broadcasted_iota(jnp.int32, (128, 128), 0)
+    dims = (((1,), (1,)), ((), ()))
+    for k, ref in enumerate((own_ref, other_ref)):
+        slab = jnp.zeros((8, 128), jnp.float32)
+        last = jnp.zeros((8, 128), jnp.float32)
+        for u in (0, 1):
+            value = ref[160 + u : 161 + u, :]
+            site = ref[162 + u : 163 + u, :].astype(jnp.int32)
+            weight = ref[164 + u : 165 + u, :]
+            both = jnp.where(sub == 0, weight, jnp.where(sub == 1, weight * value, 0.0))
+            in_slab = ((cell & 63) == site) & ((cell >> 6) == u)
+            in_last = ((64 + (cell & 15)) == site) & (((cell >> 4) & 1) == u)
+            slab += lax.dot_general(
+                both, in_slab.astype(jnp.float32), dims, precision=HIGHEST,
+                preferred_element_type=jnp.float32,
+            )
+            last += lax.dot_general(
+                both, in_last.astype(jnp.float32), dims, precision=HIGHEST,
+                preferred_element_type=jnp.float32,
+            )
+        out = jnp.where(sub < 2, slab, jnp.where(sub < 4, pltpu.roll(last, 2, 0), 0.0))
+        for t in (0, 1):
+            gain = ref[166 + t : 167 + t, :]
+            out = jnp.where(sub == 4 + t, gain, out)
+            gain = jnp.where(((lane >> 4) & 1) == 0, gain[:, 0:1], gain[:, 64:65])
+            out = jnp.where(sub == 6 + t, gain, out)
+        out_ref[8 * k : 8 * k + 8, :] = out
 
 
 def dot(a, b):
     return jnp.dot(a, b, precision=HIGHEST, preferred_element_type=jnp.float32)
 
 
-def analysis_kernel(half_ref, own_ref, other_ref, own_stats_ref, out_ref):
+def analysis_kernel(half_ref, in_ref, stats_ref, out_ref):
     lane8 = lanes_of((8, 128))
     sub8 = lax.broadcasted_iota(jnp.int32, (8, 128), 0)
     lane = lanes_of((MEMBERS, 128))
@@ -153,17 +194,17 @@
         slabs.append(
             jnp.concatenate(
                 [
-                    ref[s * 20 + 8 * b : s * 20 + 8 * b + 8, :]
-                    for ref in (own_ref, other_ref)
+                    in_ref[s * 40 + start + 8 * b : s * 40 + start + 8 * b + 8, :]
+                    for start in (0, 20)
                     for s in range(8)
                 ],
                 axis=0,
             )
         )
     parts = []
-    for ref in (own_ref, other_ref):
+    for start in (0, 20):
         for s in range(8):
-            four = ref[s * 20 + 16 : s * 20 + 20, :]
+            four = in_ref[s * 40 + start + 16 : s * 40 + start + 20, :]
             eight = jnp.concatenate([four, four], axis=0)
             eight = jnp.where(sub8 < 4, eight, pltpu.roll(eight, 64, 1))
             parts.append(jnp.where(lane8 < 64, eight, 0.0))
@@ -171,8 +212,8 @@
     means = [jnp.sum(x, axis=0, keepdims=True) * (1.0 / MEMBERS) for x in slabs]
     slabs = [x - m for x, m in zip(slabs, means)]
     first = half_ref[0] == 0
-    own = own_stats_ref[...]
-    other = other_ref[160:168, :]
+    own = stats_ref[0:8, :]
+    other = stats_ref[8:16, :]
     stats = [jnp.where(first, own, other), jnp.where(first, other, own)]
     eye = (lax.broadcasted_iota(jnp.int32, (MEMBERS, 128), 0) == lane).astype(jnp.float32)
     tiles = [(b, t) for b in (0, 1) for t in (0, 1)]
@@ -281,57 +322,65 @@
     return jax.ShapeDtypeStruct(shape, jnp.float32)
 
 
+def call(kernel, name, in_specs, *out, scratch=()):
+    return pl.pallas_call(
+        kernel,
+        out_shape=out if len(out) > 1 else out[0],
+        in_specs=in_specs,
+        out_specs=(VMEM,) * len(out) if len(out) > 1 else VMEM,
+        scratch_shapes=scratch,
+        compiler_params=LARGE if name == "head" else SMALL,
+    )
+
+
+def exchange(x):
+    return lax.all_to_all(
+        x.reshape(8, -1, 4, 128), "q", split_axis=0, concat_axis=0, tiled=True
+    ).reshape(x.shape)
+
+
 def shards(ensemble, obs_value, obs_site, obs_count, obs_precision, loc_weight, neighbours):
     bands = lax.axis_size("band")
     forward = [(i, i + 1) for i in range(bands - 1)]
     backward = [(target, source) for source, target in forward]
     here = jnp.stack([lax.axis_index("band"), jnp.int32(bands)])
-    fields = ensemble.reshape(160, 128)
-    low = lax.ppermute(fields, "band", forward)
-    high = lax.ppermute(fields, "band", backward)
-    stats = pl.pallas_call(
-        statistics_kernel,
-        out_shape=array(8, 128),
-        in_specs=[SMEM] * 3 + [VMEM] * 3,
-        out_specs=VMEM,
-        name="statistics",
-    )(obs_count, loc_weight, neighbours, obs_value, obs_site, obs_precision)
-    packed = pl.pallas_call(
-        background_kernel,
-        out_shape=array(160, 128),
-        in_specs=[SMEM] + [VMEM] * 3,
-        out_specs=VMEM,
-        name="background",
-    )(here, fields, low, high)
-    own = lax.all_to_all(packed.reshape(8, 5, 4, 128), "q", split_axis=0, concat_axis=0, tiled=True)
-    own = own.reshape(160, 128)
-    other = lax.ppermute(jnp.concatenate([own, stats], axis=0), "half", [(0, 1), (1, 0)])
-    analysed = pl.pallas_call(
-        analysis_kernel,
-        out_shape=array(160, 128),
-        in_specs=[SMEM] + [VMEM] * 3,
-        out_specs=VMEM,
-        name="analysis",
-    )(jnp.reshape(lax.axis_index("half"), (1,)), own, other, stats)
-    returned = lax.all_to_all(
-        analysed.reshape(8, 5, 4, 128), "q", split_axis=0, concat_axis=0, tiled=True
-    )
-    low, high = pl.pallas_call(
-        unpack_kernel,
-        out_shape=(array(80, 128), array(80, 128)),
-        in_specs=[VMEM],
-        out_specs=(VMEM, VMEM),
-        name="unpack",
-    )(returned.reshape(160, 128))
+    half = jnp.reshape(lax.axis_index("half"), (1,))
+    own = call(
+        head_kernel, "head", [HBM] * 7, array(168, 128),
+        scratch=[
+            pltpu.SMEM((2,), jnp.int32),
+            pltpu.SMEM((2, 3), jnp.float32),
+            pltpu.SMEM((2, 3), jnp.int32),
+            pltpu.VMEM((2, 128), jnp.float32),
+            pltpu.VMEM((2, 128), jnp.int32),
+            pltpu.VMEM((2, 128), jnp.float32),
+            pltpu.SemaphoreType.DMA((7,)),
+        ],
+    )(
+        ensemble.reshape(160, 128), obs_count, loc_weight, neighbours,
+        obs_value, obs_site, obs_precision,
+    )
+    other = lax.ppermute(own, "half", [(0, 1), (1, 0)])
+    low = lax.ppermute(own, "band", forward)
+    high = lax.ppermute(own, "band", backward)
+    packed = call(
+        own_background_kernel, "own_background", [SMEM] + [VMEM] * 3, array(320, 128)
+    )(here, own, low, high)
+    low = lax.ppermute(other, "band", forward)
+    high = lax.ppermute(other, "band", backward)
+    stats = call(statistics_kernel, "statistics", [VMEM] * 2, array(16, 128))(own, other)
+    packed = call(
+        other_background_kernel, "other_background", [SMEM] + [VMEM] * 4, array(320, 128)
+    )(here, other, low, high, packed)
+    analysed = call(analysis_kernel, "analysis", [SMEM] + [VMEM] * 2, array(160, 128))(
+        half, exchange(packed), stats
+    )
+    low, high = call(unpack_kernel, "unpack", [VMEM], array(80, 128), array(80, 128))(
+        exchange(analysed)
+    )
     below = lax.ppermute(high, "band", forward)
     above = lax.ppermute(low, "band", backward)
-    out = pl.pallas_call(
-        forecast_kernel,
-        out_shape=array(160, 128),
-        in_specs=[VMEM] * 4,
-        out_specs=VMEM,
-        name="forecast",
-    )(below, low, high, above)
+    out = call(forecast_kernel, "forecast", [VMEM] * 4, array(160, 128))(below, low, high, above)
     return out.reshape(8, 5, 4, 128)
 
 

time: 99.8 us -> 94.5 us (0.947)
  starting transfers between devices: 57.6 us -> 61.3 us
  waiting for transfers between devices: 14.6 us -> 11.6 us
  Pallas kernels: 14.1 us -> 12 us
  blocking collectives: 9.66 us -> 8.08 us
  other arithmetic: 1.33 us -> 0.08 us
    ppermute x3 -> x5, starting transfers between devices: 36.9 us -> 49.1 us  [the longest x1 29 us: shards(): other = lax.ppermute(own, 'half', [(0, 1), (1, 0)])]
    ppermute x1, starting transfers between devices: 14.5 us -> 5.85 us  [shards(): below = lax.ppermute(high, 'band', forward)]
    ppermute x3 -> x5, waiting for transfers between devices: 4.58 us -> 0.01 us  [the longest x1 0.01 us: shards(): high = lax.ppermute(own, 'band', backward)]
    pallas_call x5 -> x7, Pallas kernels: 14.1 us -> 12 us  [the longest x1 4.35 us: shards(): call(analysis_kernel, 'analysis', [SMEM] + [VMEM] * 2, array(160, 128))]
    all_to_all x1, waiting for transfers between devices: 3.73 us -> 5.49 us  [exchange(): lax.all_to_all(x.reshape(8, -1, 4, 128), 'q', split_axis=0, concat_axis=0...]
    all_to_all x1, blocking collectives: 9.66 us -> 8.08 us  [exchange(): lax.all_to_all(x.reshape(8, -1, 4, 128), 'q', split_axis=0, concat_axis=0...]
  transfers between devices with their start and end apart: 6 -> 8, of which waited for: 4 -> 2; matrix products, arithmetic and copies ran while one was open for 1% -> 0% of each run, Pallas kernels for 2% -> 3%
where the time goes in v3:
time: 94.5 us; the launch traced here: 94.1 us
  starting transfers between devices  61.3 us (65%)
  Pallas kernels  12 us (13%)
  waiting for transfers between devices  11.6 us (12%)
  blocking collectives  8.08 us (9%)
    ppermute x1, starting transfers between devices, shards(): other = lax.ppermute(own, 'half', [(0, 1), (1, 0)])  29 us
    ppermute x1, starting transfers between devices, shards(): low = lax.ppermute(other, 'band', forward)  10.3 us
    all_to_all x1, blocking collectives, exchange(): lax.all_to_all(x.reshape(8, -1, 4, 128), 'q', split_axis=0, concat_axis=0...  8.08 us
    ppermute x1, waiting for transfers between devices, shards(): above = lax.ppermute(low, 'band', backward)  6.07 us
    ppermute x1, starting transfers between devices, shards(): below = lax.ppermute(high, 'band', forward)  5.85 us
    all_to_all x1, waiting for transfers between devices, exchange(): lax.all_to_all(x.reshape(8, -1, 4, 128), 'q', split_axis=0, concat_axis=0...  5.49 us
    ppermute x1, starting transfers between devices, shards(): low = lax.ppermute(own, 'band', forward)  5.3 us
    all_to_all x1, starting transfers between devices, exchange(): lax.all_to_all(x.reshape(8, -1, 4, 128), 'q', split_axis=0, concat_axis=0...  4.43 us
  transfers between devices with their start and end apart: 8, of which 2 were waited for; matrix products, arithmetic and copies ran while one was open for 0% of the time, Pallas kernels for 3%

profile of v3, /device:TPU:24, one launch (start us, length us, event | category | flops | bytes accessed | tf_op | source)
XLA Modules:
  0.0 94.1 jit_solution(7696809298541960052)
XLA Ops:
  0.0 1.6 %shard_map.73.centre_ref.own_ref = f32[168,128]{1,0:T(8,128)} custom-call(f32[160,128]{1,0:T(8,128)} %bitcast.11, s32[2]{0:T(128)} %refs_1_.1, f32[2,3]{1,0:T(2,128)} %refs_2_.1, s32[2,3]{1,0:T(2,128)} %refs_3_.1, f32[2,128]{1,0:T(2,128)} %refs_4_.1, s32[2,128]{1,0:T(2,128)} %refs_5_.1, f32[2,128]{1,0:T(2,128)} %refs_6_.1), custom_call_target="tpu_custom_call" | custom-call | tf_op jit(solution)/shard_map/pallas_call | solution.py:348
  1.6 29.0 %collective-permute-start = (f32[168,128]{1,0:T(8,128)}, f32[168,128]{1,0:T(8,128)S(1)}, u32[]{:S(2)}, u32[]{:S(2)}) collective-permute-start(f32[168,128]{1,0:T(8,128)} %shard_map.73.centre_ref.own_ref), channel_id=1, source_target_pairs={{0,8},{8,0},{1,9},{9,1},{2,10},{10,2},{3,11},{11,3},{4,12},{12,4},... | collective-permute-start | bytes 258056 | tf_op jit(solution)/shard_map/ppermute | solution.py:363
  30.6 2.7 %collective-permute-start.4 = (f32[168,128]{1,0:T(8,128)}, f32[168,128]{1,0:T(8,128)S(1)}, u32[]{:S(2)}, u32[]{:S(2)}) collective-permute-start(f32[168,128]{1,0:T(8,128)} %shard_map.73.centre_ref.own_ref), channel_id=1, source_target_pairs={{16,0},{32,16},{48,32},{64,48},{80,64},{96,80},{112,96},{128,112},... | collective-permute-start | bytes 258056 | tf_op jit(solution)/shard_map/ppermute | solution.py:365
  33.2 5.3 %collective-permute-start.3 = (f32[168,128]{1,0:T(8,128)}, f32[168,128]{1,0:T(8,128)S(1)}, u32[]{:S(2)}, u32[]{:S(2)}) collective-permute-start(f32[168,128]{1,0:T(8,128)} %shard_map.73.centre_ref.own_ref), channel_id=1, source_target_pairs={{0,16},{16,32},{32,48},{48,64},{64,80},{80,96},{96,112},{112,128},... | collective-permute-start | bytes 258056 | tf_op jit(solution)/shard_map/ppermute | solution.py:364
  38.5 0.0 collective-permute-done.centre_ref.other_ref
  38.6 1.9 %collective-permute-start.2 = (f32[168,128]{1,0:T(8,128)S(1)}, f32[168,128]{1,0:T(8,128)S(1)}, u32[]{:S(2)}, u32[]{:S(2)}) collective-permute-start(f32[168,128]{1,0:T(8,128)S(1)} %collective-permute-done.centre_ref.other_ref), channel_id=1, source_target_pairs={{16,0},{32,16},{48,32},{64,48},{80,64},{96,80},{112,96},{128,112},... | collective-permute-start | bytes 258056 | tf_op jit(solution)/shard_map/ppermute | solution.py:370
  40.5 10.3 %collective-permute-start.1 = (f32[168,128]{1,0:T(8,128)S(1)}, f32[168,128]{1,0:T(8,128)S(1)}, u32[]{:S(2)}, u32[]{:S(2)}) collective-permute-start(f32[168,128]{1,0:T(8,128)S(1)} %collective-permute-done.centre_ref.other_ref), channel_id=1, source_target_pairs={{0,16},{16,32},{32,48},{48,64},{64,80},{80,96},{96,112},{112,128},... | collective-permute-start | bytes 258056 | tf_op jit(solution)/shard_map/ppermute | solution.py:369
  50.8 0.1 pad_add_fusion.band_ref
  50.9 0.0 collective-permute-done.4.high_ref
  50.9 0.0 collective-permute-done.3.low_ref
  50.9 0.0 copy-start
  50.9 0.9 copy-done
  51.8 1.6 %shard_map.74.own_ref = f32[320,128]{1,0:T(8,128)S(1)} custom-call(s32[2]{0:T(128)S(1)} %pad_add_fusion.band_ref, f32[168,128]{1,0:T(8,128)S(1)} %copy-done, f32[168,128]{1,0:T(8,128)S(1)} %collective-permute-done.3.low_ref, f32[168,128]{1,0:T(8,128)S(1)} %collective-permute-done.4.high_ref), custom_call_target="tpu_custom_call" | custom-call | tf_op jit(solution)/shard_map/pallas_call | solution.py:366
  53.4 0.0 collective-permute-done.2.high_ref
  53.4 0.0 collective-permute-done.1.low_ref
  53.4 2.3 %shard_map.75 = f32[320,128]{1,0:T(8,128)} custom-call(s32[2]{0:T(128)S(1)} %pad_add_fusion.band_ref, f32[168,128]{1,0:T(8,128)S(1)} %collective-permute-done.centre_ref.other_ref, f32[168,128]{1,0:T(8,128)S(1)} %collective-permute-done.1.low_ref, f32[168,128]{1,0:T(8,128)S(1)} %collective-permute-done.2.high_ref, f32[320,128]{1,0:T(8,128)S(1)} %shard_map.74.own_ref), custom_call_target="tpu_custom_call" | custom-call | tf_op jit(solution)/shard_map/pallas_call | solution.py:372
  55.7 0.0 copy-start.1
  55.7 4.4 %all-to-all-start = ((f32[8,10,4,128]{3,2,1,0:T(4,128)}), f32[8,10,4,128]{3,2,1,0:T(4,128)S(1)}, u32[]{:S(2)}, u32[]{:S(2)}) async-start(f32[8,10,4,128]{3,2,1,0:T(4,128)} %bitcast.3), calls=%async_computation | async-start | bytes 327680 | tf_op jit(solution)/shard_map/all_to_all | solution.py:337
  60.1 0.0 copy-done.1
  60.2 1.0 %shard_map.76.stats_ref = f32[16,128]{1,0:T(8,128)S(1)} custom-call(f32[168,128]{1,0:T(8,128)S(1)} %copy-done.1, f32[168,128]{1,0:T(8,128)S(1)} %collective-permute-done.centre_ref.other_ref), custom_call_target="tpu_custom_call" | custom-call | tf_op jit(solution)/shard_map/pallas_call | solution.py:371
  61.1 5.5 %all-to-all-done = f32[8,10,4,128]{3,2,1,0:T(4,128)S(1)} async-done(((f32[8,10,4,128]{3,2,1,0:T(4,128)}), f32[8,10,4,128]{3,2,1,0:T(4,128)S(1)}, u32[]{:S(2)}, u32[]{:S(2)}) %all-to-all-start) | async-done | bytes 163872 | tf_op jit(solution)/shard_map/all_to_all | solution.py:337
  66.6 4.4 %shard_map.77 = f32[160,128]{1,0:T(8,128)S(1)} custom-call(s32[1]{0:T(128)} %bitcast.half_ref, f32[320,128]{1,0:T(8,128)S(1)} %bitcast.8, f32[16,128]{1,0:T(8,128)S(1)} %shard_map.76.stats_ref), custom_call_target="tpu_custom_call" | custom-call | tf_op jit(solution)/shard_map/pallas_call | solution.py:375
  71.0 8.1 %all_to_all.10 = f32[8,5,4,128]{3,2,1,0:T(4,128)S(1)} all-to-all(f32[8,5,4,128]{3,2,1,0:T(4,128)S(1)} %bitcast.9), channel_id=1, replica_groups=mesh['band'=64,'half'=2,'q'=8] {'q'}, dimensions={0} | all-to-all | bytes 163840 | tf_op jit(solution)/shard_map/all_to_all | solution.py:337
  79.0 0.2 shard_map.78
  79.2 5.9 %collective-permute-start.5 = (f32[80,128]{1,0:T(8,128)S(1)}, f32[80,128]{1,0:T(8,128)S(1)}, u32[]{:S(2)}, u32[]{:S(2)}) collective-permute-start(f32[80,128]{1,0:T(8,128)S(1)} %get-tuple-element.7.high_ref), channel_id=1, source_target_pairs={{0,16},{16,32},{32,48},{48,64},{64,80},{80,96},{96,112},{112,128},... | collective-permute-start | bytes 122888 | tf_op jit(solution)/shard_map/ppermute | solution.py:381
  85.1 1.9 %collective-permute-start.6 = (f32[80,128]{1,0:T(8,128)S(1)}, f32[80,128]{1,0:T(8,128)S(1)}, u32[]{:S(2)}, u32[]{:S(2)}) collective-permute-start(f32[80,128]{1,0:T(8,128)S(1)} %get-tuple-element.8.low_ref), channel_id=1, source_target_pairs={{16,0},{32,16},{48,32},{64,48},{80,64},{96,80},{112,96},{128,112},... | collective-permute-start | bytes 122888 | tf_op jit(solution)/shard_map/ppermute | solution.py:382
  87.0 0.0 collective-permute-done.5.below_ref
  87.0 6.1 %collective-permute-done.6.above_ref = f32[80,128]{1,0:T(8,128)S(1)} collective-permute-done((f32[80,128]{1,0:T(8,128)S(1)}, f32[80,128]{1,0:T(8,128)S(1)}, u32[]{:S(2)}, u32[]{:S(2)}) %collective-permute-start.6) | collective-permute-done | bytes 40992 | tf_op jit(solution)/shard_map/ppermute | solution.py:382
  93.1 0.9 %shard_map.79 = f32[160,128]{1,0:T(8,128)} custom-call(f32[80,128]{1,0:T(8,128)S(1)} %collective-permute-done.5.below_ref, f32[80,128]{1,0:T(8,128)S(1)} %get-tuple-element.8.low_ref, f32[80,128]{1,0:T(8,128)S(1)} %get-tuple-element.7.high_ref, f32[80,128]{1,0:T(8,128)S(1)} %collective-permute-done.6.above_ref), custom_call_target="tpu_custom_call" | custom-call | tf_op jit(solution)/shard_map/pallas_call | solution.py:383
Async XLA Ops:
  1.6 37.0 %collective-permute-start = (f32[168,128]{1,0:T(8,128)}, f32[168,128]{1,0:T(8,128)S(1)}, u32[]{:S(2)}, u32[]{:S(2)}) collective-permute-start(f32[168,128]{1,0:T(8,128)} %shard_map.73.centre_ref.own_ref), channel_id=1, source_target_pairs={{0,8},{8,0},{1,9},{9,1},{2,10},{10,2},{3,11},{11,3},{4,12},{12,4},... | collective-permute-start | bytes 258056 | tf_op jit(solution)/shard_map/ppermute | solution.py:363
  30.6 20.3 %collective-permute-start.4 = (f32[168,128]{1,0:T(8,128)}, f32[168,128]{1,0:T(8,128)S(1)}, u32[]{:S(2)}, u32[]{:S(2)}) collective-permute-start(f32[168,128]{1,0:T(8,128)} %shard_map.73.centre_ref.own_ref), channel_id=1, source_target_pairs={{16,0},{32,16},{48,32},{64,48},{80,64},{96,80},{112,96},{128,112},... | collective-permute-start | bytes 258056 | tf_op jit(solution)/shard_map/ppermute | solution.py:365
  33.2 17.6 %collective-permute-start.3 = (f32[168,128]{1,0:T(8,128)}, f32[168,128]{1,0:T(8,128)S(1)}, u32[]{:S(2)}, u32[]{:S(2)}) collective-permute-start(f32[168,128]{1,0:T(8,128)} %shard_map.73.centre_ref.own_ref), channel_id=1, source_target_pairs={{0,16},{16,32},{32,48},{48,64},{64,80},{80,96},{96,112},{112,128},... | collective-permute-start | bytes 258056 | tf_op jit(solution)/shard_map/ppermute | solution.py:364
  38.6 14.8 %collective-permute-start.2 = (f32[168,128]{1,0:T(8,128)S(1)}, f32[168,128]{1,0:T(8,128)S(1)}, u32[]{:S(2)}, u32[]{:S(2)}) collective-permute-start(f32[168,128]{1,0:T(8,128)S(1)} %collective-permute-done.centre_ref.other_ref), channel_id=1, source_target_pairs={{16,0},{32,16},{48,32},{64,48},{80,64},{96,80},{112,96},{128,112},... | collective-permute-start | bytes 258056 | tf_op jit(solution)/shard_map/ppermute | solution.py:370
  40.5 12.9 %collective-permute-start.1 = (f32[168,128]{1,0:T(8,128)S(1)}, f32[168,128]{1,0:T(8,128)S(1)}, u32[]{:S(2)}, u32[]{:S(2)}) collective-permute-start(f32[168,128]{1,0:T(8,128)S(1)} %collective-permute-done.centre_ref.other_ref), channel_id=1, source_target_pairs={{0,16},{16,32},{32,48},{48,64},{64,80},{80,96},{96,112},{112,128},... | collective-permute-start | bytes 258056 | tf_op jit(solution)/shard_map/ppermute | solution.py:369
  50.9 0.9 copy-start
  55.7 4.4 %copy-start.1 = (f32[168,128]{1,0:T(8,128)S(1)}, f32[168,128]{1,0:T(8,128)}, u32[]{:S(2)}) copy-start(f32[168,128]{1,0:T(8,128)} %shard_map.73.centre_ref.own_ref) | copy-start | bytes 258052
  55.7 10.9 %all-to-all-start = ((f32[8,10,4,128]{3,2,1,0:T(4,128)}), f32[8,10,4,128]{3,2,1,0:T(4,128)S(1)}, u32[]{:S(2)}, u32[]{:S(2)}) async-start(f32[8,10,4,128]{3,2,1,0:T(4,128)} %bitcast.3), calls=%async_computation | async-start | bytes 327680 | tf_op jit(solution)/shard_map/all_to_all | solution.py:337
  79.2 7.8 %collective-permute-start.5 = (f32[80,128]{1,0:T(8,128)S(1)}, f32[80,128]{1,0:T(8,128)S(1)}, u32[]{:S(2)}, u32[]{:S(2)}) collective-permute-start(f32[80,128]{1,0:T(8,128)S(1)} %get-tuple-element.7.high_ref), channel_id=1, source_target_pairs={{0,16},{16,32},{32,48},{48,64},{64,80},{80,96},{96,112},{112,128},... | collective-permute-start | bytes 122888 | tf_op jit(solution)/shard_map/ppermute | solution.py:381
  85.1 8.0 %collective-permute-start.6 = (f32[80,128]{1,0:T(8,128)S(1)}, f32[80,128]{1,0:T(8,128)S(1)}, u32[]{:S(2)}, u32[]{:S(2)}) collective-permute-start(f32[80,128]{1,0:T(8,128)S(1)} %get-tuple-element.8.low_ref), channel_id=1, source_target_pairs={{16,0},{32,16},{48,32},{64,48},{80,64},{96,80},{112,96},{128,112},... | collective-permute-start | bytes 122888 | tf_op jit(solution)/shard_map/ppermute | solution.py:382

commit v4 on v1

--- a/solution.py
+++ b/solution.py
@@ -1,3 +1,5 @@
+import functools
+
 import jax
 import jax.numpy as jnp
 from jax import lax
@@ -6,12 +8,12 @@
 from jax.sharding import Mesh, PartitionSpec as P
 
 NSI = 6
-STEPS = 2
 COURANT = 0.08
 HIGHEST = lax.Precision.HIGHEST
 MEMBERS = 128
 VMEM = pl.BlockSpec(memory_space=pltpu.VMEM)
 SMEM = pl.BlockSpec(memory_space=pltpu.SMEM)
+SMALL = pltpu.CompilerParams(vmem_limit_bytes=8 * 2**20)
 
 
 def half_minmod(lower, upper):
@@ -71,14 +73,23 @@
     return lax.broadcasted_iota(jnp.int32, shape, 1)
 
 
-def background_kernel(band_ref, centre_ref, low_ref, high_ref, out_ref):
-    def row(ref, r):
-        return [ref[pl.ds(v * 4 + r, 8, stride=20), :] for v in range(5)]
-
-    rows = [row(ref, r) for ref in (low_ref, centre_ref, high_ref) for r in range(4)]
+def ordered(band_ref, near, far):
+    even = jnp.full(near.shape, (band_ref[0] & 1) == 0)
+    return jnp.where(even, far, near), jnp.where(even, near, far)
+
+
+def background_kernel(bands, band_ref, centre_ref, near_ref, far_ref, out_ref):
+    low, centre, high = [], [], []
+    for r in range(4):
+        at = [slice((v * 4 + r) * 8, (v * 4 + r) * 8 + 8) for v in range(5)]
+        pairs = [ordered(band_ref, near_ref[x, :], far_ref[x, :]) for x in at]
+        low.append([below for below, _ in pairs])
+        centre.append([centre_ref[x, :] for x in at])
+        high.append([above for _, above in pairs])
+    rows = low + centre + high
     rows = transport(rows)
     keep_low = (band_ref[0] > 0).astype(jnp.float32)
-    keep_high = (band_ref[0] < band_ref[1] - 1).astype(jnp.float32)
+    keep_high = (band_ref[0] < bands - 1).astype(jnp.float32)
     for i in (0, 1):
         rows[i] = [x * keep_low for x in rows[i]]
     for i in (6, 7):
@@ -139,11 +150,21 @@
     out_ref[...] = out
 
 
-def dot(a, b):
-    return jnp.dot(a, b, precision=HIGHEST, preferred_element_type=jnp.float32)
-
-
-def analysis_kernel(half_ref, own_ref, other_ref, own_stats_ref, out_ref):
+def split(x):
+    head = x.astype(jnp.bfloat16)
+    return head, (x - head.astype(jnp.float32)).astype(jnp.bfloat16)
+
+
+def product(left, right, axis):
+    return lax.dot_general(
+        jnp.concatenate([left[0], left[1], left[0]], axis=1),
+        jnp.concatenate([right[0], right[0], right[1]], axis=axis),
+        (((1,), (axis,)), ((), ())),
+        preferred_element_type=jnp.float32,
+    )
+
+
+def analysis_kernel(half_ref, own_ref, other_ref, own_stats_ref, other_stats_ref, out_ref):
     lane8 = lanes_of((8, 128))
     sub8 = lax.broadcasted_iota(jnp.int32, (8, 128), 0)
     lane = lanes_of((MEMBERS, 128))
@@ -172,7 +193,7 @@
     slabs = [x - m for x, m in zip(slabs, means)]
     first = half_ref[0] == 0
     own = own_stats_ref[...]
-    other = other_ref[160:168, :]
+    other = other_stats_ref[...]
     stats = [jnp.where(first, own, other), jnp.where(first, other, own)]
     eye = (lax.broadcasted_iota(jnp.int32, (MEMBERS, 128), 0) == lane).astype(jnp.float32)
     tiles = [(b, t) for b in (0, 1) for t in (0, 1)]
@@ -185,12 +206,10 @@
         pull = gain * (s[1:2] - s[0:1] * means[b])
         pull_last = gain_last * (s[3:4] - s[2:3] * means[2])
         p, r = slabs[b], slabs[2]
-        gram = lax.dot_general(
-            jnp.concatenate([p * (gain * s[0:1]), r * (gain_last * s[2:3])], axis=1),
-            jnp.concatenate([p, r], axis=1),
-            (((1,), (1,)), ((), ())),
-            precision=HIGHEST,
-            preferred_element_type=jnp.float32,
+        gram = product(
+            split(jnp.concatenate([p * (gain * s[0:1]), r * (gain_last * s[2:3])], axis=1)),
+            split(jnp.concatenate([p, r], axis=1)),
+            1,
         )
         gram = gram + (MEMBERS - 1.0) * eye
         norm = jnp.sqrt(jnp.sum(jnp.sum(gram * gram, axis=0, keepdims=True), axis=1, keepdims=True))
@@ -207,15 +226,16 @@
             field = jnp.where(lane == 0, b_col, field)
         fields.append(field)
     for sweep in range(NSI):
-        factors = [1.5 * eye - 0.5 * x for x in tops]
+        factors = [split(1.5 * eye - 0.5 * x) for x in tops]
         if sweep < NSI - 1:
             both = [
-                dot(f, jnp.concatenate([x, y], axis=1)) for f, x, y in zip(factors, tops, fields)
+                product(f, split(jnp.concatenate([x, y], axis=1)), 0)
+                for f, x, y in zip(factors, tops, fields)
             ]
             fields = [x[:, 128:] for x in both]
-            tops = [dot(x[:, :128], f) for f, x in zip(factors, both)]
+            tops = [product(split(x[:, :128]), f, 0) for f, x in zip(factors, both)]
         else:
-            fields = [dot(f, y) for f, y in zip(factors, fields)]
+            fields = [product(f, split(y), 0) for f, y in zip(factors, fields)]
     moved = []
     for (b, t), field, norm in zip(tiles, fields, norms):
         column = field[:, 127:128] if t == 0 else field[:, 0:1]
@@ -239,7 +259,7 @@
         )
 
 
-def unpack_kernel(in_ref, low_ref, high_ref):
+def unpack_kernel(band_ref, in_ref, near_ref, far_ref):
     lane = lanes_of((8, 128))
     sub = lax.broadcasted_iota(jnp.int32, (8, 128), 0)
     group = lane >> 4
@@ -248,29 +268,39 @@
         four = in_ref[q * 20 + 16 : q * 20 + 20, :]
         eight = jnp.concatenate([four, four], axis=0)
         lasts.append(jnp.where(sub < 4, eight, pltpu.roll(eight, 64, 1)))
-    for r in range(4):
-        b, out_ref = r // 2, (low_ref if r < 2 else high_ref)
-        for v in range(5):
-            field = None
-            for j in range(4):
-                q = (r % 2) * 4 + j
-                if v < 4:
-                    slab = in_ref[q * 20 + 8 * b : q * 20 + 8 * b + 8, :]
-                    for u in (0, 1):
-                        piece = turned(slab, 2 * j + u - 4 * u - v)
-                        field = piece if field is None else jnp.where(group == 2 * j + u, piece, field)
-                else:
-                    piece = turned(lasts[q], 2 * j - 2 * b)
-                    field = piece if field is None else jnp.where((group >> 1) == j, piece, field)
-            at = (v * 2 + r % 2) * 8
-            out_ref[at : at + 8, :] = field
-
-
-def forecast_kernel(below_ref, low_ref, high_ref, above_ref, out_ref):
-    def row(ref, r):
-        return [ref[(v * 2 + r) * 8 : (v * 2 + r) * 8 + 8, :] for v in range(5)]
-
-    rows = [row(ref, r) for ref in (below_ref, low_ref, high_ref, above_ref) for r in (0, 1)]
+    def field(r, v):
+        b, result = r // 2, None
+        for j in range(4):
+            q = (r % 2) * 4 + j
+            if v < 4:
+                slab = in_ref[q * 20 + 8 * b : q * 20 + 8 * b + 8, :]
+                for u in (0, 1):
+                    piece = turned(slab, 2 * j + u - 4 * u - v)
+                    result = piece if result is None else jnp.where(group == 2 * j + u, piece, result)
+            else:
+                piece = turned(lasts[q], 2 * j - 2 * b)
+                result = piece if result is None else jnp.where((group >> 1) == j, piece, result)
+        return result
+
+    for v in range(5):
+        for r in (0, 1):
+            at = (v * 2 + r) * 8
+            far, near = ordered(band_ref, field(2 + r, v), field(r, v))
+            near_ref[at : at + 8, :] = near
+            far_ref[at : at + 8, :] = far
+
+
+def forecast_kernel(band_ref, near_ref, far_ref, from_near_ref, from_far_ref, out_ref):
+    below, low, high, above = [], [], [], []
+    for r in (0, 1):
+        at = [slice((v * 2 + r) * 8, (v * 2 + r) * 8 + 8) for v in range(5)]
+        own = [ordered(band_ref, near_ref[x, :], far_ref[x, :]) for x in at]
+        got = [ordered(band_ref, from_near_ref[x, :], from_far_ref[x, :]) for x in at]
+        low.append([x for x, _ in own])
+        high.append([x for _, x in own])
+        below.append([x for x, _ in got])
+        above.append([x for _, x in got])
+    rows = below + low + high + above
     rows = transport(rows)
     for r in range(4):
         for v in range(5):
@@ -281,57 +311,54 @@
     return jax.ShapeDtypeStruct(shape, jnp.float32)
 
 
+def call(kernel, in_specs, *out):
+    return pl.pallas_call(
+        kernel,
+        out_shape=out if len(out) > 1 else out[0],
+        in_specs=in_specs,
+        out_specs=(VMEM,) * len(out) if len(out) > 1 else VMEM,
+        compiler_params=SMALL,
+    )
+
+
+def swap(x, axis, first):
+    pairs = [(i, i + 1) for i in range(first, lax.axis_size(axis) - 1, 2)]
+    return lax.ppermute(x, axis, pairs + [(b, a) for a, b in pairs])
+
+
+def exchange(x):
+    return lax.all_to_all(
+        x.reshape(8, 5, 4, 128), "q", split_axis=0, concat_axis=0, tiled=True
+    ).reshape(160, 128)
+
+
 def shards(ensemble, obs_value, obs_site, obs_count, obs_precision, loc_weight, neighbours):
-    bands = lax.axis_size("band")
-    forward = [(i, i + 1) for i in range(bands - 1)]
-    backward = [(target, source) for source, target in forward]
-    here = jnp.stack([lax.axis_index("band"), jnp.int32(bands)])
-    fields = ensemble.reshape(160, 128)
-    low = lax.ppermute(fields, "band", forward)
-    high = lax.ppermute(fields, "band", backward)
-    stats = pl.pallas_call(
-        statistics_kernel,
-        out_shape=array(8, 128),
-        in_specs=[SMEM] * 3 + [VMEM] * 3,
-        out_specs=VMEM,
-        name="statistics",
-    )(obs_count, loc_weight, neighbours, obs_value, obs_site, obs_precision)
-    packed = pl.pallas_call(
-        background_kernel,
-        out_shape=array(160, 128),
-        in_specs=[SMEM] + [VMEM] * 3,
-        out_specs=VMEM,
-        name="background",
-    )(here, fields, low, high)
-    own = lax.all_to_all(packed.reshape(8, 5, 4, 128), "q", split_axis=0, concat_axis=0, tiled=True)
-    own = own.reshape(160, 128)
-    other = lax.ppermute(jnp.concatenate([own, stats], axis=0), "half", [(0, 1), (1, 0)])
-    analysed = pl.pallas_call(
-        analysis_kernel,
-        out_shape=array(160, 128),
-        in_specs=[SMEM] + [VMEM] * 3,
-        out_specs=VMEM,
-        name="analysis",
-    )(jnp.reshape(lax.axis_index("half"), (1,)), own, other, stats)
-    returned = lax.all_to_all(
-        analysed.reshape(8, 5, 4, 128), "q", split_axis=0, concat_axis=0, tiled=True
-    )
-    low, high = pl.pallas_call(
-        unpack_kernel,
-        out_shape=(array(80, 128), array(80, 128)),
-        in_specs=[VMEM],
-        out_specs=(VMEM, VMEM),
-        name="unpack",
-    )(returned.reshape(160, 128))
-    below = lax.ppermute(high, "band", forward)
-    above = lax.ppermute(low, "band", backward)
-    out = pl.pallas_call(
-        forecast_kernel,
-        out_shape=array(160, 128),
-        in_specs=[VMEM] * 4,
-        out_specs=VMEM,
-        name="forecast",
-    )(below, low, high, above)
+    band = jnp.reshape(lax.axis_index("band"), (1,))
+    half = jnp.reshape(lax.axis_index("half"), (1,))
+    fields = ensemble.transpose(1, 2, 0, 3).reshape(160, 128)
+    near = swap(fields, "band", 0)
+    far = swap(fields, "band", 1)
+    stats = call(statistics_kernel, [SMEM] * 3 + [VMEM] * 3, array(8, 128))(
+        obs_count, loc_weight, neighbours, obs_value, obs_site, obs_precision
+    )
+    packed = call(
+        functools.partial(background_kernel, lax.axis_size("band")),
+        [SMEM] + [VMEM] * 3, array(160, 128),
+    )(band, fields, near, far)
+    own = exchange(packed)
+    other = swap(own, "half", 0)
+    other_stats = swap(stats, "half", 0)
+    analysed = call(analysis_kernel, [SMEM] + [VMEM] * 4, array(160, 128))(
+        half, own, other, stats, other_stats
+    )
+    near, far = call(
+        unpack_kernel, [SMEM, VMEM], array(80, 128), array(80, 128)
+    )(band, exchange(analysed))
+    from_near = swap(near, "band", 0)
+    from_far = swap(far, "band", 1)
+    out = call(forecast_kernel, [SMEM] + [VMEM] * 4, array(160, 128))(
+        band, near, far, from_near, from_far
+    )
     return out.reshape(8, 5, 4, 128)
 
 

time: 99.8 us -> 99.2 us (level)
  waiting for transfers between devices: 14.6 us -> 30.6 us
  starting transfers between devices: 57.6 us -> 43.3 us
  blocking collectives: 9.66 us -> 18 us
  Pallas kernels: 14.1 us -> 5.89 us
  other arithmetic: 1.33 us -> 0 us
    ppermute x5 -> x6, waiting for transfers between devices: 10.9 us -> 30.6 us  [swap(): return lax.ppermute(x, axis, pairs + [(b, a) for a, b in pairs])]
    ppermute x5 -> x6, starting transfers between devices: 53.3 us -> 43.3 us  [swap(): return lax.ppermute(x, axis, pairs + [(b, a) for a, b in pairs])]
    all_to_all x1 -> x2, blocking collectives: 9.66 us -> 18 us  [exchange(): lax.all_to_all(x.reshape(8, 5, 4, 128), 'q', split_axis=0, concat_axis=0,...]
    pallas_call x5, Pallas kernels: 14.1 us -> 5.89 us  [the longest x1 2.63 us: shards(): call(analysis_kernel, [SMEM] + [VMEM] * 4, array(160, 128))]
    all_to_all x1 -> x0, starting transfers between devices: 4.3 us -> none  [shards(): lax.all_to_all(packed.reshape(8, 5, 4, 128), 'q', split_axis=0, concat_ax...]
    all_to_all x1 -> x0, waiting for transfers between devices: 3.73 us -> none  [shards(): lax.all_to_all(packed.reshape(8, 5, 4, 128), 'q', split_axis=0, concat_ax...]
    unnamed x12, local copies, waits for them, and re-layouts: 1.88 us -> 0.03 us
  transfers between devices with their start and end apart: 6 -> 6, of which waited for: 4 -> 4; matrix products, arithmetic and copies ran while one was open for 1% -> 0% of each run, Pallas kernels for 2% -> 1%
where the time goes in v4:
time: 99.2 us; the launch traced here: 98.9 us
  starting transfers between devices  43.3 us (44%)
  waiting for transfers between devices  30.6 us (31%)
  blocking collectives  18 us (18%)
  Pallas kernels  5.89 us (6%)
    ppermute x6, starting transfers between devices, swap(): return lax.ppermute(x, axis, pairs + [(b, a) for a, b in pairs])  43.3 us
    ppermute x6, waiting for transfers between devices, swap(): return lax.ppermute(x, axis, pairs + [(b, a) for a, b in pairs])  30.6 us
    all_to_all x2, blocking collectives, exchange(): lax.all_to_all(x.reshape(8, 5, 4, 128), 'q', split_axis=0, concat_axis=0,...  18 us
    pallas_call x1, Pallas kernels, shards(): call(analysis_kernel, [SMEM] + [VMEM] * 4, array(160, 128))  2.63 us
  transfers between devices with their start and end apart: 6, of which 4 were waited for; matrix products, arithmetic and copies ran while one was open for 0% of the time, Pallas kernels for 1%

profile of v4, /device:TPU:24, one launch (start us, length us, event | category | flops | bytes accessed | tf_op | source)
XLA Modules:
  0.0 98.9 jit_solution(1207988569706685719)
XLA Ops:
  0.0 0.9 copy.8
  0.9 2.6 %collective-permute-start = (f32[160,128]{1,0:T(8,128)S(1)}, f32[160,128]{1,0:T(8,128)S(1)}, u32[]{:S(2)}, u32[]{:S(2)}) collective-permute-start(f32[160,128]{1,0:T(8,128)S(1)} %bitcast.9), channel_id=1, source_target_pairs={{0,16},{32,48},{64,80},{96,112},{128,144},{160,176},{192,208},{224... | collective-permute-start | bytes 245768 | tf_op jit(solution)/shard_map/ppermute | solution.py:326
  3.5 4.3 %collective-permute-start.1 = (f32[160,128]{1,0:T(8,128)S(1)}, f32[160,128]{1,0:T(8,128)S(1)}, u32[]{:S(2)}, u32[]{:S(2)}) collective-permute-start(f32[160,128]{1,0:T(8,128)S(1)} %bitcast.10), channel_id=1, source_target_pairs={{16,32},{48,64},{80,96},{112,128},{144,160},{176,192},{208,224},{2... | collective-permute-start | bytes 245768 | tf_op jit(solution)/shard_map/ppermute | solution.py:326
  7.9 0.0 collective-permute-done.near_ref
  7.9 4.1 %collective-permute-done.1.far_ref = f32[160,128]{1,0:T(8,128)S(1)} collective-permute-done((f32[160,128]{1,0:T(8,128)S(1)}, f32[160,128]{1,0:T(8,128)S(1)}, u32[]{:S(2)}, u32[]{:S(2)}) %collective-permute-start.1) | collective-permute-done | bytes 81952 | tf_op jit(solution)/shard_map/ppermute | solution.py:326
  12.0 1.0 %shard_map.73 = f32[160,128]{1,0:T(8,128)S(1)} custom-call(s32[1]{0:T(128)} %bitcast.band_ref, f32[160,128]{1,0:T(8,128)S(1)} %bitcast.11, f32[160,128]{1,0:T(8,128)S(1)} %collective-permute-done.near_ref, f32[160,128]{1,0:T(8,128)S(1)} %collective-permute-done.1.far_ref), custom_call_target="tpu_custom_call" | custom-call | tf_op jit(solution)/shard_map/pallas_call | solution.py:344
  13.0 0.0 copy-start.1
  13.0 0.0 copy-start.2
  13.0 0.0 copy-start.3
  13.0 0.0 copy-start.4
  13.0 9.9 %all_to_all.10 = f32[8,5,4,128]{3,2,1,0:T(4,128)S(1)} all-to-all(f32[8,5,4,128]{3,2,1,0:T(4,128)S(1)} %bitcast.12), channel_id=1, replica_groups=mesh['band'=64,'half'=2,'q'=8] {'q'}, dimensions={0} | all-to-all | bytes 163840 | tf_op jit(solution)/shard_map/all_to_all | solution.py:330
  23.0 0.0 copy-start
  23.0 0.0 copy-start.5
  23.0 29.1 %collective-permute-start.2 = (f32[160,128]{1,0:T(8,128)S(1)}, f32[160,128]{1,0:T(8,128)S(1)}, u32[]{:S(2)}, u32[]{:S(2)}) collective-permute-start(f32[160,128]{1,0:T(8,128)S(1)} %bitcast.13), channel_id=1, source_target_pairs={{0,8},{8,0},{1,9},{9,1},{2,10},{10,2},{3,11},{11,3},{4,12},{12,4},... | collective-permute-start | bytes 245768 | tf_op jit(solution)/shard_map/ppermute | solution.py:326
  52.1 0.0 copy-done.1
  52.1 0.0 copy-done.2
  52.1 0.0 copy-done.3
  52.1 0.0 copy-done.4
  52.1 0.0 copy-done
  52.1 0.0 copy-done.5
  52.2 1.1 %shard_map.74.own_stats_ref = f32[8,128]{1,0:T(8,128)S(1)} custom-call(s32[2]{0:T(128)S(1)} %copy-done.5, f32[2,3]{1,0:T(2,128)S(1)} %copy-done, s32[2,3]{1,0:T(2,128)S(1)} %copy-done.1, f32[2,128]{1,0:T(2,128)S(1)} %copy-done.2, s32[2,128]{1,0:T(2,128)S(1)} %copy-done.3, f32[2,128]{1,0:T(2,128)S(1)} %copy-done.4), custom_call_target="tpu_custom_call" | custom-call | tf_op jit(solution)/shard_map/pallas_call | solution.py:341
  53.2 1.9 %collective-permute-start.3 = (f32[8,128]{1,0:T(8,128)S(1)}, f32[8,128]{1,0:T(8,128)S(1)}, u32[]{:S(2)}, u32[]{:S(2)}) collective-permute-start(f32[8,128]{1,0:T(8,128)S(1)} %shard_map.74.own_stats_ref), channel_id=1, source_target_pairs={{0,8},{8,0},{1,9},{9,1},{2,10},{10,2},{3,11},{11,3},{4,12},{12,4},... | collective-permute-start | bytes 12296 | tf_op jit(solution)/shard_map/ppermute | solution.py:326
  55.2 21.9 %collective-permute-done.3.other_stats_ref = f32[8,128]{1,0:T(8,128)S(1)} collective-permute-done((f32[8,128]{1,0:T(8,128)S(1)}, f32[8,128]{1,0:T(8,128)S(1)}, u32[]{:S(2)}, u32[]{:S(2)}) %collective-permute-start.3) | collective-permute-done | bytes 4128 | tf_op jit(solution)/shard_map/ppermute | solution.py:326
  77.1 0.0 collective-permute-done.2.other_ref
  77.1 2.6 %shard_map.75 = f32[160,128]{1,0:T(8,128)S(1)} custom-call(s32[1]{0:T(128)} %bitcast.1.half_ref, f32[160,128]{1,0:T(8,128)S(1)} %bitcast.14, f32[160,128]{1,0:T(8,128)S(1)} %collective-permute-done.2.other_ref, f32[8,128]{1,0:T(8,128)S(1)} %shard_map.74.own_stats_ref, f32[8,128]{1,0:T(8,128)S(1)} %collective-permute-done.3.other_stats_ref), custom_call_target="tpu_custom_call" | custom-call | tf_op jit(solution)/shard_map/pallas_call | solution.py:351
  79.7 8.1 %all_to_all.11 = f32[8,5,4,128]{3,2,1,0:T(4,128)S(1)} all-to-all(f32[8,5,4,128]{3,2,1,0:T(4,128)S(1)} %bitcast.15), channel_id=1, replica_groups=mesh['band'=64,'half'=2,'q'=8] {'q'}, dimensions={0} | all-to-all | bytes 163840 | tf_op jit(solution)/shard_map/all_to_all | solution.py:330
  87.8 0.2 shard_map.76
  88.0 1.9 %collective-permute-start.4 = (f32[80,128]{1,0:T(8,128)S(1)}, f32[80,128]{1,0:T(8,128)S(1)}, u32[]{:S(2)}, u32[]{:S(2)}) collective-permute-start(f32[80,128]{1,0:T(8,128)S(1)} %get-tuple-element.7.near_ref), channel_id=1, source_target_pairs={{0,16},{32,48},{64,80},{96,112},{128,144},{160,176},{192,208},{224... | collective-permute-start | bytes 122888 | tf_op jit(solution)/shard_map/ppermute | solution.py:326
  89.9 3.4 %collective-permute-start.5 = (f32[80,128]{1,0:T(8,128)S(1)}, f32[80,128]{1,0:T(8,128)S(1)}, u32[]{:S(2)}, u32[]{:S(2)}) collective-permute-start(f32[80,128]{1,0:T(8,128)S(1)} %get-tuple-element.8.far_ref), channel_id=1, source_target_pairs={{16,32},{48,64},{80,96},{112,128},{144,160},{176,192},{208,224},{2... | collective-permute-start | bytes 122888 | tf_op jit(solution)/shard_map/ppermute | solution.py:326
  93.4 0.5 collective-permute-done.4.from_near_ref
  93.9 4.0 %collective-permute-done.5.from_far_ref = f32[80,128]{1,0:T(8,128)S(1)} collective-permute-done((f32[80,128]{1,0:T(8,128)S(1)}, f32[80,128]{1,0:T(8,128)S(1)}, u32[]{:S(2)}, u32[]{:S(2)}) %collective-permute-start.5) | collective-permute-done | bytes 40992 | tf_op jit(solution)/shard_map/ppermute | solution.py:326
  97.9 0.9 shard_map.77
Async XLA Ops:
  0.9 7.0 %collective-permute-start = (f32[160,128]{1,0:T(8,128)S(1)}, f32[160,128]{1,0:T(8,128)S(1)}, u32[]{:S(2)}, u32[]{:S(2)}) collective-permute-start(f32[160,128]{1,0:T(8,128)S(1)} %bitcast.9), channel_id=1, source_target_pairs={{0,16},{32,48},{64,80},{96,112},{128,144},{160,176},{192,208},{224... | collective-permute-start | bytes 245768 | tf_op jit(solution)/shard_map/ppermute | solution.py:326
  3.5 8.4 %collective-permute-start.1 = (f32[160,128]{1,0:T(8,128)S(1)}, f32[160,128]{1,0:T(8,128)S(1)}, u32[]{:S(2)}, u32[]{:S(2)}) collective-permute-start(f32[160,128]{1,0:T(8,128)S(1)} %bitcast.10), channel_id=1, source_target_pairs={{16,32},{48,64},{80,96},{112,128},{144,160},{176,192},{208,224},{2... | collective-permute-start | bytes 245768 | tf_op jit(solution)/shard_map/ppermute | solution.py:326
  13.0 39.1 %copy-start.1 = (s32[2,3]{1,0:T(2,128)S(1)}, s32[2,3]{1,0:T(2,128)}, u32[]{:S(2)}) copy-start(s32[2,3]{1,0:T(2,128)} %near_ref.1) | copy-start | bytes 76
  13.0 39.1 %copy-start.2 = (f32[2,128]{1,0:T(2,128)S(1)}, f32[2,128]{1,0:T(2,128)}, u32[]{:S(2)}) copy-start(f32[2,128]{1,0:T(2,128)} %value_ref.1) | copy-start | bytes 3076
  13.0 39.1 %copy-start.3 = (s32[2,128]{1,0:T(2,128)S(1)}, s32[2,128]{1,0:T(2,128)}, u32[]{:S(2)}) copy-start(s32[2,128]{1,0:T(2,128)} %site_ref.1) | copy-start | bytes 3076
  13.0 39.1 %copy-start.4 = (f32[2,128]{1,0:T(2,128)S(1)}, f32[2,128]{1,0:T(2,128)}, u32[]{:S(2)}) copy-start(f32[2,128]{1,0:T(2,128)} %precision_ref.1) | copy-start | bytes 3076
  23.0 29.1 %copy-start = (f32[2,3]{1,0:T(2,128)S(1)}, f32[2,3]{1,0:T(2,128)}, u32[]{:S(2)}) copy-start(f32[2,3]{1,0:T(2,128)} %loc_ref.1) | copy-start | bytes 76
  23.0 29.2 %copy-start.5 = (s32[2]{0:T(128)S(1)}, s32[2]{0:T(128)}, u32[]{:S(2)}) copy-start(s32[2]{0:T(128)} %count_ref.1) | copy-start | bytes 28
  23.0 54.1 %collective-permute-start.2 = (f32[160,128]{1,0:T(8,128)S(1)}, f32[160,128]{1,0:T(8,128)S(1)}, u32[]{:S(2)}, u32[]{:S(2)}) collective-permute-start(f32[160,128]{1,0:T(8,128)S(1)} %bitcast.13), channel_id=1, source_target_pairs={{0,8},{8,0},{1,9},{9,1},{2,10},{10,2},{3,11},{11,3},{4,12},{12,4},... | collective-permute-start | bytes 245768 | tf_op jit(solution)/shard_map/ppermute | solution.py:326
  53.2 23.8 %collective-permute-start.3 = (f32[8,128]{1,0:T(8,128)S(1)}, f32[8,128]{1,0:T(8,128)S(1)}, u32[]{:S(2)}, u32[]{:S(2)}) collective-permute-start(f32[8,128]{1,0:T(8,128)S(1)} %shard_map.74.own_stats_ref), channel_id=1, source_target_pairs={{0,8},{8,0},{1,9},{9,1},{2,10},{10,2},{3,11},{11,3},{4,12},{12,4},... | collective-permute-start | bytes 12296 | tf_op jit(solution)/shard_map/ppermute | solution.py:326
  88.0 5.9 %collective-permute-start.4 = (f32[80,128]{1,0:T(8,128)S(1)}, f32[80,128]{1,0:T(8,128)S(1)}, u32[]{:S(2)}, u32[]{:S(2)}) collective-permute-start(f32[80,128]{1,0:T(8,128)S(1)} %get-tuple-element.7.near_ref), channel_id=1, source_target_pairs={{0,16},{32,48},{64,80},{96,112},{128,144},{160,176},{192,208},{224... | collective-permute-start | bytes 122888 | tf_op jit(solution)/shard_map/ppermute | solution.py:326
  89.9 8.0 %collective-permute-start.5 = (f32[80,128]{1,0:T(8,128)S(1)}, f32[80,128]{1,0:T(8,128)S(1)}, u32[]{:S(2)}, u32[]{:S(2)}) collective-permute-start(f32[80,128]{1,0:T(8,128)S(1)} %get-tuple-element.8.far_ref), channel_id=1, source_target_pairs={{16,32},{48,64},{80,96},{112,128},{144,160},{176,192},{208,224},{2... | collective-permute-start | bytes 122888 | tf_op jit(solution)/shard_map/ppermute | solution.py:326

commit v5 on v4

--- a/solution.py
+++ b/solution.py
@@ -164,7 +164,7 @@
     )
 
 
-def analysis_kernel(half_ref, own_ref, other_ref, own_stats_ref, other_stats_ref, out_ref):
+def analysis_kernel(half_ref, own_ref, other_ref, own_stats_ref, out_ref):
     lane8 = lanes_of((8, 128))
     sub8 = lax.broadcasted_iota(jnp.int32, (8, 128), 0)
     lane = lanes_of((MEMBERS, 128))
@@ -193,7 +193,7 @@
     slabs = [x - m for x, m in zip(slabs, means)]
     first = half_ref[0] == 0
     own = own_stats_ref[...]
-    other = other_stats_ref[...]
+    other = other_ref[160:168, :]
     stats = [jnp.where(first, own, other), jnp.where(first, other, own)]
     eye = (lax.broadcasted_iota(jnp.int32, (MEMBERS, 128), 0) == lane).astype(jnp.float32)
     tiles = [(b, t) for b in (0, 1) for t in (0, 1)]
@@ -346,11 +346,8 @@
         [SMEM] + [VMEM] * 3, array(160, 128),
     )(band, fields, near, far)
     own = exchange(packed)
-    other = swap(own, "half", 0)
-    other_stats = swap(stats, "half", 0)
-    analysed = call(analysis_kernel, [SMEM] + [VMEM] * 4, array(160, 128))(
-        half, own, other, stats, other_stats
-    )
+    other = swap(jnp.concatenate([own, stats], axis=0), "half", 0)
+    analysed = call(analysis_kernel, [SMEM] + [VMEM] * 3, array(160, 128))(half, own, other, stats)
     near, far = call(
         unpack_kernel, [SMEM, VMEM], array(80, 128), array(80, 128)
     )(band, exchange(analysed))

time: 99.2 us -> 89 us (0.90)
  the two profiles are of different devices: /device:TPU:24 before, /device:TPU:56 now
where the time goes in v5:
time: 89 us; the launch traced here: 88.6 us
  starting transfers between devices  43.3 us (49%)
  waiting for transfers between devices  29.7 us (33%)
  blocking collectives  8.08 us (9%)
  Pallas kernels  6.54 us (7%)
  local copies, waits for them, and re-layouts  0.92 us (1%)
    ppermute x5, starting transfers between devices, swap(): return lax.ppermute(x, axis, pairs + [(b, a) for a, b in pairs])  38.9 us
    ppermute x5, waiting for transfers between devices, swap(): return lax.ppermute(x, axis, pairs + [(b, a) for a, b in pairs])  25.1 us
    all_to_all x1, blocking collectives, exchange(): lax.all_to_all(x.reshape(8, 5, 4, 128), 'q', split_axis=0, concat_axis=0,...  8.08 us
    all_to_all x1, waiting for transfers between devices, exchange(): lax.all_to_all(x.reshape(8, 5, 4, 128), 'q', split_axis=0, concat_axis=0,...  4.56 us
    all_to_all x1, starting transfers between devices, exchange(): lax.all_to_all(x.reshape(8, 5, 4, 128), 'q', split_axis=0, concat_axis=0,...  4.44 us
    pallas_call x1, Pallas kernels, shards(): call(analysis_kernel, [SMEM] + [VMEM] * 3, array(160, 128))  2.63 us
  transfers between devices with their start and end apart: 6, of which 5 were waited for; matrix products, arithmetic and copies ran while one was open for 0% of the time, Pallas kernels for 1%

profile of v5, /device:TPU:56, one launch (start us, length us, event | category | flops | bytes accessed | tf_op | source)
XLA Modules:
  0.0 88.6 jit_solution(4382604991142788308)
XLA Ops:
  0.0 0.9 %copy.8 = f32[5,4,8,128]{3,2,1,0:T(8,128)S(1)} copy(f32[5,4,8,128]{3,1,0,2:T(4,128)} %bitcast.16) | data formatting | bytes 163840 | tf_op jit(solution)/shard_map/transpose | solution.py:338
  0.9 2.6 %collective-permute-start = (f32[160,128]{1,0:T(8,128)S(1)}, f32[160,128]{1,0:T(8,128)S(1)}, u32[]{:S(2)}, u32[]{:S(2)}) collective-permute-start(f32[160,128]{1,0:T(8,128)S(1)} %bitcast.11), channel_id=1, source_target_pairs={{0,16},{32,48},{64,80},{96,112},{128,144},{160,176},{192,208},{224... | collective-permute-start | bytes 245768 | tf_op jit(solution)/shard_map/ppermute | solution.py:326
  3.5 4.3 %collective-permute-start.1 = (f32[160,128]{1,0:T(8,128)S(1)}, f32[160,128]{1,0:T(8,128)S(1)}, u32[]{:S(2)}, u32[]{:S(2)}) collective-permute-start(f32[160,128]{1,0:T(8,128)S(1)} %bitcast.12), channel_id=1, source_target_pairs={{16,32},{48,64},{80,96},{112,128},{144,160},{176,192},{208,224},{2... | collective-permute-start | bytes 245768 | tf_op jit(solution)/shard_map/ppermute | solution.py:326
  7.9 0.0 collective-permute-done.near_ref
  7.9 4.1 %collective-permute-done.1.far_ref = f32[160,128]{1,0:T(8,128)S(1)} collective-permute-done((f32[160,128]{1,0:T(8,128)S(1)}, f32[160,128]{1,0:T(8,128)S(1)}, u32[]{:S(2)}, u32[]{:S(2)}) %collective-permute-start.1) | collective-permute-done | bytes 81952 | tf_op jit(solution)/shard_map/ppermute | solution.py:326
  12.0 1.7 %shard_map.73 = f32[160,128]{1,0:T(8,128)} custom-call(s32[1]{0:T(128)} %bitcast.band_ref, f32[160,128]{1,0:T(8,128)S(1)} %bitcast.13, f32[160,128]{1,0:T(8,128)S(1)} %collective-permute-done.near_ref, f32[160,128]{1,0:T(8,128)S(1)} %collective-permute-done.1.far_ref), custom_call_target="tpu_custom_call" | custom-call | tf_op jit(solution)/shard_map/pallas_call | solution.py:344
  13.6 0.0 copy-start
  13.6 0.0 copy-start.1
  13.7 0.0 copy-start.2
  13.7 0.0 copy-start.3
  13.7 0.0 copy-start.4
  13.7 0.0 copy-start.5
  13.7 4.4 %all-to-all-start = ((f32[8,5,4,128]{3,2,1,0:T(4,128)}), f32[8,5,4,128]{3,2,1,0:T(4,128)S(1)}, u32[]{:S(2)}, u32[]{:S(2)}) async-start(f32[8,5,4,128]{3,2,1,0:T(4,128)} %bitcast.4), calls=%async_computation | async-start | bytes 163840 | tf_op jit(solution)/shard_map/all_to_all | solution.py:330
  18.1 0.0 copy-done
  18.1 0.0 copy-done.1
  18.1 0.0 copy-done.2
  18.2 0.0 copy-done.3
  18.2 0.0 copy-done.4
  18.2 0.0 copy-done.5
  18.2 1.1 %shard_map.74.own_stats_ref = f32[8,128]{1,0:T(8,128)S(1)} custom-call(s32[2]{0:T(128)S(1)} %copy-done.5, f32[2,3]{1,0:T(2,128)S(1)} %copy-done, s32[2,3]{1,0:T(2,128)S(1)} %copy-done.1, f32[2,128]{1,0:T(2,128)S(1)} %copy-done.2, s32[2,128]{1,0:T(2,128)S(1)} %copy-done.3, f32[2,128]{1,0:T(2,128)S(1)} %copy-done.4), custom_call_target="tpu_custom_call" | custom-call | tf_op jit(solution)/shard_map/pallas_call | solution.py:341
  19.3 4.6 %all-to-all-done = f32[8,5,4,128]{3,2,1,0:T(4,128)S(1)} async-done(((f32[8,5,4,128]{3,2,1,0:T(4,128)}), f32[8,5,4,128]{3,2,1,0:T(4,128)S(1)}, u32[]{:S(2)}, u32[]{:S(2)}) %all-to-all-start) | async-done | bytes 81952 | tf_op jit(solution)/shard_map/all_to_all | solution.py:330
  23.8 28.1 %collective-permute-start.2 = (f32[168,128]{1,0:T(8,128)S(1)}, f32[168,128]{1,0:T(8,128)S(1)}, u32[]{:S(2)}, u32[]{:S(2)}) collective-permute-start(f32[168,128]{1,0:T(8,128)S(1)} %pad_maximum_fusion), channel_id=1, source_target_pairs={{0,8},{8,0},{1,9},{9,1},{2,10},{10,2},{3,11},{11,3},{4,12},{12,4},... | collective-permute-start | bytes 258056 | tf_op jit(solution)/shard_map/ppermute | solution.py:326
  51.9 14.9 %collective-permute-done.2.other_ref = f32[168,128]{1,0:T(8,128)S(1)} collective-permute-done((f32[168,128]{1,0:T(8,128)S(1)}, f32[168,128]{1,0:T(8,128)S(1)}, u32[]{:S(2)}, u32[]{:S(2)}) %collective-permute-start.2) | collective-permute-done | bytes 86048 | tf_op jit(solution)/shard_map/ppermute | solution.py:326
  66.8 2.6 %shard_map.75 = f32[160,128]{1,0:T(8,128)S(1)} custom-call(s32[1]{0:T(128)} %bitcast.1.half_ref, f32[160,128]{1,0:T(8,128)S(1)} %bitcast.10, f32[168,128]{1,0:T(8,128)S(1)} %collective-permute-done.2.other_ref, f32[8,128]{1,0:T(8,128)S(1)} %shard_map.74.own_stats_ref), custom_call_target="tpu_custom_call" | custom-call | tf_op jit(solution)/shard_map/pallas_call | solution.py:350
  69.5 8.1 %all_to_all.10 = f32[8,5,4,128]{3,2,1,0:T(4,128)S(1)} all-to-all(f32[8,5,4,128]{3,2,1,0:T(4,128)S(1)} %bitcast.14), channel_id=1, replica_groups=mesh['band'=64,'half'=2,'q'=8] {'q'}, dimensions={0} | all-to-all | bytes 163840 | tf_op jit(solution)/shard_map/all_to_all | solution.py:330
  77.6 0.2 shard_map.76
  77.8 1.9 %collective-permute-start.3 = (f32[80,128]{1,0:T(8,128)S(1)}, f32[80,128]{1,0:T(8,128)S(1)}, u32[]{:S(2)}, u32[]{:S(2)}) collective-permute-start(f32[80,128]{1,0:T(8,128)S(1)} %get-tuple-element.7.near_ref), channel_id=1, source_target_pairs={{0,16},{32,48},{64,80},{96,112},{128,144},{160,176},{192,208},{224... | collective-permute-start | bytes 122888 | tf_op jit(solution)/shard_map/ppermute | solution.py:326
  79.7 1.9 %collective-permute-start.4 = (f32[80,128]{1,0:T(8,128)S(1)}, f32[80,128]{1,0:T(8,128)S(1)}, u32[]{:S(2)}, u32[]{:S(2)}) collective-permute-start(f32[80,128]{1,0:T(8,128)S(1)} %get-tuple-element.8.far_ref), channel_id=1, source_target_pairs={{16,32},{48,64},{80,96},{112,128},{144,160},{176,192},{208,224},{2... | collective-permute-start | bytes 122888 | tf_op jit(solution)/shard_map/ppermute | solution.py:326
  81.6 2.0 %collective-permute-done.3.from_near_ref = f32[80,128]{1,0:T(8,128)S(1)} collective-permute-done((f32[80,128]{1,0:T(8,128)S(1)}, f32[80,128]{1,0:T(8,128)S(1)}, u32[]{:S(2)}, u32[]{:S(2)}) %collective-permute-start.3) | collective-permute-done | bytes 40992 | tf_op jit(solution)/shard_map/ppermute | solution.py:326
  83.7 4.0 %collective-permute-done.4.from_far_ref = f32[80,128]{1,0:T(8,128)S(1)} collective-permute-done((f32[80,128]{1,0:T(8,128)S(1)}, f32[80,128]{1,0:T(8,128)S(1)}, u32[]{:S(2)}, u32[]{:S(2)}) %collective-permute-start.4) | collective-permute-done | bytes 40992 | tf_op jit(solution)/shard_map/ppermute | solution.py:326
  87.7 0.9 %shard_map.77 = f32[160,128]{1,0:T(8,128)} custom-call(s32[1]{0:T(128)} %bitcast.band_ref, f32[80,128]{1,0:T(8,128)S(1)} %get-tuple-element.7.near_ref, f32[80,128]{1,0:T(8,128)S(1)} %get-tuple-element.8.far_ref, f32[80,128]{1,0:T(8,128)S(1)} %collective-permute-done.3.from_near_ref, f32[80,128]{1,0:T(8,128)S(1)} %collective-permute-done.4.from_far_ref), custom_call_target="tpu_custom_call" | custom-call | tf_op jit(solution)/shard_map/pallas_call | solution.py:356
  (1 shorter events, 0.0 us)
Async XLA Ops:
  0.9 7.0 %collective-permute-start = (f32[160,128]{1,0:T(8,128)S(1)}, f32[160,128]{1,0:T(8,128)S(1)}, u32[]{:S(2)}, u32[]{:S(2)}) collective-permute-start(f32[160,128]{1,0:T(8,128)S(1)} %bitcast.11), channel_id=1, source_target_pairs={{0,16},{32,48},{64,80},{96,112},{128,144},{160,176},{192,208},{224... | collective-permute-start | bytes 245768 | tf_op jit(solution)/shard_map/ppermute | solution.py:326
  3.5 8.4 %collective-permute-start.1 = (f32[160,128]{1,0:T(8,128)S(1)}, f32[160,128]{1,0:T(8,128)S(1)}, u32[]{:S(2)}, u32[]{:S(2)}) collective-permute-start(f32[160,128]{1,0:T(8,128)S(1)} %bitcast.12), channel_id=1, source_target_pairs={{16,32},{48,64},{80,96},{112,128},{144,160},{176,192},{208,224},{2... | collective-permute-start | bytes 245768 | tf_op jit(solution)/shard_map/ppermute | solution.py:326
  13.6 4.5 %copy-start = (f32[2,3]{1,0:T(2,128)S(1)}, f32[2,3]{1,0:T(2,128)}, u32[]{:S(2)}) copy-start(f32[2,3]{1,0:T(2,128)} %loc_ref.1) | copy-start | bytes 76
  13.6 4.5 %copy-start.1 = (s32[2,3]{1,0:T(2,128)S(1)}, s32[2,3]{1,0:T(2,128)}, u32[]{:S(2)}) copy-start(s32[2,3]{1,0:T(2,128)} %near_ref.1) | copy-start | bytes 76
  13.7 4.5 %copy-start.2 = (f32[2,128]{1,0:T(2,128)S(1)}, f32[2,128]{1,0:T(2,128)}, u32[]{:S(2)}) copy-start(f32[2,128]{1,0:T(2,128)} %value_ref.1) | copy-start | bytes 3076
  13.7 4.5 %copy-start.3 = (s32[2,128]{1,0:T(2,128)S(1)}, s32[2,128]{1,0:T(2,128)}, u32[]{:S(2)}) copy-start(s32[2,128]{1,0:T(2,128)} %site_ref.1) | copy-start | bytes 3076
  13.7 4.5 %copy-start.4 = (f32[2,128]{1,0:T(2,128)S(1)}, f32[2,128]{1,0:T(2,128)}, u32[]{:S(2)}) copy-start(f32[2,128]{1,0:T(2,128)} %precision_ref.1) | copy-start | bytes 3076
  13.7 4.5 %copy-start.5 = (s32[2]{0:T(128)S(1)}, s32[2]{0:T(128)}, u32[]{:S(2)}) copy-start(s32[2]{0:T(128)} %count_ref.1) | copy-start | bytes 28
  13.7 10.2 %all-to-all-start = ((f32[8,5,4,128]{3,2,1,0:T(4,128)}), f32[8,5,4,128]{3,2,1,0:T(4,128)S(1)}, u32[]{:S(2)}, u32[]{:S(2)}) async-start(f32[8,5,4,128]{3,2,1,0:T(4,128)} %bitcast.4), calls=%async_computation | async-start | bytes 163840 | tf_op jit(solution)/shard_map/all_to_all | solution.py:330
  23.8 43.0 %collective-permute-start.2 = (f32[168,128]{1,0:T(8,128)S(1)}, f32[168,128]{1,0:T(8,128)S(1)}, u32[]{:S(2)}, u32[]{:S(2)}) collective-permute-start(f32[168,128]{1,0:T(8,128)S(1)} %pad_maximum_fusion), channel_id=1, source_target_pairs={{0,8},{8,0},{1,9},{9,1},{2,10},{10,2},{3,11},{11,3},{4,12},{12,4},... | collective-permute-start | bytes 258056 | tf_op jit(solution)/shard_map/ppermute | solution.py:326
  77.8 5.9 %collective-permute-start.3 = (f32[80,128]{1,0:T(8,128)S(1)}, f32[80,128]{1,0:T(8,128)S(1)}, u32[]{:S(2)}, u32[]{:S(2)}) collective-permute-start(f32[80,128]{1,0:T(8,128)S(1)} %get-tuple-element.7.near_ref), channel_id=1, source_target_pairs={{0,16},{32,48},{64,80},{96,112},{128,144},{160,176},{192,208},{224... | collective-permute-start | bytes 122888 | tf_op jit(solution)/shard_map/ppermute | solution.py:326
  79.7 8.0 %collective-permute-start.4 = (f32[80,128]{1,0:T(8,128)S(1)}, f32[80,128]{1,0:T(8,128)S(1)}, u32[]{:S(2)}, u32[]{:S(2)}) collective-permute-start(f32[80,128]{1,0:T(8,128)S(1)} %get-tuple-element.8.far_ref), channel_id=1, source_target_pairs={{16,32},{48,64},{80,96},{112,128},{144,160},{176,192},{208,224},{2... | collective-permute-start | bytes 122888 | tf_op jit(solution)/shard_map/ppermute | solution.py:326

commit v6 on v5

--- a/solution.py
+++ b/solution.py
@@ -164,7 +164,23 @@
     )
 
 
-def analysis_kernel(half_ref, own_ref, other_ref, own_stats_ref, out_ref):
+def first_analysis_kernel(half_ref, own_ref, other_ref, own_stats_ref, out_ref):
+    @pl.when(half_ref[0] == 0)
+    def _():
+        analysis(half_ref, own_ref, other_ref, own_stats_ref, out_ref)
+
+
+def second_analysis_kernel(half_ref, own_ref, other_ref, own_stats_ref, first_ref, out_ref):
+    @pl.when(half_ref[0] == 0)
+    def _():
+        out_ref[...] = first_ref[...]
+
+    @pl.when(half_ref[0] == 1)
+    def _():
+        analysis(half_ref, own_ref, other_ref, own_stats_ref, out_ref)
+
+
+def analysis(half_ref, own_ref, other_ref, own_stats_ref, out_ref):
     lane8 = lanes_of((8, 128))
     sub8 = lax.broadcasted_iota(jnp.int32, (8, 128), 0)
     lane = lanes_of((MEMBERS, 128))
@@ -268,6 +284,7 @@
         four = in_ref[q * 20 + 16 : q * 20 + 20, :]
         eight = jnp.concatenate([four, four], axis=0)
         lasts.append(jnp.where(sub < 4, eight, pltpu.roll(eight, 64, 1)))
+
     def field(r, v):
         b, result = r // 2, None
         for j in range(4):
@@ -326,6 +343,10 @@
     return lax.ppermute(x, axis, pairs + [(b, a) for a, b in pairs])
 
 
+def one_way(x, axis, pair):
+    return lax.ppermute(x, axis, [pair])
+
+
 def exchange(x):
     return lax.all_to_all(
         x.reshape(8, 5, 4, 128), "q", split_axis=0, concat_axis=0, tiled=True
@@ -346,8 +367,15 @@
         [SMEM] + [VMEM] * 3, array(160, 128),
     )(band, fields, near, far)
     own = exchange(packed)
-    other = swap(jnp.concatenate([own, stats], axis=0), "half", 0)
-    analysed = call(analysis_kernel, [SMEM] + [VMEM] * 3, array(160, 128))(half, own, other, stats)
+    crossing = jnp.concatenate([own, stats], axis=0)
+    other = one_way(crossing, "half", (1, 0))
+    first = call(first_analysis_kernel, [SMEM] + [VMEM] * 3, array(160, 128))(
+        half, own, other, stats
+    )
+    other = one_way(crossing, "half", (0, 1))
+    analysed = call(
+        second_analysis_kernel, [SMEM] + [VMEM] * 4, array(160, 128)
+    )(half, own, other, stats, first)
     near, far = call(
         unpack_kernel, [SMEM, VMEM], array(80, 128), array(80, 128)
     )(band, exchange(analysed))

time: 89 us -> 89.4 us (level)
  the two profiles are of different devices: /device:TPU:56 before, /device:TPU:960 now
where the time goes in v6:
time: 89.4 us; the launch traced here: 89 us
  waiting for transfers between devices  45.9 us (51%)
  starting transfers between devices  27.4 us (31%)
  blocking collectives  8.08 us (9%)
  Pallas kernels  6.57 us (7%)
  local copies, waits for them, and re-layouts  0.92 us (1%)
    ppermute x2, waiting for transfers between devices, one_way(): return lax.ppermute(x, axis, [pair])  30.9 us
    ppermute x2, starting transfers between devices, one_way(): return lax.ppermute(x, axis, [pair])  11.8 us
    ppermute x4, starting transfers between devices, swap(): return lax.ppermute(x, axis, pairs + [(b, a) for a, b in pairs])  11.1 us
    ppermute x4, waiting for transfers between devices, swap(): return lax.ppermute(x, axis, pairs + [(b, a) for a, b in pairs])  10.5 us
    all_to_all x1, blocking collectives, exchange(): lax.all_to_all(x.reshape(8, 5, 4, 128), 'q', split_axis=0, concat_axis=0,...  8.08 us
    all_to_all x1, waiting for transfers between devices, exchange(): lax.all_to_all(x.reshape(8, 5, 4, 128), 'q', split_axis=0, concat_axis=0,...  4.56 us
    all_to_all x1, starting transfers between devices, exchange(): lax.all_to_all(x.reshape(8, 5, 4, 128), 'q', split_axis=0, concat_axis=0,...  4.44 us
    pallas_call x1, Pallas kernels, shards(): call(second_analysis_kernel, [SMEM] + [VMEM] * 4, array(160, 128))  2.67 us
  transfers between devices with their start and end apart: 7, of which 7 were waited for; matrix products, arithmetic and copies ran while one was open for 0% of the time, Pallas kernels for 1%

profile of v6, /device:TPU:960, one launch (start us, length us, event | category | flops | bytes accessed | tf_op | source)
XLA Modules:
  0.0 89.0 jit_solution(16788720569990555381)
XLA Ops:
  0.0 0.9 %copy.8 = f32[5,4,8,128]{3,2,1,0:T(8,128)S(1)} copy(f32[5,4,8,128]{3,1,0,2:T(4,128)} %bitcast.17) | data formatting | bytes 163840 | tf_op jit(solution)/shard_map/transpose | solution.py:359
  0.9 5.4 %collective-permute-start.1 = (f32[160,128]{1,0:T(8,128)S(1)}, f32[160,128]{1,0:T(8,128)S(1)}, u32[]{:S(2)}, u32[]{:S(2)}) collective-permute-start(f32[160,128]{1,0:T(8,128)S(1)} %bitcast.12), channel_id=1, source_target_pairs={{16,32},{48,64},{80,96},{112,128},{144,160},{176,192},{208,224},{2... | collective-permute-start | bytes 245768 | tf_op jit(solution)/shard_map/ppermute | solution.py:343
  6.3 1.9 %collective-permute-start = (f32[160,128]{1,0:T(8,128)S(1)}, f32[160,128]{1,0:T(8,128)S(1)}, u32[]{:S(2)}, u32[]{:S(2)}) collective-permute-start(f32[160,128]{1,0:T(8,128)S(1)} %bitcast.13), channel_id=1, source_target_pairs={{0,16},{32,48},{64,80},{96,112},{128,144},{160,176},{192,208},{224... | collective-permute-start | bytes 245768 | tf_op jit(solution)/shard_map/ppermute | solution.py:343
  8.2 1.1 %collective-permute-done.1.far_ref = f32[160,128]{1,0:T(8,128)S(1)} collective-permute-done((f32[160,128]{1,0:T(8,128)S(1)}, f32[160,128]{1,0:T(8,128)S(1)}, u32[]{:S(2)}, u32[]{:S(2)}) %collective-permute-start.1) | collective-permute-done | bytes 81952 | tf_op jit(solution)/shard_map/ppermute | solution.py:343
  9.3 3.3 %collective-permute-done.near_ref = f32[160,128]{1,0:T(8,128)S(1)} collective-permute-done((f32[160,128]{1,0:T(8,128)S(1)}, f32[160,128]{1,0:T(8,128)S(1)}, u32[]{:S(2)}, u32[]{:S(2)}) %collective-permute-start) | collective-permute-done | bytes 81952 | tf_op jit(solution)/shard_map/ppermute | solution.py:343
  12.6 1.7 %shard_map.73 = f32[160,128]{1,0:T(8,128)} custom-call(s32[1]{0:T(128)} %bitcast.band_ref, f32[160,128]{1,0:T(8,128)S(1)} %bitcast.14, f32[160,128]{1,0:T(8,128)S(1)} %collective-permute-done.near_ref, f32[160,128]{1,0:T(8,128)S(1)} %collective-permute-done.1.far_ref), custom_call_target="tpu_custom_call" | custom-call | tf_op jit(solution)/shard_map/pallas_call | solution.py:365
  14.3 0.0 copy-start
  14.3 0.0 copy-start.1
  14.3 0.0 copy-start.2
  14.3 0.0 copy-start.4
  14.3 0.0 copy-start.5
  14.3 4.4 %all-to-all-start = ((f32[8,5,4,128]{3,2,1,0:T(4,128)}), f32[8,5,4,128]{3,2,1,0:T(4,128)S(1)}, u32[]{:S(2)}, u32[]{:S(2)}) async-start(f32[8,5,4,128]{3,2,1,0:T(4,128)} %bitcast.4), calls=%async_computation | async-start | bytes 163840 | tf_op jit(solution)/shard_map/all_to_all | solution.py:351
  18.7 0.0 copy-done
  18.7 0.0 copy-done.1
  18.7 0.0 copy-done.2
  18.8 0.0 copy-done.3
  18.8 0.0 copy-done.4
  18.8 0.0 copy-done.5
  18.8 1.1 %shard_map.74.own_stats_ref = f32[8,128]{1,0:T(8,128)S(1)} custom-call(s32[2]{0:T(128)S(1)} %copy-done.5, f32[2,3]{1,0:T(2,128)S(1)} %copy-done, s32[2,3]{1,0:T(2,128)S(1)} %copy-done.1, f32[2,128]{1,0:T(2,128)S(1)} %copy-done.2, s32[2,128]{1,0:T(2,128)S(1)} %copy-done.3, f32[2,128]{1,0:T(2,128)S(1)} %copy-done.4), custom_call_target="tpu_custom_call" | custom-call | tf_op jit(solution)/shard_map/pallas_call | solution.py:362
  19.9 4.6 %all-to-all-done = f32[8,5,4,128]{3,2,1,0:T(4,128)S(1)} async-done(((f32[8,5,4,128]{3,2,1,0:T(4,128)}), f32[8,5,4,128]{3,2,1,0:T(4,128)S(1)}, u32[]{:S(2)}, u32[]{:S(2)}) %all-to-all-start) | async-done | bytes 81952 | tf_op jit(solution)/shard_map/all_to_all | solution.py:351
  24.5 10.5 %collective-permute-start.3 = (f32[168,128]{1,0:T(8,128)S(1)}, f32[168,128]{1,0:T(8,128)S(1)}, u32[]{:S(2)}, u32[]{:S(2)}) collective-permute-start(f32[168,128]{1,0:T(8,128)S(1)} %pad_maximum_fusion), channel_id=1, source_target_pairs={{8,0},{9,1},{10,2},{11,3},{12,4},{13,5},{14,6},{15,7},{24,16},{25,... | collective-permute-start | bytes 258056 | tf_op jit(solution)/shard_map/ppermute | solution.py:347
  35.0 1.3 %collective-permute-start.2 = (f32[168,128]{1,0:T(8,128)S(1)}, f32[168,128]{1,0:T(8,128)S(1)}, u32[]{:S(2)}, u32[]{:S(2)}) collective-permute-start(f32[168,128]{1,0:T(8,128)S(1)} %pad_maximum_fusion), channel_id=1, source_target_pairs={{0,8},{1,9},{2,10},{3,11},{4,12},{5,13},{6,14},{7,15},{16,24},{17,... | collective-permute-start | bytes 258056 | tf_op jit(solution)/shard_map/ppermute | solution.py:347
  36.3 10.3 %collective-permute-done.3.other_ref = f32[168,128]{1,0:T(8,128)S(1)} collective-permute-done((f32[168,128]{1,0:T(8,128)S(1)}, f32[168,128]{1,0:T(8,128)S(1)}, u32[]{:S(2)}, u32[]{:S(2)}) %collective-permute-start.3) | collective-permute-done | bytes 86048 | tf_op jit(solution)/shard_map/ppermute | solution.py:347
  46.6 20.6 %collective-permute-done.2.other_ref = f32[168,128]{1,0:T(8,128)S(1)} collective-permute-done((f32[168,128]{1,0:T(8,128)S(1)}, f32[168,128]{1,0:T(8,128)S(1)}, u32[]{:S(2)}, u32[]{:S(2)}) %collective-permute-start.2) | collective-permute-done | bytes 86048 | tf_op jit(solution)/shard_map/ppermute | solution.py:347
  67.2 2.7 %shard_map.76 = f32[160,128]{1,0:T(8,128)S(1)} custom-call(s32[1]{0:T(128)} %bitcast.1.half_ref, f32[160,128]{1,0:T(8,128)S(1)} %bitcast.11, f32[168,128]{1,0:T(8,128)S(1)} %collective-permute-done.2.other_ref, f32[8,128]{1,0:T(8,128)S(1)} %shard_map.74.own_stats_ref, f32[160,128]{1,0:T(8,128)S(1)} %shard_map.75.first_ref), custom_call_target="tpu_custom_call" | custom-call | tf_op jit(solution)/shard_map/pallas_call | solution.py:376
  69.8 8.1 %all_to_all.10 = f32[8,5,4,128]{3,2,1,0:T(4,128)S(1)} all-to-all(f32[8,5,4,128]{3,2,1,0:T(4,128)S(1)} %bitcast.16), channel_id=1, replica_groups=mesh['band'=64,'half'=2,'q'=8] {'q'}, dimensions={0} | all-to-all | bytes 163840 | tf_op jit(solution)/shard_map/all_to_all | solution.py:351
  77.9 0.2 shard_map.77
  78.1 1.9 %collective-permute-start.4 = (f32[80,128]{1,0:T(8,128)S(1)}, f32[80,128]{1,0:T(8,128)S(1)}, u32[]{:S(2)}, u32[]{:S(2)}) collective-permute-start(f32[80,128]{1,0:T(8,128)S(1)} %get-tuple-element.7.near_ref), channel_id=1, source_target_pairs={{0,16},{32,48},{64,80},{96,112},{128,144},{160,176},{192,208},{224... | collective-permute-start | bytes 122888 | tf_op jit(solution)/shard_map/ppermute | solution.py:343
  80.1 1.9 %collective-permute-start.5 = (f32[80,128]{1,0:T(8,128)S(1)}, f32[80,128]{1,0:T(8,128)S(1)}, u32[]{:S(2)}, u32[]{:S(2)}) collective-permute-start(f32[80,128]{1,0:T(8,128)S(1)} %get-tuple-element.8.far_ref), channel_id=1, source_target_pairs={{16,32},{48,64},{80,96},{112,128},{144,160},{176,192},{208,224},{2... | collective-permute-start | bytes 122888 | tf_op jit(solution)/shard_map/ppermute | solution.py:343
  82.0 2.0 %collective-permute-done.4.from_near_ref = f32[80,128]{1,0:T(8,128)S(1)} collective-permute-done((f32[80,128]{1,0:T(8,128)S(1)}, f32[80,128]{1,0:T(8,128)S(1)}, u32[]{:S(2)}, u32[]{:S(2)}) %collective-permute-start.4) | collective-permute-done | bytes 40992 | tf_op jit(solution)/shard_map/ppermute | solution.py:343
  84.0 4.0 %collective-permute-done.5.from_far_ref = f32[80,128]{1,0:T(8,128)S(1)} collective-permute-done((f32[80,128]{1,0:T(8,128)S(1)}, f32[80,128]{1,0:T(8,128)S(1)}, u32[]{:S(2)}, u32[]{:S(2)}) %collective-permute-start.5) | collective-permute-done | bytes 40992 | tf_op jit(solution)/shard_map/ppermute | solution.py:343
  88.1 0.9 %shard_map.78 = f32[160,128]{1,0:T(8,128)} custom-call(s32[1]{0:T(128)} %bitcast.band_ref, f32[80,128]{1,0:T(8,128)S(1)} %get-tuple-element.7.near_ref, f32[80,128]{1,0:T(8,128)S(1)} %get-tuple-element.8.far_ref, f32[80,128]{1,0:T(8,128)S(1)} %collective-permute-done.4.from_near_ref, f32[80,128]{1,0:T(8,128)S(1)} %collective-permute-done.5.from_far_ref), custom_call_target="tpu_custom_call" | custom-call | tf_op jit(solution)/shard_map/pallas_call | solution.py:384
  (3 shorter events, 0.0 us)
Async XLA Ops:
  0.9 8.4 %collective-permute-start.1 = (f32[160,128]{1,0:T(8,128)S(1)}, f32[160,128]{1,0:T(8,128)S(1)}, u32[]{:S(2)}, u32[]{:S(2)}) collective-permute-start(f32[160,128]{1,0:T(8,128)S(1)} %bitcast.12), channel_id=1, source_target_pairs={{16,32},{48,64},{80,96},{112,128},{144,160},{176,192},{208,224},{2... | collective-permute-start | bytes 245768 | tf_op jit(solution)/shard_map/ppermute | solution.py:343
  6.3 6.3 %collective-permute-start = (f32[160,128]{1,0:T(8,128)S(1)}, f32[160,128]{1,0:T(8,128)S(1)}, u32[]{:S(2)}, u32[]{:S(2)}) collective-permute-start(f32[160,128]{1,0:T(8,128)S(1)} %bitcast.13), channel_id=1, source_target_pairs={{0,16},{32,48},{64,80},{96,112},{128,144},{160,176},{192,208},{224... | collective-permute-start | bytes 245768 | tf_op jit(solution)/shard_map/ppermute | solution.py:343
  14.3 4.5 %copy-start = (f32[2,3]{1,0:T(2,128)S(1)}, f32[2,3]{1,0:T(2,128)}, u32[]{:S(2)}) copy-start(f32[2,3]{1,0:T(2,128)} %loc_ref.1) | copy-start | bytes 76
  14.3 4.5 %copy-start.1 = (s32[2,3]{1,0:T(2,128)S(1)}, s32[2,3]{1,0:T(2,128)}, u32[]{:S(2)}) copy-start(s32[2,3]{1,0:T(2,128)} %near_ref.1) | copy-start | bytes 76
  14.3 4.5 %copy-start.2 = (f32[2,128]{1,0:T(2,128)S(1)}, f32[2,128]{1,0:T(2,128)}, u32[]{:S(2)}) copy-start(f32[2,128]{1,0:T(2,128)} %value_ref.1) | copy-start | bytes 3076
  14.3 4.5 %copy-start.3 = (s32[2,128]{1,0:T(2,128)S(1)}, s32[2,128]{1,0:T(2,128)}, u32[]{:S(2)}) copy-start(s32[2,128]{1,0:T(2,128)} %site_ref.1) | copy-start | bytes 3076
  14.3 4.5 %copy-start.4 = (f32[2,128]{1,0:T(2,128)S(1)}, f32[2,128]{1,0:T(2,128)}, u32[]{:S(2)}) copy-start(f32[2,128]{1,0:T(2,128)} %precision_ref.1) | copy-start | bytes 3076
  14.3 4.5 %copy-start.5 = (s32[2]{0:T(128)S(1)}, s32[2]{0:T(128)}, u32[]{:S(2)}) copy-start(s32[2]{0:T(128)} %count_ref.1) | copy-start | bytes 28
  14.3 10.2 %all-to-all-start = ((f32[8,5,4,128]{3,2,1,0:T(4,128)}), f32[8,5,4,128]{3,2,1,0:T(4,128)S(1)}, u32[]{:S(2)}, u32[]{:S(2)}) async-start(f32[8,5,4,128]{3,2,1,0:T(4,128)} %bitcast.4), calls=%async_computation | async-start | bytes 163840 | tf_op jit(solution)/shard_map/all_to_all | solution.py:351
  24.5 22.1 %collective-permute-start.3 = (f32[168,128]{1,0:T(8,128)S(1)}, f32[168,128]{1,0:T(8,128)S(1)}, u32[]{:S(2)}, u32[]{:S(2)}) collective-permute-start(f32[168,128]{1,0:T(8,128)S(1)} %pad_maximum_fusion), channel_id=1, source_target_pairs={{8,0},{9,1},{10,2},{11,3},{12,4},{13,5},{14,6},{15,7},{24,16},{25,... | collective-permute-start | bytes 258056 | tf_op jit(solution)/shard_map/ppermute | solution.py:347
  35.0 32.2 %collective-permute-start.2 = (f32[168,128]{1,0:T(8,128)S(1)}, f32[168,128]{1,0:T(8,128)S(1)}, u32[]{:S(2)}, u32[]{:S(2)}) collective-permute-start(f32[168,128]{1,0:T(8,128)S(1)} %pad_maximum_fusion), channel_id=1, source_target_pairs={{0,8},{1,9},{2,10},{3,11},{4,12},{5,13},{6,14},{7,15},{16,24},{17,... | collective-permute-start | bytes 258056 | tf_op jit(solution)/shard_map/ppermute | solution.py:347
  78.1 5.9 %collective-permute-start.4 = (f32[80,128]{1,0:T(8,128)S(1)}, f32[80,128]{1,0:T(8,128)S(1)}, u32[]{:S(2)}, u32[]{:S(2)}) collective-permute-start(f32[80,128]{1,0:T(8,128)S(1)} %get-tuple-element.7.near_ref), channel_id=1, source_target_pairs={{0,16},{32,48},{64,80},{96,112},{128,144},{160,176},{192,208},{224... | collective-permute-start | bytes 122888 | tf_op jit(solution)/shard_map/ppermute | solution.py:343
  80.1 8.0 %collective-permute-start.5 = (f32[80,128]{1,0:T(8,128)S(1)}, f32[80,128]{1,0:T(8,128)S(1)}, u32[]{:S(2)}, u32[]{:S(2)}) collective-permute-start(f32[80,128]{1,0:T(8,128)S(1)} %get-tuple-element.8.far_ref), channel_id=1, source_target_pairs={{16,32},{48,64},{80,96},{112,128},{144,160},{176,192},{208,224},{2... | collective-permute-start | bytes 122888 | tf_op jit(solution)/shard_map/ppermute | solution.py:343

commit v7 on v4

--- a/solution.py
+++ b/solution.py
@@ -78,7 +78,8 @@
     return jnp.where(even, far, near), jnp.where(even, near, far)
 
 
-def background_kernel(bands, band_ref, centre_ref, near_ref, far_ref, out_ref):
+def background_kernel(bands, band_ref, centre_ref, near_ref, far_ref, stats_ref, own_ref, out_ref):
+    out_ref[160:168, :] = stats_ref[...]
     low, centre, high = [], [], []
     for r in range(4):
         at = [slice((v * 4 + r) * 8, (v * 4 + r) * 8 + 8) for v in range(5)]
@@ -106,13 +107,19 @@
                 u, v = g // 4, g % 4
                 piece = turned(rows[chosen[b]][v], g - (2 * j + u))
                 slab = piece if slab is None else jnp.where(group == g, piece, slab)
+            own_ref[q * 20 + 8 * b : q * 20 + 8 * b + 8, :] = slab
             out_ref[q * 20 + 8 * b : q * 20 + 8 * b + 8, :] = slab
         last = jnp.where(
             lane < 32, turned(rows[chosen[0]][4], -2 * j), turned(rows[chosen[1]][4], 2 - 2 * j)
         )
-        out_ref[q * 20 + 16 : q * 20 + 20, :] = jnp.where(
-            lane[:4] < 64, last[:4], pltpu.roll(last, 64, 1)[4:]
-        )
+        four = jnp.where(lane[:4] < 64, last[:4], pltpu.roll(last, 64, 1)[4:])
+        own_ref[q * 20 + 16 : q * 20 + 20, :] = four
+        out_ref[q * 20 + 16 : q * 20 + 20, :] = four
+
+
+def strip_kernel(in_ref, own_ref, half_ref, out_ref, stats_ref):
+    out_ref[...] = in_ref[:160, :]
+    stats_ref[...] = in_ref[160:168, :]
 
 
 def statistics_kernel(count_ref, loc_ref, near_ref, value_ref, site_ref, precision_ref, out_ref):
@@ -341,13 +348,16 @@
     stats = call(statistics_kernel, [SMEM] * 3 + [VMEM] * 3, array(8, 128))(
         obs_count, loc_weight, neighbours, obs_value, obs_site, obs_precision
     )
-    packed = call(
+    packed, payload = call(
         functools.partial(background_kernel, lax.axis_size("band")),
-        [SMEM] + [VMEM] * 3, array(160, 128),
-    )(band, fields, near, far)
+        [SMEM] + [VMEM] * 4, array(160, 128), array(168, 128),
+    )(band, fields, near, far, stats)
+    payload = swap(payload, "half", 0)
     own = exchange(packed)
-    other = swap(own, "half", 0)
-    other_stats = swap(stats, "half", 0)
+    other, other_stats = call(
+        strip_kernel, [VMEM, VMEM, SMEM], array(160, 128), array(8, 128)
+    )(payload, own, half)
+    other = exchange(other)
     analysed = call(analysis_kernel, [SMEM] + [VMEM] * 4, array(160, 128))(
         half, own, other, stats, other_stats
     )

time: 99.2 us -> 84.2 us (0.85)
  the two profiles are of different devices: /device:TPU:24 before, /device:TPU:120 now
where the time goes in v7:
time: 84.2 us; the launch traced here: 83.8 us
  starting transfers between devices  43.8 us (52%)
  blocking collectives  16.2 us (19%)
  waiting for transfers between devices  15.6 us (19%)
  Pallas kernels  6.54 us (8%)
  local copies, waits for them, and re-layouts  1.59 us (2%)
    ppermute x5, starting transfers between devices, swap(): return lax.ppermute(x, axis, pairs + [(b, a) for a, b in pairs])  39.5 us
    all_to_all x2, blocking collectives, exchange(): lax.all_to_all(x.reshape(8, 5, 4, 128), 'q', split_axis=0, concat_axis=0,...  16.2 us
    ppermute x5, waiting for transfers between devices, swap(): return lax.ppermute(x, axis, pairs + [(b, a) for a, b in pairs])  9.85 us
    all_to_all x1, waiting for transfers between devices, exchange(): lax.all_to_all(x.reshape(8, 5, 4, 128), 'q', split_axis=0, concat_axis=0,...  5.71 us
    all_to_all x1, starting transfers between devices, exchange(): lax.all_to_all(x.reshape(8, 5, 4, 128), 'q', split_axis=0, concat_axis=0,...  4.31 us
    pallas_call x1, Pallas kernels, shards(): call(analysis_kernel, [SMEM] + [VMEM] * 4, array(160, 128))  2.64 us
  transfers between devices with their start and end apart: 6, of which 4 were waited for; matrix products, arithmetic and copies ran while one was open for 0% of the time, Pallas kernels for 1%

profile of v7, /device:TPU:120, one launch (start us, length us, event | category | flops | bytes accessed | tf_op | source)
XLA Modules:
  0.0 83.8 jit_solution(15176382675381743438)
XLA Ops:
  0.0 0.9 %copy.8 = f32[5,4,8,128]{3,2,1,0:T(8,128)S(1)} copy(f32[5,4,8,128]{3,1,0,2:T(4,128)} %bitcast.20) | data formatting | bytes 163840 | tf_op jit(solution)/shard_map/transpose | solution.py:345
  0.9 4.7 %collective-permute-start.1 = (f32[160,128]{1,0:T(8,128)S(1)}, f32[160,128]{1,0:T(8,128)S(1)}, u32[]{:S(2)}, u32[]{:S(2)}) collective-permute-start(f32[160,128]{1,0:T(8,128)S(1)} %bitcast.13), channel_id=1, source_target_pairs={{16,32},{48,64},{80,96},{112,128},{144,160},{176,192},{208,224},{2... | collective-permute-start | bytes 245768 | tf_op jit(solution)/shard_map/ppermute | solution.py:333
  5.6 1.9 %collective-permute-start = (f32[160,128]{1,0:T(8,128)S(1)}, f32[160,128]{1,0:T(8,128)S(1)}, u32[]{:S(2)}, u32[]{:S(2)}) collective-permute-start(f32[160,128]{1,0:T(8,128)S(1)} %bitcast.14), channel_id=1, source_target_pairs={{0,16},{32,48},{64,80},{96,112},{128,144},{160,176},{192,208},{224... | collective-permute-start | bytes 245768 | tf_op jit(solution)/shard_map/ppermute | solution.py:333
  7.5 0.0 copy-start.3
  7.5 0.0 copy-start.4
  7.5 0.0 copy-start.1
  7.6 0.0 copy-start.2
  7.6 0.0 copy-start
  7.6 0.0 copy-start.5
  7.6 0.6 copy-done.3
  8.2 0.0 copy-done.4
  8.2 0.0 copy-done.1
  8.2 0.0 copy-done.2
  8.2 0.0 copy-done
  8.3 0.0 copy-done.5
  8.3 1.1 %shard_map.73.stats_ref.own_stats_ref = f32[8,128]{1,0:T(8,128)S(1)} custom-call(s32[2]{0:T(128)S(1)} %copy-done.5, f32[2,3]{1,0:T(2,128)S(1)} %copy-done, s32[2,3]{1,0:T(2,128)S(1)} %copy-done.1, f32[2,128]{1,0:T(2,128)S(1)} %copy-done.2, s32[2,128]{1,0:T(2,128)S(1)} %copy-done.3, f32[2,128]{1,0:T(2,128)S(1)} %copy-done.4), custom_call_target="tpu_custom_call" | custom-call | tf_op jit(solution)/shard_map/pallas_call | solution.py:348
  9.4 1.2 %collective-permute-done.1.far_ref = f32[160,128]{1,0:T(8,128)S(1)} collective-permute-done((f32[160,128]{1,0:T(8,128)S(1)}, f32[160,128]{1,0:T(8,128)S(1)}, u32[]{:S(2)}, u32[]{:S(2)}) %collective-permute-start.1) | collective-permute-done | bytes 81952 | tf_op jit(solution)/shard_map/ppermute | solution.py:333
  10.5 1.4 %collective-permute-done.near_ref = f32[160,128]{1,0:T(8,128)S(1)} collective-permute-done((f32[160,128]{1,0:T(8,128)S(1)}, f32[160,128]{1,0:T(8,128)S(1)}, u32[]{:S(2)}, u32[]{:S(2)}) %collective-permute-start) | collective-permute-done | bytes 81952 | tf_op jit(solution)/shard_map/ppermute | solution.py:333
  11.9 1.7 %shard_map.74 = (f32[160,128]{1,0:T(8,128)}, f32[168,128]{1,0:T(8,128)S(1)}) custom-call(s32[1]{0:T(128)} %bitcast.band_ref, f32[160,128]{1,0:T(8,128)S(1)} %bitcast.15, f32[160,128]{1,0:T(8,128)S(1)} %collective-permute-done.near_ref, f32[160,128]{1,0:T(8,128)S(1)} %collective-permute-done.1.far_ref, f32[8,128]{1,0:T(8,128)S(1)} %shard_map.73.stats_ref.own_stats_ref), custom_call_target="tpu_custom_call" | custom-call | tf_op jit(solution)/shard_map/pallas_call | solution.py:351
  13.6 24.9 %collective-permute-start.2 = (f32[168,128]{1,0:T(8,128)S(1)}, f32[168,128]{1,0:T(8,128)S(1)}, u32[]{:S(2)}, u32[]{:S(2)}) collective-permute-start(f32[168,128]{1,0:T(8,128)S(1)} %get-tuple-element.12), channel_id=1, source_target_pairs={{0,8},{8,0},{1,9},{9,1},{2,10},{10,2},{3,11},{11,3},{4,12},{12,4},... | collective-permute-start | bytes 258056 | tf_op jit(solution)/shard_map/ppermute | solution.py:333
  38.5 4.3 %all-to-all-start = ((f32[8,5,4,128]{3,2,1,0:T(4,128)}), f32[8,5,4,128]{3,2,1,0:T(4,128)S(1)}, u32[]{:S(2)}, u32[]{:S(2)}) async-start(f32[8,5,4,128]{3,2,1,0:T(4,128)} %bitcast.4), calls=%async_computation | async-start | bytes 163840 | tf_op jit(solution)/shard_map/all_to_all | solution.py:337
  42.8 5.7 %all-to-all-done = f32[8,5,4,128]{3,2,1,0:T(4,128)S(1)} async-done(((f32[8,5,4,128]{3,2,1,0:T(4,128)}), f32[8,5,4,128]{3,2,1,0:T(4,128)S(1)}, u32[]{:S(2)}, u32[]{:S(2)}) %all-to-all-start) | async-done | bytes 81952 | tf_op jit(solution)/shard_map/all_to_all | solution.py:337
  48.5 0.0 collective-permute-done.2.in_ref
  48.5 8.1 %all_to_all.15 = f32[8,5,4,128]{3,2,1,0:T(4,128)S(1)} all-to-all(f32[8,5,4,128]{3,2,1,0:T(4,128)S(1)} %bitcast.19), channel_id=1, replica_groups=mesh['band'=64,'half'=2,'q'=8] {'q'}, dimensions={0} | all-to-all | bytes 163840 | tf_op jit(solution)/shard_map/all_to_all | solution.py:337
  56.6 2.6 %shard_map.76 = f32[160,128]{1,0:T(8,128)S(1)} custom-call(s32[1]{0:T(128)} %bitcast.1.half_ref, f32[160,128]{1,0:T(8,128)S(1)} %bitcast.12, f32[160,128]{1,0:T(8,128)S(1)} %bitcast.16, f32[8,128]{1,0:T(8,128)S(1)} %shard_map.73.stats_ref.own_stats_ref, f32[8,128]{1,0:T(8,128)S(1)} %get-tuple-element.14.other_stats_ref), custom_call_target="tpu_custom_call" | custom-call | tf_op jit(solution)/shard_map/pallas_call | solution.py:361
  59.2 8.1 %all_to_all.16 = f32[8,5,4,128]{3,2,1,0:T(4,128)S(1)} all-to-all(f32[8,5,4,128]{3,2,1,0:T(4,128)S(1)} %bitcast.17), channel_id=1, replica_groups=mesh['band'=64,'half'=2,'q'=8] {'q'}, dimensions={0} | all-to-all | bytes 163840 | tf_op jit(solution)/shard_map/all_to_all | solution.py:337
  67.3 0.2 shard_map.77
  67.5 6.1 %collective-permute-start.3 = (f32[80,128]{1,0:T(8,128)S(1)}, f32[80,128]{1,0:T(8,128)S(1)}, u32[]{:S(2)}, u32[]{:S(2)}) collective-permute-start(f32[80,128]{1,0:T(8,128)S(1)} %get-tuple-element.15.near_ref), channel_id=1, source_target_pairs={{0,16},{32,48},{64,80},{96,112},{128,144},{160,176},{192,208},{224... | collective-permute-start | bytes 122888 | tf_op jit(solution)/shard_map/ppermute | solution.py:333
  73.6 1.9 %collective-permute-start.4 = (f32[80,128]{1,0:T(8,128)S(1)}, f32[80,128]{1,0:T(8,128)S(1)}, u32[]{:S(2)}, u32[]{:S(2)}) collective-permute-start(f32[80,128]{1,0:T(8,128)S(1)} %get-tuple-element.16.far_ref), channel_id=1, source_target_pairs={{16,32},{48,64},{80,96},{112,128},{144,160},{176,192},{208,224},{2... | collective-permute-start | bytes 122888 | tf_op jit(solution)/shard_map/ppermute | solution.py:333
  75.6 0.0 collective-permute-done.3.from_near_ref
  75.6 7.2 %collective-permute-done.4.from_far_ref = f32[80,128]{1,0:T(8,128)S(1)} collective-permute-done((f32[80,128]{1,0:T(8,128)S(1)}, f32[80,128]{1,0:T(8,128)S(1)}, u32[]{:S(2)}, u32[]{:S(2)}) %collective-permute-start.4) | collective-permute-done | bytes 40992 | tf_op jit(solution)/shard_map/ppermute | solution.py:333
  82.8 0.9 %shard_map.78 = f32[160,128]{1,0:T(8,128)} custom-call(s32[1]{0:T(128)} %bitcast.band_ref, f32[80,128]{1,0:T(8,128)S(1)} %get-tuple-element.15.near_ref, f32[80,128]{1,0:T(8,128)S(1)} %get-tuple-element.16.far_ref, f32[80,128]{1,0:T(8,128)S(1)} %collective-permute-done.3.from_near_ref, f32[80,128]{1,0:T(8,128)S(1)} %collective-permute-done.4.from_far_ref), custom_call_target="tpu_custom_call" | custom-call | tf_op jit(solution)/shard_map/pallas_call | solution.py:369
  (1 shorter events, 0.0 us)
Async XLA Ops:
  0.9 9.6 %collective-permute-start.1 = (f32[160,128]{1,0:T(8,128)S(1)}, f32[160,128]{1,0:T(8,128)S(1)}, u32[]{:S(2)}, u32[]{:S(2)}) collective-permute-start(f32[160,128]{1,0:T(8,128)S(1)} %bitcast.13), channel_id=1, source_target_pairs={{16,32},{48,64},{80,96},{112,128},{144,160},{176,192},{208,224},{2... | collective-permute-start | bytes 245768 | tf_op jit(solution)/shard_map/ppermute | solution.py:333
  5.6 6.3 %collective-permute-start = (f32[160,128]{1,0:T(8,128)S(1)}, f32[160,128]{1,0:T(8,128)S(1)}, u32[]{:S(2)}, u32[]{:S(2)}) collective-permute-start(f32[160,128]{1,0:T(8,128)S(1)} %bitcast.14), channel_id=1, source_target_pairs={{0,16},{32,48},{64,80},{96,112},{128,144},{160,176},{192,208},{224... | collective-permute-start | bytes 245768 | tf_op jit(solution)/shard_map/ppermute | solution.py:333
  7.5 0.7 copy-start.3
  7.5 0.7 copy-start.4
  7.5 0.7 copy-start.1
  7.6 0.7 copy-start.2
  7.6 0.7 copy-start
  7.6 0.7 copy-start.5
  13.6 34.9 %collective-permute-start.2 = (f32[168,128]{1,0:T(8,128)S(1)}, f32[168,128]{1,0:T(8,128)S(1)}, u32[]{:S(2)}, u32[]{:S(2)}) collective-permute-start(f32[168,128]{1,0:T(8,128)S(1)} %get-tuple-element.12), channel_id=1, source_target_pairs={{0,8},{8,0},{1,9},{9,1},{2,10},{10,2},{3,11},{11,3},{4,12},{12,4},... | collective-permute-start | bytes 258056 | tf_op jit(solution)/shard_map/ppermute | solution.py:333
  38.5 10.0 %all-to-all-start = ((f32[8,5,4,128]{3,2,1,0:T(4,128)}), f32[8,5,4,128]{3,2,1,0:T(4,128)S(1)}, u32[]{:S(2)}, u32[]{:S(2)}) async-start(f32[8,5,4,128]{3,2,1,0:T(4,128)} %bitcast.4), calls=%async_computation | async-start | bytes 163840 | tf_op jit(solution)/shard_map/all_to_all | solution.py:337
  67.5 8.1 %collective-permute-start.3 = (f32[80,128]{1,0:T(8,128)S(1)}, f32[80,128]{1,0:T(8,128)S(1)}, u32[]{:S(2)}, u32[]{:S(2)}) collective-permute-start(f32[80,128]{1,0:T(8,128)S(1)} %get-tuple-element.15.near_ref), channel_id=1, source_target_pairs={{0,16},{32,48},{64,80},{96,112},{128,144},{160,176},{192,208},{224... | collective-permute-start | bytes 122888 | tf_op jit(solution)/shard_map/ppermute | solution.py:333
  73.6 9.2 %collective-permute-start.4 = (f32[80,128]{1,0:T(8,128)S(1)}, f32[80,128]{1,0:T(8,128)S(1)}, u32[]{:S(2)}, u32[]{:S(2)}) collective-permute-start(f32[80,128]{1,0:T(8,128)S(1)} %get-tuple-element.16.far_ref), channel_id=1, source_target_pairs={{16,32},{48,64},{80,96},{112,128},{144,160},{176,192},{208,224},{2... | collective-permute-start | bytes 122888 | tf_op jit(solution)/shard_map/ppermute | solution.py:333

commit v8 on v7

--- a/solution.py
+++ b/solution.py
@@ -78,7 +78,7 @@
     return jnp.where(even, far, near), jnp.where(even, near, far)
 
 
-def background_kernel(bands, band_ref, centre_ref, near_ref, far_ref, stats_ref, own_ref, out_ref):
+def background_kernel(bands, band_ref, centre_ref, near_ref, far_ref, stats_ref, out_ref):
     out_ref[160:168, :] = stats_ref[...]
     low, centre, high = [], [], []
     for r in range(4):
@@ -107,14 +107,17 @@
                 u, v = g // 4, g % 4
                 piece = turned(rows[chosen[b]][v], g - (2 * j + u))
                 slab = piece if slab is None else jnp.where(group == g, piece, slab)
-            own_ref[q * 20 + 8 * b : q * 20 + 8 * b + 8, :] = slab
             out_ref[q * 20 + 8 * b : q * 20 + 8 * b + 8, :] = slab
         last = jnp.where(
             lane < 32, turned(rows[chosen[0]][4], -2 * j), turned(rows[chosen[1]][4], 2 - 2 * j)
         )
-        four = jnp.where(lane[:4] < 64, last[:4], pltpu.roll(last, 64, 1)[4:])
-        own_ref[q * 20 + 16 : q * 20 + 20, :] = four
-        out_ref[q * 20 + 16 : q * 20 + 20, :] = four
+        out_ref[q * 20 + 16 : q * 20 + 20, :] = jnp.where(
+            lane[:4] < 64, last[:4], pltpu.roll(last, 64, 1)[4:]
+        )
+
+
+def fields_kernel(in_ref, out_ref):
+    out_ref[...] = in_ref[:160, :]
 
 
 def strip_kernel(in_ref, own_ref, half_ref, out_ref, stats_ref):
@@ -348,11 +351,12 @@
     stats = call(statistics_kernel, [SMEM] * 3 + [VMEM] * 3, array(8, 128))(
         obs_count, loc_weight, neighbours, obs_value, obs_site, obs_precision
     )
-    packed, payload = call(
+    mine = call(
         functools.partial(background_kernel, lax.axis_size("band")),
-        [SMEM] + [VMEM] * 4, array(160, 128), array(168, 128),
+        [SMEM] + [VMEM] * 4, array(168, 128),
     )(band, fields, near, far, stats)
-    payload = swap(payload, "half", 0)
+    payload = swap(mine, "half", 0)
+    packed = call(fields_kernel, [VMEM], array(160, 128))(mine)
     own = exchange(packed)
     other, other_stats = call(
         strip_kernel, [VMEM, VMEM, SMEM], array(160, 128), array(8, 128)

time: 84.2 us -> 83.6 us (level)
  transfers between devices with their start and end apart: 6 -> 6, of which waited for: 4 -> 4; matrix products, arithmetic and copies ran while one was open for 0% -> 0% of each run, Pallas kernels for 1% -> 2%
where the time goes in v8:
time: 83.6 us; the launch traced here: 83.2 us
  starting transfers between devices  43.6 us (52%)
  blocking collectives  16.2 us (19%)
  waiting for transfers between devices  15.2 us (18%)
  Pallas kernels  6.55 us (8%)
  local copies, waits for them, and re-layouts  1.59 us (2%)
    ppermute x5, starting transfers between devices, swap(): return lax.ppermute(x, axis, pairs + [(b, a) for a, b in pairs])  39.3 us
    all_to_all x2, blocking collectives, exchange(): lax.all_to_all(x.reshape(8, 5, 4, 128), 'q', split_axis=0, concat_axis=0,...  16.2 us
    ppermute x5, waiting for transfers between devices, swap(): return lax.ppermute(x, axis, pairs + [(b, a) for a, b in pairs])  9.46 us
    all_to_all x1, waiting for transfers between devices, exchange(): lax.all_to_all(x.reshape(8, 5, 4, 128), 'q', split_axis=0, concat_axis=0,...  5.71 us
    all_to_all x1, starting transfers between devices, exchange(): lax.all_to_all(x.reshape(8, 5, 4, 128), 'q', split_axis=0, concat_axis=0,...  4.3 us
    pallas_call x1, Pallas kernels, shards(): call(analysis_kernel, [SMEM] + [VMEM] * 4, array(160, 128))  2.63 us
  transfers between devices with their start and end apart: 6, of which 4 were waited for; matrix products, arithmetic and copies ran while one was open for 0% of the time, Pallas kernels for 2%

profile of v8, /device:TPU:120, one launch (start us, length us, event | category | flops | bytes accessed | tf_op | source)
XLA Modules:
  0.0 83.2 jit_solution(4576863071334109796)
XLA Ops:
  0.0 0.9 %copy.8 = f32[5,4,8,128]{3,2,1,0:T(8,128)S(1)} copy(f32[5,4,8,128]{3,1,0,2:T(4,128)} %bitcast.20) | data formatting | bytes 163840 | tf_op jit(solution)/shard_map/transpose | solution.py:348
  0.9 4.7 %collective-permute-start.1 = (f32[160,128]{1,0:T(8,128)S(1)}, f32[160,128]{1,0:T(8,128)S(1)}, u32[]{:S(2)}, u32[]{:S(2)}) collective-permute-start(f32[160,128]{1,0:T(8,128)S(1)} %bitcast.16), channel_id=1, source_target_pairs={{16,32},{48,64},{80,96},{112,128},{144,160},{176,192},{208,224},{2... | collective-permute-start | bytes 245768 | tf_op jit(solution)/shard_map/ppermute | solution.py:336
  5.6 1.9 %collective-permute-start = (f32[160,128]{1,0:T(8,128)S(1)}, f32[160,128]{1,0:T(8,128)S(1)}, u32[]{:S(2)}, u32[]{:S(2)}) collective-permute-start(f32[160,128]{1,0:T(8,128)S(1)} %bitcast.17), channel_id=1, source_target_pairs={{0,16},{32,48},{64,80},{96,112},{128,144},{160,176},{192,208},{224... | collective-permute-start | bytes 245768 | tf_op jit(solution)/shard_map/ppermute | solution.py:336
  7.5 0.0 copy-start.3
  7.5 0.0 copy-start.4
  7.5 0.0 copy-start.1
  7.6 0.0 copy-start.2
  7.6 0.0 copy-start
  7.6 0.0 copy-start.5
  7.6 0.6 copy-done.3
  8.2 0.0 copy-done.4
  8.2 0.0 copy-done.1
  8.2 0.0 copy-done.2
  8.2 0.0 copy-done
  8.3 1.1 %shard_map.73.stats_ref.own_stats_ref = f32[8,128]{1,0:T(8,128)S(1)} custom-call(s32[2]{0:T(128)S(1)} %copy-done.5, f32[2,3]{1,0:T(2,128)S(1)} %copy-done, s32[2,3]{1,0:T(2,128)S(1)} %copy-done.1, f32[2,128]{1,0:T(2,128)S(1)} %copy-done.2, s32[2,128]{1,0:T(2,128)S(1)} %copy-done.3, f32[2,128]{1,0:T(2,128)S(1)} %copy-done.4), custom_call_target="tpu_custom_call" | custom-call | tf_op jit(solution)/shard_map/pallas_call | solution.py:351
  9.4 1.2 %collective-permute-done.1.far_ref = f32[160,128]{1,0:T(8,128)S(1)} collective-permute-done((f32[160,128]{1,0:T(8,128)S(1)}, f32[160,128]{1,0:T(8,128)S(1)}, u32[]{:S(2)}, u32[]{:S(2)}) %collective-permute-start.1) | collective-permute-done | bytes 81952 | tf_op jit(solution)/shard_map/ppermute | solution.py:336
  10.5 1.4 %collective-permute-done.near_ref = f32[160,128]{1,0:T(8,128)S(1)} collective-permute-done((f32[160,128]{1,0:T(8,128)S(1)}, f32[160,128]{1,0:T(8,128)S(1)}, u32[]{:S(2)}, u32[]{:S(2)}) %collective-permute-start) | collective-permute-done | bytes 81952 | tf_op jit(solution)/shard_map/ppermute | solution.py:336
  11.9 1.0 %shard_map.74.in_ref = f32[168,128]{1,0:T(8,128)S(1)} custom-call(s32[1]{0:T(128)} %bitcast.band_ref, f32[160,128]{1,0:T(8,128)S(1)} %bitcast.18, f32[160,128]{1,0:T(8,128)S(1)} %collective-permute-done.near_ref, f32[160,128]{1,0:T(8,128)S(1)} %collective-permute-done.1.far_ref, f32[8,128]{1,0:T(8,128)S(1)} %shard_map.73.stats_ref.own_stats_ref), custom_call_target="tpu_custom_call" | custom-call | tf_op jit(solution)/shard_map/pallas_call | solution.py:354
  12.9 24.9 %collective-permute-start.2 = (f32[168,128]{1,0:T(8,128)S(1)}, f32[168,128]{1,0:T(8,128)S(1)}, u32[]{:S(2)}, u32[]{:S(2)}) collective-permute-start(f32[168,128]{1,0:T(8,128)S(1)} %shard_map.74.in_ref), channel_id=1, source_target_pairs={{0,8},{8,0},{1,9},{9,1},{2,10},{10,2},{3,11},{11,3},{4,12},{12,4},... | collective-permute-start | bytes 258056 | tf_op jit(solution)/shard_map/ppermute | solution.py:336
  37.8 0.6 shard_map.75
  38.5 4.3 %all-to-all-start = ((f32[8,5,4,128]{3,2,1,0:T(4,128)}), f32[8,5,4,128]{3,2,1,0:T(4,128)S(1)}, u32[]{:S(2)}, u32[]{:S(2)}) async-start(f32[8,5,4,128]{3,2,1,0:T(4,128)} %bitcast.4), calls=%async_computation | async-start | bytes 163840 | tf_op jit(solution)/shard_map/all_to_all | solution.py:340
  42.8 5.7 %all-to-all-done = f32[8,5,4,128]{3,2,1,0:T(4,128)S(1)} async-done(((f32[8,5,4,128]{3,2,1,0:T(4,128)}), f32[8,5,4,128]{3,2,1,0:T(4,128)S(1)}, u32[]{:S(2)}, u32[]{:S(2)}) %all-to-all-start) | async-done | bytes 81952 | tf_op jit(solution)/shard_map/all_to_all | solution.py:340
  48.5 0.0 collective-permute-done.2.in_ref
  48.5 8.1 %all_to_all.15 = f32[8,5,4,128]{3,2,1,0:T(4,128)S(1)} all-to-all(f32[8,5,4,128]{3,2,1,0:T(4,128)S(1)} %bitcast.19), channel_id=1, replica_groups=mesh['band'=64,'half'=2,'q'=8] {'q'}, dimensions={0} | all-to-all | bytes 163840 | tf_op jit(solution)/shard_map/all_to_all | solution.py:340
  56.6 2.6 %shard_map.77 = f32[160,128]{1,0:T(8,128)S(1)} custom-call(s32[1]{0:T(128)} %bitcast.1.half_ref, f32[160,128]{1,0:T(8,128)S(1)} %bitcast.12, f32[160,128]{1,0:T(8,128)S(1)} %bitcast.13, f32[8,128]{1,0:T(8,128)S(1)} %shard_map.73.stats_ref.own_stats_ref, f32[8,128]{1,0:T(8,128)S(1)} %get-tuple-element.10.other_stats_ref), custom_call_target="tpu_custom_call" | custom-call | tf_op jit(solution)/shard_map/pallas_call | solution.py:365
  59.2 8.1 %all_to_all.16 = f32[8,5,4,128]{3,2,1,0:T(4,128)S(1)} all-to-all(f32[8,5,4,128]{3,2,1,0:T(4,128)S(1)} %bitcast.14), channel_id=1, replica_groups=mesh['band'=64,'half'=2,'q'=8] {'q'}, dimensions={0} | all-to-all | bytes 163840 | tf_op jit(solution)/shard_map/all_to_all | solution.py:340
  67.3 0.2 shard_map.78
  67.5 5.5 %collective-permute-start.3 = (f32[80,128]{1,0:T(8,128)S(1)}, f32[80,128]{1,0:T(8,128)S(1)}, u32[]{:S(2)}, u32[]{:S(2)}) collective-permute-start(f32[80,128]{1,0:T(8,128)S(1)} %get-tuple-element.11.near_ref), channel_id=1, source_target_pairs={{0,16},{32,48},{64,80},{96,112},{128,144},{160,176},{192,208},{224... | collective-permute-start | bytes 122888 | tf_op jit(solution)/shard_map/ppermute | solution.py:336
  73.0 2.3 %collective-permute-start.4 = (f32[80,128]{1,0:T(8,128)S(1)}, f32[80,128]{1,0:T(8,128)S(1)}, u32[]{:S(2)}, u32[]{:S(2)}) collective-permute-start(f32[80,128]{1,0:T(8,128)S(1)} %get-tuple-element.12.far_ref), channel_id=1, source_target_pairs={{16,32},{48,64},{80,96},{112,128},{144,160},{176,192},{208,224},{2... | collective-permute-start | bytes 122888 | tf_op jit(solution)/shard_map/ppermute | solution.py:336
  75.3 0.0 collective-permute-done.3.from_near_ref
  75.3 6.9 %collective-permute-done.4.from_far_ref = f32[80,128]{1,0:T(8,128)S(1)} collective-permute-done((f32[80,128]{1,0:T(8,128)S(1)}, f32[80,128]{1,0:T(8,128)S(1)}, u32[]{:S(2)}, u32[]{:S(2)}) %collective-permute-start.4) | collective-permute-done | bytes 40992 | tf_op jit(solution)/shard_map/ppermute | solution.py:336
  82.2 0.9 %shard_map.79 = f32[160,128]{1,0:T(8,128)} custom-call(s32[1]{0:T(128)} %bitcast.band_ref, f32[80,128]{1,0:T(8,128)S(1)} %get-tuple-element.11.near_ref, f32[80,128]{1,0:T(8,128)S(1)} %get-tuple-element.12.far_ref, f32[80,128]{1,0:T(8,128)S(1)} %collective-permute-done.3.from_near_ref, f32[80,128]{1,0:T(8,128)S(1)} %collective-permute-done.4.from_far_ref), custom_call_target="tpu_custom_call" | custom-call | tf_op jit(solution)/shard_map/pallas_call | solution.py:373
  (2 shorter events, 0.0 us)
Async XLA Ops:
  0.9 9.6 %collective-permute-start.1 = (f32[160,128]{1,0:T(8,128)S(1)}, f32[160,128]{1,0:T(8,128)S(1)}, u32[]{:S(2)}, u32[]{:S(2)}) collective-permute-start(f32[160,128]{1,0:T(8,128)S(1)} %bitcast.16), channel_id=1, source_target_pairs={{16,32},{48,64},{80,96},{112,128},{144,160},{176,192},{208,224},{2... | collective-permute-start | bytes 245768 | tf_op jit(solution)/shard_map/ppermute | solution.py:336
  5.6 6.3 %collective-permute-start = (f32[160,128]{1,0:T(8,128)S(1)}, f32[160,128]{1,0:T(8,128)S(1)}, u32[]{:S(2)}, u32[]{:S(2)}) collective-permute-start(f32[160,128]{1,0:T(8,128)S(1)} %bitcast.17), channel_id=1, source_target_pairs={{0,16},{32,48},{64,80},{96,112},{128,144},{160,176},{192,208},{224... | collective-permute-start | bytes 245768 | tf_op jit(solution)/shard_map/ppermute | solution.py:336
  7.5 0.7 copy-start.3
  7.5 0.7 copy-start.4
  7.5 0.7 copy-start.1
  7.6 0.7 copy-start.2
  7.6 0.7 copy-start
  7.6 0.7 copy-start.5
  12.9 35.6 %collective-permute-start.2 = (f32[168,128]{1,0:T(8,128)S(1)}, f32[168,128]{1,0:T(8,128)S(1)}, u32[]{:S(2)}, u32[]{:S(2)}) collective-permute-start(f32[168,128]{1,0:T(8,128)S(1)} %shard_map.74.in_ref), channel_id=1, source_target_pairs={{0,8},{8,0},{1,9},{9,1},{2,10},{10,2},{3,11},{11,3},{4,12},{12,4},... | collective-permute-start | bytes 258056 | tf_op jit(solution)/shard_map/ppermute | solution.py:336
  38.5 10.0 %all-to-all-start = ((f32[8,5,4,128]{3,2,1,0:T(4,128)}), f32[8,5,4,128]{3,2,1,0:T(4,128)S(1)}, u32[]{:S(2)}, u32[]{:S(2)}) async-start(f32[8,5,4,128]{3,2,1,0:T(4,128)} %bitcast.4), calls=%async_computation | async-start | bytes 163840 | tf_op jit(solution)/shard_map/all_to_all | solution.py:340
  67.5 7.8 %collective-permute-start.3 = (f32[80,128]{1,0:T(8,128)S(1)}, f32[80,128]{1,0:T(8,128)S(1)}, u32[]{:S(2)}, u32[]{:S(2)}) collective-permute-start(f32[80,128]{1,0:T(8,128)S(1)} %get-tuple-element.11.near_ref), channel_id=1, source_target_pairs={{0,16},{32,48},{64,80},{96,112},{128,144},{160,176},{192,208},{224... | collective-permute-start | bytes 122888 | tf_op jit(solution)/shard_map/ppermute | solution.py:336
  73.0 9.2 %collective-permute-start.4 = (f32[80,128]{1,0:T(8,128)S(1)}, f32[80,128]{1,0:T(8,128)S(1)}, u32[]{:S(2)}, u32[]{:S(2)}) collective-permute-start(f32[80,128]{1,0:T(8,128)S(1)} %get-tuple-element.12.far_ref), channel_id=1, source_target_pairs={{16,32},{48,64},{80,96},{112,128},{144,160},{176,192},{208,224},{2... | collective-permute-start | bytes 122888 | tf_op jit(solution)/shard_map/ppermute | solution.py:336
